TPU v7x, 256 devices: a whole 4x4x8 slice. The times are simulated.
256 devices in a mesh: seq: 32 (over z, y_hi, core), tp: 8 (over y_lo, x).
Axes of the slice: x: 4, y: 4 (y_hi: 2, y_lo: 2; y = y_hi * 2 + y_lo), z: 8, core: 2. Of those that a mesh axis runs over, the one named last changes fastest.
Arguments:
- video_query: bfloat16 [2, 16384, 3072], P(None, 'seq', 'tp'), may hold values from -2048 to 2048
- text_states: bfloat16 [2, 256, 4096], P(None, 'seq'), may hold values from -24 to 24
- key_weight: bfloat16 [4096, 3072], P(None, 'tp'), may hold values from -1 to 1
- value_weight: bfloat16 [4096, 3072], P(None, 'tp'), may hold values from -0.09375 to 0.09375
- text_lengths: int32 [2], replicated, may hold values from 64 to 256, as said below
- output_grad: bfloat16 [2, 16384, 3072], P(None, 'seq', 'tp'), may hold values from -6 to 6
Outputs:
- attended: bfloat16 [2, 16384, 3072], P(None, 'seq', 'tp')
- query_grad: bfloat16 [2, 16384, 3072], P(None, 'seq', 'tp')
- key_weight_grad: float32 [4096, 3072], P('seq', 'tp')
- value_weight_grad: float32 [4096, 3072], P('seq', 'tp')
Inputs may be any that keep to these rules, and one draw needn't show every extreme that they name: Keys of sample b at text positions from text_lengths[b] on are masked; one sample has all 256 text tokens.
All inputs are finite; a program needn't handle non-finite values.
Results may differ from a plain program's by a relative error of at most 0.012.
The roundings to bfloat16 on the way count: a program that leaves them out, or rounds other values in their place, can miss the bound.
Values may be sent and summed in bfloat16 or wider, within the bound.
No kernel may reach another device: no remote copies, remote signals or barrier semaphores. Data moves between devices by JAX's collectives and lax.ppermute only.
A program may use at most 128 MiB of HBM per device.

v0:
```python
import functools
import math

import jax
import jax.numpy as jnp
from jax import lax
from jax.sharding import Mesh
from jax.sharding import PartitionSpec as P

DT = 4096
HEADS = 24
HEAD = 128
SEQ = ("seq_0", "seq_1", "seq_2")
SEQ_TP = ("seq_0", "seq_1", "seq_2", "tp_0", "tp_1")
TP = ("tp_0", "tp_1")


def in_one_piece(arrays, axis, dim, along):
    both = jnp.concatenate(arrays, axis=along)
    out, at, finished = (lax.all_gather(both, axis, axis=dim, tiled=True), 0, [])
    for a in arrays:
        finished.append(lax.slice_in_dim(out, at, at + a.shape[along], axis=along))
        at += a.shape[along]
    return tuple(finished)


def over_axes(array, axes):
    return functools.reduce(lax.psum, axes, array)


def split_product(text_low, gradients):
    leading = lax.optimization_barrier(gradients.astype(jnp.bfloat16))
    remainder = (gradients - leading.astype(jnp.float32)).astype(jnp.bfloat16)
    dimensions = (((0,), (0,)), ((), ()))
    first = lax.dot_general(text_low, leading, dimensions, preferred_element_type=jnp.float32)
    second = lax.dot_general(text_low, remainder, dimensions, preferred_element_type=jnp.float32)
    return first + second


def per_device(video_query, text_states, key_weight, value_weight, text_lengths, output_grad):
    samples, video_rows, feature_count = video_query.shape
    head_count = feature_count // HEAD
    scaling = 1.0 / math.sqrt(HEAD)
    key_part = jnp.dot(text_states, key_weight, preferred_element_type=jnp.float32).astype(
        jnp.bfloat16
    )
    value_part = jnp.dot(text_states, value_weight, preferred_element_type=jnp.float32).astype(
        jnp.bfloat16
    )
    key_states, value_states = in_one_piece((key_part, value_part), SEQ, 1, 0)
    text_count = key_states.shape[1]
    query_heads = video_query.reshape(samples, video_rows, head_count, HEAD)
    key_heads = key_states.reshape(samples, text_count, head_count, HEAD)
    value_heads = value_states.reshape(samples, text_count, head_count, HEAD)
    grad_heads = output_grad.reshape(samples, video_rows, head_count, HEAD)
    scores = (
        jnp.einsum("bthe,blhe->bhtl", query_heads, key_heads, preferred_element_type=jnp.float32)
        * scaling
    )
    allowed = jnp.arange(text_count)[None, None, None, :] < text_lengths[:, None, None, None]
    scores = jnp.where(allowed, scores, -1e30)
    highest = jnp.max(scores, axis=-1, keepdims=True)
    weights = jnp.exp(scores - highest)
    probs = weights / jnp.sum(weights, axis=-1, keepdims=True)
    probs_low = probs.astype(jnp.bfloat16)
    attended = jnp.einsum(
        "bhtl,blhe->bthe", probs_low, value_heads, preferred_element_type=jnp.float32
    )
    attended = attended.astype(jnp.bfloat16).reshape(samples, video_rows, feature_count)
    dprob = jnp.einsum(
        "bthe,blhe->bhtl", grad_heads, value_heads, preferred_element_type=jnp.float32
    )
    delta = jnp.sum(probs * dprob, axis=-1, keepdims=True)
    dscore = (probs * (dprob - delta) * scaling).astype(jnp.bfloat16)
    query_grad = jnp.einsum(
        "bhtl,blhe->bthe", dscore, key_heads, preferred_element_type=jnp.float32
    )
    query_grad = query_grad.astype(jnp.bfloat16).reshape(samples, video_rows, feature_count)
    key_grad = jnp.einsum(
        "bhtl,bthe->blhe", dscore, query_heads, preferred_element_type=jnp.float32
    )
    key_grad = key_grad.reshape(samples, text_count, feature_count)
    value_grad = jnp.einsum(
        "bhtl,bthe->blhe", probs_low, grad_heads, preferred_element_type=jnp.float32
    )
    value_grad = value_grad.reshape(samples, text_count, feature_count)
    states_all = lax.all_gather(text_states, SEQ, axis=1, tiled=True)
    flattened = states_all.reshape(samples * text_count, -1)
    stacked = jnp.concatenate([key_grad, value_grad], axis=-1).reshape(
        samples * text_count, 2 * feature_count
    )
    summed = lax.psum_scatter(
        split_product(flattened, stacked), SEQ, scatter_dimension=0, tiled=True
    )
    squares = jnp.sum(summed * summed)
    overall = over_axes(squares, SEQ_TP)
    spread = jnp.sqrt(overall / (2.0 * DT * HEADS * HEAD) + 1e-06)
    factor = 1.0 / jnp.maximum(spread, 1.0)
    return (
        attended,
        query_grad,
        summed[:, :feature_count] * factor,
        summed[:, feature_count:] * factor,
    )


def solution(mesh):
    split = Mesh(mesh.devices.reshape(8, 2, 2, 2, 4), ("seq_0", "seq_1", "seq_2", "tp_0", "tp_1"))
    return jax.shard_map(
        per_device,
        mesh=split,
        in_specs=(
            P(None, SEQ, TP),
            P(None, SEQ, None),
            P(None, TP),
            P(None, TP),
            P(),
            P(None, SEQ, TP),
        ),
        out_specs=(P(None, SEQ, TP), P(None, SEQ, TP), P(SEQ, TP), P(SEQ, TP)),
        check_vma=False,
    )
```

profile of v0, /device:TPU:1, one launch (start us, length us, event | category | flops | bytes accessed | tf_op | source)
XLA Modules:
  0.0 352.6 jit_solution(15601900455384549609)
XLA Ops:
  7.2 0.0 copy-start
  7.2 0.0 all-gather.2.cloned.1.call-start
  7.2 0.7 all-gather.2.cloned.1.call-update
  7.9 0.0 reduce-scatter.2.cloned.1.call-start
  8.0 1.1 copy-done
  9.1 1.6 fusion.19
  10.6 0.0 copy-done.6
  10.6 0.4 copy-done.3
  11.0 0.5 fusion.22
  11.5 48.8 %all_gather.6 = bf16[4,256,384]{2,1,0:T(8,128)(2,1)S(1)} all-gather(bf16[4,8,384]{2,1,0:T(8,128)(2,1)S(1)} %pad_maximum_fusion), channel_id=1, replica_groups=mesh['seq_0'=8,'seq_1'=2,'seq_2'=2,'tp_0'=2,'tp_1'=4] {'seq_0','seq_1','..., dimensions={1}, use_global_device_ids=true | all-gather | bytes 811008 | tf_op jit(solution)/shard_map/all_gather | solution.py:20
  60.4 0.8 fusion.35
  61.2 0.9 copy.25
  62.1 1.2 copy.24
  63.3 0.0 copy-start.7
  63.3 2.5 copy.26
  65.8 2.3 copy.30
  68.1 0.1 iota_compare_fusion
  68.2 3.4 fusion.37
  71.6 4.2 %fusion.36 = (f32[2,3,512]{2,1,0:T(4,128)S(1)}, f32[2,3,512,256]{2,3,1,0:T(8,128)}) fusion(pred[2,256]{1,0:T(4,128)(4,1)S(1)} %iota_compare_fusion, bf16[2,256,3,128]{1,3,2,0:T(8,128)(2,1)} %bitcast.101, bf16[2,512,3,128]{1,3,2,0:T(8,128)(2,1)} %bitcast.98), kind=kOutput, calls=%fused_computation.47 | convolution fusion | flops 204472576 | bytes 4338176 | tf_op jit(solution)/shard_map/sub | solution.py:63
  75.9 7.2 %fusion.18 = f32[2,256,3,128]{3,1,2,0:T(8,128)} fusion(bf16[2,512,3,128]{1,3,2,0:T(8,128)(2,1)} %bitcast.99, f32[2,3,256,512]{3,2,1,0:T(8,128)} %fusion.37, f32[2,3,512,256]{2,3,1,0:T(8,128)} %get-tuple-element.17, f32[2,3,512]{2,1,0:T(4,128)S(1)} %get-tuple-element.16), kind=kOutput, calls=%fused_computation.26 | convolution fusion | flops 206834944 | bytes 7876608 | tf_op jit(solution)/shard_map/bhtl,bthe->blhe/dot_general | solution.py:79
  83.1 2.1 copy.35
  85.2 2.1 copy.50
  87.2 3.5 %convolution_bitcast_fusion = f32[2,256,3,128]{3,1,2,0:T(8,128)} fusion(bf16[2,512,3,128]{1,3,2,0:T(8,128)(2,1)} %bitcast.94, f32[2,3,512,256]{2,3,1,0:T(8,128)} %get-tuple-element.17, f32[2,3,512]{2,1,0:T(4,128)S(1)} %get-tuple-element.16), kind=kOutput, calls=%fused_computation.27 | convolution fusion | flops 202899456 | bytes 4730880 | tf_op jit(solution)/shard_map/bhtl,bthe->blhe/dot_general | solution.py:83
  90.8 2.1 copy.37
  92.9 1.2 copy.51
  94.1 1.2 constant_dynamic-update-slice_fusion.1
  95.3 0.1 constant_dynamic-update-slice_fusion
  95.3 1.2 copy-done.1
  96.5 1.0 convert_element_type.41
  97.5 4.1 %all-gather.2.cloned.1.call-done = bf16[2,256,4096]{2,1,0:T(8,128)(2,1)} async-done(((bf16[2,8,4096]{2,1,0:T(8,128)(2,1)}), bf16[2,256,4096]{2,1,0:T(8,128)(2,1)}) %all-gather.2.cloned.1.call-update) | async-done | bytes 4194320 | tf_op jit(solution)/shard_map/all_gather | solution.py:87
  101.6 5.5 %fusion.38 = f32[768,4096]{1,0:T(8,128)S(1)} fusion(bf16[512,768]{0,1:T(8,128)(2,1)} %convert_element_type.41, bf16[512,4096]{1,0:T(8,128)(2,1)} %bitcast.87), kind=kOutput, calls=%fused_computation.49 | convolution fusion | flops 3221225472 | bytes 17563648 | tf_op jit(solution)/shard_map/dot_general | solution.py:35
  107.2 6.4 %add_bitcast_fusion = f32[4096,768]{0,1:T(8,128)} fusion(f32[768,4096]{1,0:T(8,128)S(1)} %fusion.38, bf16[512,4096]{1,0:T(8,128)(2,1)S(1)} %bitcast.88, f32[512,768]{0,1:T(8,128)S(1)} %copy-done.2, bf16[512,768]{0,1:T(8,128)(2,1)S(1)} %copy-done.5), kind=kOutput, calls=%fused_computation.2 | convolution fusion | flops 3225550848 | bytes 31719424 | tf_op jit(solution)/shard_map/dot_general | solution.py:36
  113.5 0.0 reduce-scatter.2.cloned.1.call-update
  113.6 165.4 %reduce-scatter.2.cloned.1.call-done = f32[128,768]{0,1:T(8,128)} async-done(((f32[4096,768]{0,1:T(8,128)}), f32[128,768]{0,1:T(8,128)}) %reduce-scatter.2.cloned.1.call-update) | async-done | bytes 393232 | tf_op jit(solution)/shard_map/reduce_scatter | solution.py:92
  279.0 1.7 multiply_reduce_fusion
  280.7 12.5 %psum.35 = f32[]{:T(128)} all-reduce(f32[]{:T(128)} %multiply_reduce_fusion), channel_id=1, replica_groups=mesh['seq_0'=8,'seq_1'=2,'seq_2'=2,'tp_0'=2,'tp_1'=4] {'seq_0'}, use_global_device_ids=true, to_apply=%region_5.6 | all-reduce | flops 1 | bytes 8 | tf_op jit(solution)/shard_map/psum | solution.py:28
  293.2 0.0 copy-done.12
  293.2 3.2 convolution_convert_fusion.1
  296.3 5.9 %psum.36 = f32[]{:T(128)} all-reduce(f32[]{:T(128)} %psum.35), channel_id=1, replica_groups=mesh['seq_0'=8,'seq_1'=2,'seq_2'=2,'tp_0'=2,'tp_1'=4] {'seq_1'}, use_global_device_ids=true, to_apply=%region_6.7 | all-reduce | flops 1 | bytes 8 | tf_op jit(solution)/shard_map/psum | solution.py:28
  302.2 7.1 %convolution_convert_fusion = bf16[2,3,128,512]{3,2,1,0:T(8,128)(2,1)} fusion(bf16[2,256,3,128]{1,3,2,0:T(8,128)(2,1)} %bitcast.102, f32[2,3,256,512]{3,2,1,0:T(8,128)} %fusion.37, f32[2,3,512,256]{2,3,1,0:T(8,128)} %get-tuple-element.17, f32[2,3,512]{2,1,0:T(4,128)S(1)} %copy-done.12), kind=kOutput, calls=%fused_computation.22 | convolution fusion | flops 207228160 | bytes 7483392 | tf_op jit(solution)/shard_map/bhtl,blhe->bthe/dot_general | solution.py:75
  309.3 13.5 %psum.37 = f32[]{:T(128)} all-reduce(f32[]{:T(128)} %psum.36), channel_id=1, replica_groups=mesh['seq_0'=8,'seq_1'=2,'seq_2'=2,'tp_0'=2,'tp_1'=4] {'seq_2'}, use_global_device_ids=true, to_apply=%region_7.8 | all-reduce | flops 1 | bytes 8 | tf_op jit(solution)/shard_map/psum | solution.py:28
  322.8 2.3 copy.39
  325.1 4.4 %psum.38 = f32[]{:T(128)} all-reduce(f32[]{:T(128)} %psum.37), channel_id=1, replica_groups=mesh['seq_0'=8,'seq_1'=2,'seq_2'=2,'tp_0'=2,'tp_1'=4] {'tp_0'}, use_global_device_ids=true, to_apply=%region_8.9 | all-reduce | flops 1 | bytes 8 | tf_op jit(solution)/shard_map/psum | solution.py:28
  329.5 2.3 copy.38
  331.8 9.0 %psum.39 = f32[]{:T(128)} all-reduce(f32[]{:T(128)} %psum.38), channel_id=1, replica_groups=mesh['seq_0'=8,'seq_1'=2,'seq_2'=2,'tp_0'=2,'tp_1'=4] {'tp_1'}, use_global_device_ids=true, to_apply=%region_9.10 | all-reduce | flops 1 | bytes 8 | tf_op jit(solution)/shard_map/psum | solution.py:28
  341.6 0.8 slice_multiply_fusion
  342.3 1.7 copy.41
  344.1 1.7 copy.40
  (20 shorter events, 0.0 us)
Async XLA Ops:
  7.2 1.9 copy-start
  7.2 3.5 copy-start.6
  7.2 94.4 %all-gather.2.cloned.1.call-start = ((), (), s32[]{:S(2)}) async-start(), calls=%async_computation.1 | async-start | bytes 4325376 | tf_op jit(solution)/shard_map/all_gather | solution.py:87
  7.9 271.1 %reduce-scatter.2.cloned.1.call-start = ((), (), s32[]{:S(2)}) async-start(), calls=%async_computation.2 | async-start | bytes 12976128 | tf_op jit(solution)/shard_map/reduce_scatter | solution.py:92
  9.1 2.0 copy-start.3
  60.4 7.7 %copy-start.10 = (s32[2]{0:T(128)S(1)}, s32[2]{0:T(128)}, u32[]{:S(2)}) copy-start(s32[2]{0:T(128)} %param.10) | copy-start | bytes 28
  63.3 8.3 %copy-start.7 = (bf16[2,256,384]{1,2,0:T(8,128)(2,1)}, bf16[2,256,384]{1,2,0:T(8,128)(2,1)S(1)}, u32[]{:S(2)}) copy-start(bf16[2,256,384]{1,2,0:T(8,128)(2,1)S(1)} %copy.24) | copy-start | bytes 1179652
  75.9 11.4 %copy-start.11 = (f32[2,3,512]{2,1,0:T(4,128)}, f32[2,3,512]{2,1,0:T(4,128)S(1)}, u32[]{:S(2)}) copy-start(f32[2,3,512]{2,1,0:T(4,128)S(1)} %get-tuple-element.16) | copy-start | bytes 36868
  95.3 1.2 copy-start.1
  101.6 5.6 %copy-start.2 = (f32[512,768]{0,1:T(8,128)S(1)}, f32[512,768]{0,1:T(8,128)}, u32[]{:S(2)}) copy-start(f32[512,768]{0,1:T(8,128)} %copy-done.1) | copy-start | bytes 4718596
  101.6 5.6 %copy-start.4 = (bf16[2,256,4096]{2,1,0:T(8,128)(2,1)S(1)}, bf16[2,256,4096]{2,1,0:T(8,128)(2,1)}, u32[]{:S(2)}) copy-start(bf16[2,256,4096]{2,1,0:T(8,128)(2,1)} %all-gather.2.cloned.1.call-done) | copy-start | bytes 12582916
  101.6 5.6 %copy-start.5 = (bf16[512,768]{0,1:T(8,128)(2,1)S(1)}, bf16[512,768]{0,1:T(8,128)(2,1)}, u32[]{:S(2)}) copy-start(bf16[512,768]{0,1:T(8,128)(2,1)} %convert_element_type.41) | copy-start | bytes 2359300
  113.5 179.6 %copy-start.8 = (bf16[2,256,384]{1,2,0:T(8,128)(2,1)S(1)}, bf16[2,256,384]{1,2,0:T(8,128)(2,1)}, u32[]{:S(2)}) copy-start(bf16[2,256,384]{1,2,0:T(8,128)(2,1)} %copy-done.7) | copy-start | bytes 1179652
  113.5 179.6 %copy-start.12 = (f32[2,3,512]{2,1,0:T(4,128)S(1)}, f32[2,3,512]{2,1,0:T(4,128)}, u32[]{:S(2)}) copy-start(f32[2,3,512]{2,1,0:T(4,128)} %copy-done.11) | copy-start | bytes 36868
  309.3 32.2 %copy-start.9 = (f32[128,768]{0,1:T(8,128)S(1)}, f32[128,768]{0,1:T(8,128)}, u32[]{:S(2)}) copy-start(f32[128,768]{0,1:T(8,128)} %reduce-scatter.2.cloned.1.call-done) | copy-start | bytes 1179652
Sparse Core Ops, SparseCore 0:
  10.8 90.7 all-gather.1
  113.7 165.2 reduce-scatter.1
where the time goes:
time: 354 us; the launch traced here: 353 us
  waiting for transfers between devices  170 us (48%)
  blocking collectives  94.1 us (27%)
  matrix products  42.7 us (12%)
  local copies, waits for them, and re-layouts  27.2 us (8%)
  between operations  14.9 us (4%)
    reduce_scatter x1, waiting for transfers between devices, per_device(): lax.psum_scatter(split_product(flattened, stacked), SEQ, scatter_dimensio...  165 us
    all_gather x1, blocking collectives, in_one_piece(): lax.all_gather(both, axis, axis=dim, tiled=True)  48.8 us
    psum x5, blocking collectives, over_axes(): return functools.reduce(lax.psum, axes, array)  45.3 us
    unnamed x35, local copies, waits for them, and re-layouts  20 us
    dot_general x1, matrix products, per_device(): jnp.einsum('bhtl,bthe->blhe', dscore, query_heads, preferred_element_type...  7.21 us
    dot_general x1, matrix products, per_device(): jnp.einsum('bhtl,blhe->bthe', dscore, key_heads, preferred_element_type=j...  7.1 us
  transfers between devices with their start and end apart: 2, of which 2 were waited for; matrix products, arithmetic and copies ran while one was open for 11% of the time, Pallas kernels for 0%

commit v1 on v0

v1 whole, which is shorter than its diff:
```python
import functools
import math

import jax
import jax.numpy as jnp
from jax import lax
from jax.experimental import pallas as pl
from jax.experimental.pallas import tpu as pltpu
from jax.sharding import Mesh
from jax.sharding import PartitionSpec as P

DT = 4096
HEADS = 24
HEAD = 128
ZY = ("z", "yh")
SEQ = ("z", "yh", "core")
TP = ("yl", "x")
ALL = SEQ + TP
SCALING = 1.0 / math.sqrt(HEAD)
BF16 = jnp.bfloat16
F32 = jnp.float32


def dot(a, b, ca, cb):
    return lax.dot_general(a, b, (((ca,), (cb,)), ((), ())), preferred_element_type=F32)


def project_kernel(text_ref, key_ref, value_ref, out_ref):
    groups = out_ref.shape[0]
    features = key_ref.shape[1]
    text = text_ref[...].reshape(-1, DT)
    key = dot(text, key_ref[...], 1, 0).astype(BF16)
    value = dot(text, value_ref[...], 1, 0).astype(BF16)
    both = jnp.concatenate([key, value], axis=-1)
    wide = DT // groups
    for g in range(groups):
        out_ref[g, :, : 2 * features] = both
        out_ref[g, :, 2 * features :] = text[:, g * wide : (g + 1) * wide]


def attend_kernel(lengths_ref, core_ref, query_ref, grad_ref, own_ref, other_ref, attended_ref, query_grad_ref, own_sum_ref, other_sum_ref):
    samples, rows, features = query_ref.shape
    groups = own_ref.shape[0]
    heads = features // HEAD
    core = core_ref[0]
    half = groups * 8
    place = lax.broadcasted_iota(jnp.int32, (2 * half, 1), 0)
    within = place % half
    side = jnp.where(place < half, core, 1 - core)
    token = (within // 8) * 16 + side * 8 + within % 8

    def text_of(b, first):
        cols = slice(first, first + HEAD)
        pieces = [ref[:, b * 8 : (b + 1) * 8, cols].reshape(half, HEAD) for ref in (own_ref, other_ref)]
        return jnp.concatenate(pieces, axis=0)

    def put_sum(value, b, first):
        cols = slice(first, first + HEAD)
        own_sum_ref[:, b * 8 : (b + 1) * 8, cols] = value[:half].reshape(groups, 8, HEAD)
        other_sum_ref[:, b * 8 : (b + 1) * 8, cols] = value[half:].reshape(groups, 8, HEAD).astype(BF16)

    for b in range(samples):
        allowed = token < lengths_ref[b]
        for h in range(heads):
            cols = slice(h * HEAD, (h + 1) * HEAD)
            key = text_of(b, h * HEAD)
            value = text_of(b, features + h * HEAD)
            query = query_ref[b, :, cols]
            grad = grad_ref[b, :, cols]
            scores = dot(key, query, 1, 1) * SCALING
            scores = jnp.where(allowed, scores, -1e30)
            weights = jnp.exp(scores - jnp.max(scores, axis=0, keepdims=True))
            probs = weights * (1.0 / jnp.sum(weights, axis=0, keepdims=True))
            probs_low = probs.astype(BF16)
            dprob = dot(value, grad, 1, 1)
            delta = jnp.sum(probs * dprob, axis=0, keepdims=True)
            dscore = (probs * (dprob - delta) * SCALING).astype(BF16)
            put_sum(dot(dscore, query, 1, 0), b, h * HEAD)
            put_sum(dot(probs_low, grad, 1, 0), b, features + h * HEAD)
            attended_ref[b, :, cols] = dot(probs_low, value, 0, 0).astype(BF16)
            query_grad_ref[b, :, cols] = dot(dscore, key, 0, 0).astype(BF16)


def pair_sum_kernel(own_ref, other_ref, out_ref):
    out_ref[...] = (own_ref[...] + other_ref[...].astype(F32)).astype(BF16)


def total_kernel(parts_ref, out_ref):
    total = parts_ref[0].astype(F32)
    for g in range(1, parts_ref.shape[0]):
        total = total + parts_ref[g].astype(F32)
    total = total.astype(BF16)
    for g in range(out_ref.shape[0]):
        out_ref[g] = total


def weight_kernel(core_ref, own_text_ref, other_text_ref, own_ref, other_ref, raw_ref, square_ref):
    groups, rows, width = own_ref.shape
    first = pl.multiple_of(width + core_ref[0] * HEAD, HEAD)
    raw = None
    for text_ref, sum_ref in ((own_text_ref, own_ref), (other_text_ref, other_ref)):
        text = text_ref[:, :, pl.ds(first, HEAD)].reshape(groups * rows, HEAD)
        part = dot(text, sum_ref[...].reshape(groups * rows, width), 0, 0)
        raw = part if raw is None else raw + part
    raw_ref[...] = raw
    squares = jnp.sum((raw * raw).reshape(-1, 8, width), axis=0)
    lanes = squares[:, :HEAD]
    for at in range(HEAD, width, HEAD):
        lanes = lanes + squares[:, at : at + HEAD]
    square_ref[...] = jnp.sum(lanes, axis=0, keepdims=True)


def call(kernel, out, *args, scalars=0):
    specs = [pl.BlockSpec(memory_space=pltpu.SMEM)] * scalars
    specs += [pl.BlockSpec(memory_space=pltpu.VMEM)] * (len(args) - scalars)
    one = pl.BlockSpec(memory_space=pltpu.VMEM)
    out_specs = one if isinstance(out, jax.ShapeDtypeStruct) else [one] * len(out)
    return pl.pallas_call(kernel, out_shape=out, in_specs=specs, out_specs=out_specs)(*args)


def shape(dims, dtype):
    return jax.ShapeDtypeStruct(dims, dtype)


def swap(array):
    return lax.ppermute(array, "core", [(0, 1), (1, 0)])


def per_device(video_query, text_states, key_weight, value_weight, text_lengths, output_grad):
    samples, video_rows, features = video_query.shape
    text_rows = samples * text_states.shape[1]
    groups = lax.axis_size(ZY)
    wide = 2 * features
    core = lax.axis_index("core").astype(jnp.int32).reshape(1)
    packed = call(project_kernel, shape((groups, text_rows, wide + DT // groups), BF16), text_states, key_weight, value_weight)
    own = lax.all_to_all(packed, ZY, 0, 0, tiled=True)
    other = swap(own)
    like = shape(video_query.shape, BF16)
    block = (groups, text_rows, wide)
    attended, query_grad, own_sum, other_sum = call(
        attend_kernel, [like, like, shape(block, F32), shape(block, BF16)],
        text_lengths, core, video_query, output_grad, own, other, scalars=2,
    )
    pair = call(pair_sum_kernel, shape(block, BF16), own_sum, swap(other_sum))
    parts = lax.all_to_all(pair, ZY, 0, 0, tiled=True)
    own_total = lax.all_to_all(call(total_kernel, shape(block, BF16), parts), ZY, 0, 0, tiled=True)
    other_total = swap(own_total)
    raw, squares = call(
        weight_kernel, [shape((HEAD, wide), F32), shape((1, HEAD), F32)],
        core, own, other, own_total, other_total, scalars=1,
    )
    every = lax.axis_size(ALL)
    local = jnp.sum(squares)
    overall = jnp.sum(lax.all_to_all(jnp.full((every, 1), local), ALL, 0, 0, tiled=True))
    spread = jnp.sqrt(overall / (2.0 * DT * HEADS * HEAD) + 1e-06)
    factor = 1.0 / jnp.maximum(spread, 1.0)
    return (attended, query_grad, raw[:, :features] * factor, raw[:, features:] * factor)


def solution(mesh):
    split = Mesh(mesh.devices.reshape(8, 2, 2, 2, 4), ALL)
    return jax.shard_map(
        per_device,
        mesh=split,
        in_specs=(P(None, SEQ, TP), P(None, SEQ, None), P(None, TP), P(None, TP), P(), P(None, SEQ, TP)),
        out_specs=(P(None, SEQ, TP), P(None, SEQ, TP), P(SEQ, TP), P(SEQ, TP)),
        check_vma=False,
    )
```

time: 354 us -> 123 us (0.35)
  waiting for transfers between devices: 170 us -> 4.46 us
  matrix products: 42.7 us -> 0 us
  local copies, waits for them, and re-layouts: 27.2 us -> 3.02 us
  Pallas kernels: 0 us -> 18.4 us
  between operations: 14.9 us -> 1.39 us
  blocking collectives: 94.1 us -> 84.7 us
  starting transfers between devices: 0.08 us -> 6.46 us
    reduce_scatter x1 -> x0, waiting for transfers between devices: 165 us -> none  [per_device(): lax.psum_scatter(split_product(flattened, stacked), SEQ, scatter_dimensio...]
    all_to_all x0 -> x4, blocking collectives: none -> 84.7 us  [the longest x1 28.9 us: per_device(): own = lax.all_to_all(packed, ZY, 0, 0, tiled=True)]
    all_gather x1 -> x0, blocking collectives: 48.8 us -> none  [in_one_piece(): lax.all_gather(both, axis, axis=dim, tiled=True)]
    psum x5 -> x0, blocking collectives: 45.3 us -> none  [over_axes(): return functools.reduce(lax.psum, axes, array)]
    dot_general x9 -> x0, matrix products: 38.4 us -> none  [the longest x1 7.21 us: per_device(): jnp.einsum('bhtl,bthe->blhe', dscore, query_heads, preferred_element_type...]
    pallas_call x0 -> x5, Pallas kernels: none -> 18.4 us  [call(): pl.pallas_call(kernel, out_shape=out, in_specs=specs, out_specs=out_specs)]
    unnamed x35 -> x10, local copies, waits for them, and re-layouts: 20 us -> 2.31 us
    ppermute x0 -> x3, starting transfers between devices: none -> 6.46 us  [swap(): return lax.ppermute(array, 'core', [(0, 1), (1, 0)])]
  transfers between devices with their start and end apart: 2 -> 3, of which waited for: 2 -> 3; matrix products, arithmetic and copies ran while one was open for 11% -> 0% of each run, Pallas kernels for 0% -> 0%
where the time goes in v1:
time: 123 us; the launch traced here: 122 us
  blocking collectives  84.7 us (69%)
  Pallas kernels  18.4 us (15%)
  starting transfers between devices  6.46 us (5%)
  waiting for transfers between devices  4.46 us (4%)
  other arithmetic  3.92 us (3%)
  local copies, waits for them, and re-layouts  3.02 us (2%)
  between operations  1.39 us (1%)
    all_to_all x1, blocking collectives, per_device(): own = lax.all_to_all(packed, ZY, 0, 0, tiled=True)  28.9 us
    all_to_all x1, blocking collectives, per_device(): parts = lax.all_to_all(pair, ZY, 0, 0, tiled=True)  19.4 us
    all_to_all x1, blocking collectives, per_device(): lax.all_to_all(jnp.full((every, 1), local), ALL, 0, 0, tiled=True)  18.9 us
    pallas_call x5, Pallas kernels, call(): pl.pallas_call(kernel, out_shape=out, in_specs=specs, out_specs=out_specs)  18.4 us
    all_to_all x1, blocking collectives, per_device(): lax.all_to_all(call(total_kernel, shape(block, BF16), parts), ZY, 0, 0, t...  17.5 us
    ppermute x3, starting transfers between devices, swap(): return lax.ppermute(array, 'core', [(0, 1), (1, 0)])  6.46 us
    ppermute x3, waiting for transfers between devices, swap(): return lax.ppermute(array, 'core', [(0, 1), (1, 0)])  4.46 us
  transfers between devices with their start and end apart: 3, of which 3 were waited for; matrix products, arithmetic and copies ran while one was open for 0% of the time, Pallas kernels for 0%

profile of v1, /device:TPU:1, one launch (start us, length us, event | category | flops | bytes accessed | tf_op | source)
XLA Modules:
  0.0 122.4 jit_solution(11401921529624795702)
XLA Ops:
  0.6 4.6 %shard_map.93 = bf16[16,16,1024]{2,1,0:T(8,128)(2,1)} custom-call(bf16[2,8,4096]{2,1,0:T(8,128)(2,1)} %text_ref.1, bf16[4096,384]{1,0:T(8,128)(2,1)} %key_ref.1, bf16[4096,384]{1,0:T(8,128)(2,1)} %value_ref.1), custom_call_target="tpu_custom_call" | custom-call | tf_op jit(solution)/shard_map/pallas_call | solution.py:118
  5.3 28.9 %all_to_all.21.own_ref.own_text_ref = bf16[16,16,1024]{2,1,0:T(8,128)(2,1)S(1)} all-to-all(bf16[16,16,1024]{2,1,0:T(8,128)(2,1)} %shard_map.93), channel_id=1, replica_groups=mesh['z'=8,'yh'=2,'core'=2,'yl'=2,'x'=4] {'z','yh'}, dimensions={0} | all-to-all | bytes 1048576 | tf_op jit(solution)/shard_map/all_to_all | solution.py:136
  34.2 0.0 copy-start
  34.2 2.6 %collective-permute-start = (bf16[16,16,1024]{2,1,0:T(8,128)(2,1)S(1)}, bf16[16,16,1024]{2,1,0:T(8,128)(2,1)S(1)}, u32[]{:S(2)}, u32[]{:S(2)}) collective-permute-start(bf16[16,16,1024]{2,1,0:T(8,128)(2,1)S(1)} %all_to_all.21.own_ref.own_text_ref), channel_id=1, source_target_pairs={{0,8},{8,0},{1,9},{9,1},{2,10},{10,2},{3,11},{11,3},{4,12},{12,4},... | collective-permute-start | bytes 1572872 | tf_op jit(solution)/shard_map/ppermute | solution.py:126
  36.8 1.5 %collective-permute-done.other_ref.other_text_ref = bf16[16,16,1024]{2,1,0:T(8,128)(2,1)S(1)} collective-permute-done((bf16[16,16,1024]{2,1,0:T(8,128)(2,1)S(1)}, bf16[16,16,1024]{2,1,0:T(8,128)(2,1)S(1)}, u32[]{:S(2)}, u32[]{:S(2)}) %collective-permute-start) | collective-permute-done | bytes 524320 | tf_op jit(solution)/shard_map/ppermute | solution.py:126
  38.3 0.0 copy-start.1
  38.3 0.0 copy-done
  38.3 0.8 copy-done.1
  39.1 7.4 %shard_map.94 = (bf16[2,512,384]{2,1,0:T(8,128)(2,1)}, bf16[2,512,384]{2,1,0:T(8,128)(2,1)}, f32[16,16,768]{2,1,0:T(8,128)}, bf16[16,16,768]{2,1,0:T(8,128)(2,1)}) custom-call(s32[2]{0:T(128)} %lengths_ref.1, s32[1]{0:T(128)} %bitcast.core_ref, bf16[2,512,384]{2,1,0:T(8,128)(2,1)} %query_ref.1, bf16[2,512,384]{2,1,0:T(8,128)(2,1)} %grad_ref.1, ...), custom_call_target="tpu_custom_call" | custom-call | tf_op jit(solution)/shard_map/pallas_call | solution.py:118
  46.5 0.4 collective-permute-start.1
  46.9 1.6 %collective-permute-done.1.other_ref = bf16[16,16,768]{2,1,0:T(8,128)(2,1)S(1)} collective-permute-done((bf16[16,16,768]{2,1,0:T(8,128)(2,1)}, bf16[16,16,768]{2,1,0:T(8,128)(2,1)S(1)}, u32[]{:S(2)}, u32[]{:S(2)}) %collective-permute-start.1) | collective-permute-done | bytes 393248 | tf_op jit(solution)/shard_map/ppermute | solution.py:126
  48.4 0.0 copy-start.4
  48.4 0.7 copy-done.4
  49.2 2.1 %shard_map.95 = bf16[16,16,768]{2,1,0:T(8,128)(2,1)} custom-call(f32[16,16,768]{2,1,0:T(8,128)} %get-tuple-element.12.own_ref, bf16[16,16,768]{2,1,0:T(8,128)(2,1)} %copy-done.4), custom_call_target="tpu_custom_call" | custom-call | tf_op jit(solution)/shard_map/pallas_call | solution.py:118
  51.2 19.4 %all_to_all.22.parts_ref = bf16[16,16,768]{2,1,0:T(8,128)(2,1)} all-to-all(bf16[16,16,768]{2,1,0:T(8,128)(2,1)} %shard_map.95), channel_id=1, replica_groups=mesh['z'=8,'yh'=2,'core'=2,'yl'=2,'x'=4] {'z','yh'}, dimensions={0} | all-to-all | bytes 786432 | tf_op jit(solution)/shard_map/all_to_all | solution.py:145
  70.7 1.8 %shard_map.96 = bf16[16,16,768]{2,1,0:T(8,128)(2,1)} custom-call(bf16[16,16,768]{2,1,0:T(8,128)(2,1)} %all_to_all.22.parts_ref), custom_call_target="tpu_custom_call" | custom-call | tf_op jit(solution)/shard_map/pallas_call | solution.py:118
  72.5 17.5 %all_to_all.23.own_ref = bf16[16,16,768]{2,1,0:T(8,128)(2,1)S(1)} all-to-all(bf16[16,16,768]{2,1,0:T(8,128)(2,1)} %shard_map.96), channel_id=1, replica_groups=mesh['z'=8,'yh'=2,'core'=2,'yl'=2,'x'=4] {'z','yh'}, dimensions={0} | all-to-all | bytes 786432 | tf_op jit(solution)/shard_map/all_to_all | solution.py:146
  90.0 0.0 copy-start.2
  90.0 3.5 %collective-permute-start.2 = (bf16[16,16,768]{2,1,0:T(8,128)(2,1)S(1)}, bf16[16,16,768]{2,1,0:T(8,128)(2,1)S(1)}, u32[]{:S(2)}, u32[]{:S(2)}) collective-permute-start(bf16[16,16,768]{2,1,0:T(8,128)(2,1)S(1)} %all_to_all.23.own_ref), channel_id=1, source_target_pairs={{0,8},{8,0},{1,9},{9,1},{2,10},{10,2},{3,11},{11,3},{4,12},{12,4},... | collective-permute-start | bytes 1179656 | tf_op jit(solution)/shard_map/ppermute | solution.py:126
  93.5 1.3 %collective-permute-done.2.other_ref = bf16[16,16,768]{2,1,0:T(8,128)(2,1)S(1)} collective-permute-done((bf16[16,16,768]{2,1,0:T(8,128)(2,1)S(1)}, bf16[16,16,768]{2,1,0:T(8,128)(2,1)S(1)}, u32[]{:S(2)}, u32[]{:S(2)}) %collective-permute-start.2) | collective-permute-done | bytes 393248 | tf_op jit(solution)/shard_map/ppermute | solution.py:126
  94.9 0.0 copy-done.2
  94.9 0.0 copy-start.3
  94.9 0.8 copy-done.3
  95.6 2.5 %shard_map.97 = (f32[128,768]{1,0:T(8,128)}, f32[1,128]{1,0:T(1,128)}) custom-call(s32[1]{0:T(128)} %bitcast.core_ref, bf16[16,16,1024]{2,1,0:T(8,128)(2,1)} %copy-done, bf16[16,16,1024]{2,1,0:T(8,128)(2,1)} %copy-done.1, bf16[16,16,768]{2,1,0:T(8,128)(2,1)} %copy-done.2, bf16[16,16,768]{2,1,0:T(8,128)(2,1)} %copy-done.3), custom_call_target="tpu_custom_call" | custom-call | tf_op jit(solution)/shard_map/pallas_call | solution.py:118
  98.1 1.3 %reduce_sum.18 = f32[]{:T(128)} reduce(f32[1,128]{1,0:T(1,128)} %get-tuple-element.15, f32[]{:T(128)} %constant.12.clone.1), dimensions={0,1}, to_apply=%region_0.0 | reduce | flops 127 | bytes 520 | tf_op jit(solution)/shard_map/reduce_sum | solution.py:153
  99.4 0.7 broadcast_in_dim.3
  100.1 18.9 %all_to_all.24 = f32[256,1,1]{2,1,0:T(1,128)S(1)} all-to-all(f32[256,1,1]{2,1,0:T(1,128)S(1)} %broadcast_in_dim.3), channel_id=1, replica_groups=mesh['z'=8,'yh'=2,'core'=2,'yl'=2,'x'=4] {'z','yh','core','yl','x'}, dimensions={0} | all-to-all | bytes 2048 | tf_op jit(solution)/shard_map/all_to_all | solution.py:154
  119.0 0.9 reduce_sum.19
  120.6 1.8 %slice_multiply_fusion = (f32[128,384]{1,0:T(8,128)}, f32[128,384]{1,0:T(8,128)}) fusion(f32[128,768]{1,0:T(8,128)} %get-tuple-element.14, f32[]{:T(128)S(6)} %div.7), kind=kLoop, calls=%fused_computation | loop fusion | flops 98304 | bytes 786436 | tf_op jit(solution)/shard_map/mul | solution.py:157
Async XLA Ops:
  34.2 4.1 %copy-start = (bf16[16,16,1024]{2,1,0:T(8,128)(2,1)}, bf16[16,16,1024]{2,1,0:T(8,128)(2,1)S(1)}, u32[]{:S(2)}) copy-start(bf16[16,16,1024]{2,1,0:T(8,128)(2,1)S(1)} %all_to_all.21.own_ref.own_text_ref) | copy-start | bytes 1572868
  34.2 4.1 %collective-permute-start = (bf16[16,16,1024]{2,1,0:T(8,128)(2,1)S(1)}, bf16[16,16,1024]{2,1,0:T(8,128)(2,1)S(1)}, u32[]{:S(2)}, u32[]{:S(2)}) collective-permute-start(bf16[16,16,1024]{2,1,0:T(8,128)(2,1)S(1)} %all_to_all.21.own_ref.own_text_ref), channel_id=1, source_target_pairs={{0,8},{8,0},{1,9},{9,1},{2,10},{10,2},{3,11},{11,3},{4,12},{12,4},... | collective-permute-start | bytes 1572872 | tf_op jit(solution)/shard_map/ppermute | solution.py:126
  38.3 0.8 copy-start.1
  46.5 1.9 %collective-permute-start.1 = (bf16[16,16,768]{2,1,0:T(8,128)(2,1)}, bf16[16,16,768]{2,1,0:T(8,128)(2,1)S(1)}, u32[]{:S(2)}, u32[]{:S(2)}) collective-permute-start(bf16[16,16,768]{2,1,0:T(8,128)(2,1)} %get-tuple-element.13), channel_id=1, source_target_pairs={{0,8},{8,0},{1,9},{9,1},{2,10},{10,2},{3,11},{11,3},{4,12},{12,4},... | collective-permute-start | bytes 1179656 | tf_op jit(solution)/shard_map/ppermute | solution.py:126
  48.4 0.7 copy-start.4
  90.0 4.9 %copy-start.2 = (bf16[16,16,768]{2,1,0:T(8,128)(2,1)}, bf16[16,16,768]{2,1,0:T(8,128)(2,1)S(1)}, u32[]{:S(2)}) copy-start(bf16[16,16,768]{2,1,0:T(8,128)(2,1)S(1)} %all_to_all.23.own_ref) | copy-start | bytes 1179652
  90.0 4.9 %collective-permute-start.2 = (bf16[16,16,768]{2,1,0:T(8,128)(2,1)S(1)}, bf16[16,16,768]{2,1,0:T(8,128)(2,1)S(1)}, u32[]{:S(2)}, u32[]{:S(2)}) collective-permute-start(bf16[16,16,768]{2,1,0:T(8,128)(2,1)S(1)} %all_to_all.23.own_ref), channel_id=1, source_target_pairs={{0,8},{8,0},{1,9},{9,1},{2,10},{10,2},{3,11},{11,3},{4,12},{12,4},... | collective-permute-start | bytes 1179656 | tf_op jit(solution)/shard_map/ppermute | solution.py:126
  94.9 0.8 copy-start.3

commit v2 on v1

--- a/solution.py
+++ b/solution.py
@@ -12,6 +12,7 @@
 DT = 4096
 HEADS = 24
 HEAD = 128
+CHUNKS = 8
 ZY = ("z", "yh")
 SEQ = ("z", "yh", "core")
 TP = ("yl", "x")
@@ -25,13 +26,26 @@
     return lax.dot_general(a, b, (((ca,), (cb,)), ((), ())), preferred_element_type=F32)
 
 
-def project_kernel(text_ref, key_ref, value_ref, out_ref):
+def project_kernel(text_ref, key_ref, value_ref, out_ref, held_ref, arrived):
     groups = out_ref.shape[0]
     features = key_ref.shape[1]
+    step = DT // CHUNKS
+    copies = []
+    for at in range(CHUNKS):
+        rows = pl.ds(at * step, step)
+        for which, ref in enumerate((key_ref, value_ref)):
+            copy = pltpu.make_async_copy(ref.at[rows], held_ref.at[which, rows], arrived.at[which, at])
+            copy.start()
+            copies.append(copy)
     text = text_ref[...].reshape(-1, DT)
-    key = dot(text, key_ref[...], 1, 0).astype(BF16)
-    value = dot(text, value_ref[...], 1, 0).astype(BF16)
-    both = jnp.concatenate([key, value], axis=-1)
+    sums = [None, None]
+    for at in range(CHUNKS):
+        rows = slice(at * step, (at + 1) * step)
+        for which in range(2):
+            copies[2 * at + which].wait()
+            part = dot(text[:, rows], held_ref[which, rows], 1, 0)
+            sums[which] = part if sums[which] is None else sums[which] + part
+    both = jnp.concatenate([total.astype(BF16) for total in sums], axis=-1)
     wide = DT // groups
     for g in range(groups):
         out_ref[g, :, : 2 * features] = both
@@ -110,12 +124,17 @@
     square_ref[...] = jnp.sum(lanes, axis=0, keepdims=True)
 
 
-def call(kernel, out, *args, scalars=0):
+def call(kernel, out, *args, scalars=0, far=0, scratch=(), mib=12, flops=0):
     specs = [pl.BlockSpec(memory_space=pltpu.SMEM)] * scalars
-    specs += [pl.BlockSpec(memory_space=pltpu.VMEM)] * (len(args) - scalars)
+    specs += [pl.BlockSpec(memory_space=pltpu.VMEM)] * (len(args) - scalars - far)
+    specs += [pl.BlockSpec(memory_space=pltpu.HBM)] * far
     one = pl.BlockSpec(memory_space=pltpu.VMEM)
     out_specs = one if isinstance(out, jax.ShapeDtypeStruct) else [one] * len(out)
-    return pl.pallas_call(kernel, out_shape=out, in_specs=specs, out_specs=out_specs)(*args)
+    return pl.pallas_call(
+        kernel, out_shape=out, in_specs=specs, out_specs=out_specs, scratch_shapes=scratch,
+        compiler_params=pltpu.CompilerParams(vmem_limit_bytes=mib << 20),
+        cost_estimate=pl.CostEstimate(flops=flops, bytes_accessed=0, transcendentals=0) if flops else None,
+    )(*args)
 
 
 def shape(dims, dtype):
@@ -132,7 +151,10 @@
     groups = lax.axis_size(ZY)
     wide = 2 * features
     core = lax.axis_index("core").astype(jnp.int32).reshape(1)
-    packed = call(project_kernel, shape((groups, text_rows, wide + DT // groups), BF16), text_states, key_weight, value_weight)
+    packed = call(
+        project_kernel, shape((groups, text_rows, wide + DT // groups), BF16), text_states, key_weight, value_weight, far=2, mib=61,
+        scratch=[pltpu.VMEM((2, DT, features), BF16), pltpu.SemaphoreType.DMA((2, CHUNKS))],
+    )
     own = lax.all_to_all(packed, ZY, 0, 0, tiled=True)
     other = swap(own)
     like = shape(video_query.shape, BF16)

time: 123 us -> 110 us (0.89)
  Pallas kernels: 18.4 us -> 11.9 us
  local copies, waits for them, and re-layouts: 3.02 us -> 0.73 us
  other arithmetic: 3.92 us -> 2.25 us
    pallas_call x5, Pallas kernels: 18.4 us -> 11.9 us  [call(): pl.pallas_call(kernel, out_shape=out, in_specs=specs, out_specs=out_specs...]
    unnamed x10 -> x6, local copies, waits for them, and re-layouts: 2.31 us -> 0.01 us
    all_to_all x1, blocking collectives: 19.4 us -> 17.6 us  [per_device(): parts = lax.all_to_all(pair, ZY, 0, 0, tiled=True)]
where the time goes in v2:
time: 110 us
  blocking collectives  83.7 us (76%)
  Pallas kernels  11.9 us (11%)
  starting transfers between devices  5.72 us (5%)
  waiting for transfers between devices  4.24 us (4%)
  other arithmetic  2.25 us (2%)
  between operations  1.42 us (1%)
    all_to_all x1, blocking collectives, per_device(): own = lax.all_to_all(packed, ZY, 0, 0, tiled=True)  29 us
    all_to_all x1, blocking collectives, per_device(): lax.all_to_all(jnp.full((every, 1), local), ALL, 0, 0, tiled=True)  19 us
    all_to_all x1, blocking collectives, per_device(): lax.all_to_all(call(total_kernel, shape(block, BF16), parts), ZY, 0, 0, t...  18.2 us
    all_to_all x1, blocking collectives, per_device(): parts = lax.all_to_all(pair, ZY, 0, 0, tiled=True)  17.6 us
    pallas_call x5, Pallas kernels, call(): pl.pallas_call(kernel, out_shape=out, in_specs=specs, out_specs=out_specs...  11.9 us
    ppermute x3, starting transfers between devices, swap(): return lax.ppermute(array, 'core', [(0, 1), (1, 0)])  5.72 us
    ppermute x3, waiting for transfers between devices, swap(): return lax.ppermute(array, 'core', [(0, 1), (1, 0)])  4.24 us
  transfers between devices with their start and end apart: 3, of which 3 were waited for; matrix products, arithmetic and copies ran while one was open for 0% of the time, Pallas kernels for 0%

profile of v2, /device:TPU:1, one launch (start us, length us, event | category | flops | bytes accessed | tf_op | source)
XLA Modules:
  0.0 110.0 jit_solution(8184336882228303929)
XLA Ops:
  0.6 0.0 copy-start.1
  0.6 0.0 copy-start.2
  0.7 0.0 copy-start
  0.7 5.5 %shard_map.93 = bf16[16,16,1024]{2,1,0:T(8,128)(2,1)} custom-call(bf16[2,8,4096]{2,1,0:T(8,128)(2,1)} %text_ref.1, bf16[4096,384]{1,0:T(8,128)(2,1)} %key_ref.1, bf16[4096,384]{1,0:T(8,128)(2,1)} %value_ref.1), custom_call_target="tpu_custom_call" | custom-call | tf_op jit(solution)/shard_map/pallas_call | solution.py:133
  6.2 29.0 %all_to_all.21.own_ref.own_text_ref = bf16[16,16,1024]{2,1,0:T(8,128)(2,1)S(1)} all-to-all(bf16[16,16,1024]{2,1,0:T(8,128)(2,1)} %shard_map.93), channel_id=1, replica_groups=mesh['z'=8,'yh'=2,'core'=2,'yl'=2,'x'=4] {'z','yh'}, dimensions={0} | all-to-all | bytes 1048576 | tf_op jit(solution)/shard_map/all_to_all | solution.py:158
  35.2 2.6 %collective-permute-start = (bf16[16,16,1024]{2,1,0:T(8,128)(2,1)S(1)}, bf16[16,16,1024]{2,1,0:T(8,128)(2,1)S(1)}, u32[]{:S(2)}, u32[]{:S(2)}) collective-permute-start(bf16[16,16,1024]{2,1,0:T(8,128)(2,1)S(1)} %all_to_all.21.own_ref.own_text_ref), channel_id=1, source_target_pairs={{0,8},{8,0},{1,9},{9,1},{2,10},{10,2},{3,11},{11,3},{4,12},{12,4},... | collective-permute-start | bytes 1572872 | tf_op jit(solution)/shard_map/ppermute | solution.py:145
  37.7 1.5 %collective-permute-done.other_ref.other_text_ref = bf16[16,16,1024]{2,1,0:T(8,128)(2,1)S(1)} collective-permute-done((bf16[16,16,1024]{2,1,0:T(8,128)(2,1)S(1)}, bf16[16,16,1024]{2,1,0:T(8,128)(2,1)S(1)}, u32[]{:S(2)}, u32[]{:S(2)}) %collective-permute-start) | collective-permute-done | bytes 524320 | tf_op jit(solution)/shard_map/ppermute | solution.py:145
  39.3 0.0 copy-done.1
  39.3 0.0 copy-done.2
  39.3 0.0 copy-done
  39.3 6.0 %shard_map.94 = (bf16[2,512,384]{2,1,0:T(8,128)(2,1)}, bf16[2,512,384]{2,1,0:T(8,128)(2,1)}, f32[16,16,768]{2,1,0:T(8,128)S(1)}, bf16[16,16,768]{2,1,0:T(8,128)(2,1)S(1)}) custom-call(s32[2]{0:T(128)S(1)} %copy-done.2, s32[1]{0:T(128)} %bitcast.core_ref, bf16[2,512,384]{2,1,0:T(8,128)(2,1)S(1)} %copy-done, bf16[2,512,384]{2,1,0:T(8,128)(2,1)S(1)} %copy-done.1, ...), custom_call_target="tpu_custom_call" | custom-call | tf_op jit(solution)/shard_map/pallas_call | solution.py:133
  45.2 0.4 collective-permute-start.1
  45.6 1.3 %collective-permute-done.1.other_ref = bf16[16,16,768]{2,1,0:T(8,128)(2,1)S(1)} collective-permute-done((bf16[16,16,768]{2,1,0:T(8,128)(2,1)S(1)}, bf16[16,16,768]{2,1,0:T(8,128)(2,1)S(1)}, u32[]{:S(2)}, u32[]{:S(2)}) %collective-permute-start.1) | collective-permute-done | bytes 393248 | tf_op jit(solution)/shard_map/ppermute | solution.py:145
  46.9 0.1 shard_map.95
  47.0 17.6 %all_to_all.22.parts_ref = bf16[16,16,768]{2,1,0:T(8,128)(2,1)S(1)} all-to-all(bf16[16,16,768]{2,1,0:T(8,128)(2,1)S(1)} %shard_map.95), channel_id=1, replica_groups=mesh['z'=8,'yh'=2,'core'=2,'yl'=2,'x'=4] {'z','yh'}, dimensions={0} | all-to-all | bytes 786432 | tf_op jit(solution)/shard_map/all_to_all | solution.py:167
  64.6 0.1 shard_map.96
  64.7 18.2 %all_to_all.23.own_ref = bf16[16,16,768]{2,1,0:T(8,128)(2,1)S(1)} all-to-all(bf16[16,16,768]{2,1,0:T(8,128)(2,1)S(1)} %shard_map.96), channel_id=1, replica_groups=mesh['z'=8,'yh'=2,'core'=2,'yl'=2,'x'=4] {'z','yh'}, dimensions={0} | all-to-all | bytes 786432 | tf_op jit(solution)/shard_map/all_to_all | solution.py:168
  82.9 2.8 %collective-permute-start.2 = (bf16[16,16,768]{2,1,0:T(8,128)(2,1)S(1)}, bf16[16,16,768]{2,1,0:T(8,128)(2,1)S(1)}, u32[]{:S(2)}, u32[]{:S(2)}) collective-permute-start(bf16[16,16,768]{2,1,0:T(8,128)(2,1)S(1)} %all_to_all.23.own_ref), channel_id=1, source_target_pairs={{0,8},{8,0},{1,9},{9,1},{2,10},{10,2},{3,11},{11,3},{4,12},{12,4},... | collective-permute-start | bytes 1179656 | tf_op jit(solution)/shard_map/ppermute | solution.py:145
  85.7 1.3 %collective-permute-done.2.other_ref = bf16[16,16,768]{2,1,0:T(8,128)(2,1)S(1)} collective-permute-done((bf16[16,16,768]{2,1,0:T(8,128)(2,1)S(1)}, bf16[16,16,768]{2,1,0:T(8,128)(2,1)S(1)}, u32[]{:S(2)}, u32[]{:S(2)}) %collective-permute-start.2) | collective-permute-done | bytes 393248 | tf_op jit(solution)/shard_map/ppermute | solution.py:145
  87.0 0.3 shard_map.97
  87.3 0.6 reduce_sum.18
  87.9 0.7 broadcast_in_dim.3
  88.7 19.0 %all_to_all.24 = f32[256,1,1]{2,1,0:T(1,128)S(1)} all-to-all(f32[256,1,1]{2,1,0:T(1,128)S(1)} %broadcast_in_dim.3), channel_id=1, replica_groups=mesh['z'=8,'yh'=2,'core'=2,'yl'=2,'x'=4] {'z','yh','core','yl','x'}, dimensions={0} | all-to-all | bytes 2048 | tf_op jit(solution)/shard_map/all_to_all | solution.py:176
  107.6 0.9 reduce_sum.19
  109.2 0.8 slice_multiply_fusion
Async XLA Ops:
  0.6 38.6 %copy-start.1 = (bf16[2,512,384]{2,1,0:T(8,128)(2,1)S(1)}, bf16[2,512,384]{2,1,0:T(8,128)(2,1)}, u32[]{:S(2)}) copy-start(bf16[2,512,384]{2,1,0:T(8,128)(2,1)} %grad_ref.1) | copy-start | bytes 2359300
  0.6 38.6 %copy-start.2 = (s32[2]{0:T(128)S(1)}, s32[2]{0:T(128)}, u32[]{:S(2)}) copy-start(s32[2]{0:T(128)} %lengths_ref.1) | copy-start | bytes 28
  0.7 38.6 %copy-start = (bf16[2,512,384]{2,1,0:T(8,128)(2,1)S(1)}, bf16[2,512,384]{2,1,0:T(8,128)(2,1)}, u32[]{:S(2)}) copy-start(bf16[2,512,384]{2,1,0:T(8,128)(2,1)} %query_ref.1) | copy-start | bytes 2359300
  35.2 4.1 %collective-permute-start = (bf16[16,16,1024]{2,1,0:T(8,128)(2,1)S(1)}, bf16[16,16,1024]{2,1,0:T(8,128)(2,1)S(1)}, u32[]{:S(2)}, u32[]{:S(2)}) collective-permute-start(bf16[16,16,1024]{2,1,0:T(8,128)(2,1)S(1)} %all_to_all.21.own_ref.own_text_ref), channel_id=1, source_target_pairs={{0,8},{8,0},{1,9},{9,1},{2,10},{10,2},{3,11},{11,3},{4,12},{12,4},... | collective-permute-start | bytes 1572872 | tf_op jit(solution)/shard_map/ppermute | solution.py:145
  45.2 1.7 %collective-permute-start.1 = (bf16[16,16,768]{2,1,0:T(8,128)(2,1)S(1)}, bf16[16,16,768]{2,1,0:T(8,128)(2,1)S(1)}, u32[]{:S(2)}, u32[]{:S(2)}) collective-permute-start(bf16[16,16,768]{2,1,0:T(8,128)(2,1)S(1)} %get-tuple-element.13), channel_id=1, source_target_pairs={{0,8},{8,0},{1,9},{9,1},{2,10},{10,2},{3,11},{11,3},{4,12},{12,4},... | collective-permute-start | bytes 1179656 | tf_op jit(solution)/shard_map/ppermute | solution.py:145
  82.9 4.1 %collective-permute-start.2 = (bf16[16,16,768]{2,1,0:T(8,128)(2,1)S(1)}, bf16[16,16,768]{2,1,0:T(8,128)(2,1)S(1)}, u32[]{:S(2)}, u32[]{:S(2)}) collective-permute-start(bf16[16,16,768]{2,1,0:T(8,128)(2,1)S(1)} %all_to_all.23.own_ref), channel_id=1, source_target_pairs={{0,8},{8,0},{1,9},{9,1},{2,10},{10,2},{3,11},{11,3},{4,12},{12,4},... | collective-permute-start | bytes 1179656 | tf_op jit(solution)/shard_map/ppermute | solution.py:145

commit v3 on v2

--- a/solution.py
+++ b/solution.py
@@ -52,7 +52,13 @@
         out_ref[g, :, 2 * features :] = text[:, g * wide : (g + 1) * wide]
 
 
-def attend_kernel(lengths_ref, core_ref, query_ref, grad_ref, own_ref, other_ref, attended_ref, query_grad_ref, own_sum_ref, other_sum_ref):
+def text_of(own_ref, other_ref, b, first):
+    half = own_ref.shape[0] * 8
+    pieces = [ref[:, b * 8 : (b + 1) * 8, first : first + HEAD].reshape(half, HEAD) for ref in (own_ref, other_ref)]
+    return jnp.concatenate(pieces, axis=0)
+
+
+def score_kernel(lengths_ref, core_ref, query_ref, grad_ref, own_ref, other_ref, own_sum_ref, other_sum_ref, probs_ref, dscore_ref):
     samples, rows, features = query_ref.shape
     groups = own_ref.shape[0]
     heads = features // HEAD
@@ -63,11 +69,6 @@
     side = jnp.where(place < half, core, 1 - core)
     token = (within // 8) * 16 + side * 8 + within % 8
 
-    def text_of(b, first):
-        cols = slice(first, first + HEAD)
-        pieces = [ref[:, b * 8 : (b + 1) * 8, cols].reshape(half, HEAD) for ref in (own_ref, other_ref)]
-        return jnp.concatenate(pieces, axis=0)
-
     def put_sum(value, b, first):
         cols = slice(first, first + HEAD)
         own_sum_ref[:, b * 8 : (b + 1) * 8, cols] = value[:half].reshape(groups, 8, HEAD)
@@ -77,8 +78,8 @@
         allowed = token < lengths_ref[b]
         for h in range(heads):
             cols = slice(h * HEAD, (h + 1) * HEAD)
-            key = text_of(b, h * HEAD)
-            value = text_of(b, features + h * HEAD)
+            key = text_of(own_ref, other_ref, b, h * HEAD)
+            value = text_of(own_ref, other_ref, b, features + h * HEAD)
             query = query_ref[b, :, cols]
             grad = grad_ref[b, :, cols]
             scores = dot(key, query, 1, 1) * SCALING
@@ -91,8 +92,20 @@
             dscore = (probs * (dprob - delta) * SCALING).astype(BF16)
             put_sum(dot(dscore, query, 1, 0), b, h * HEAD)
             put_sum(dot(probs_low, grad, 1, 0), b, features + h * HEAD)
-            attended_ref[b, :, cols] = dot(probs_low, value, 0, 0).astype(BF16)
-            query_grad_ref[b, :, cols] = dot(dscore, key, 0, 0).astype(BF16)
+            probs_ref[b, h] = probs_low
+            dscore_ref[b, h] = dscore
+
+
+def attend_kernel(own_ref, other_ref, probs_ref, dscore_ref, attended_ref, query_grad_ref):
+    samples, heads = probs_ref.shape[:2]
+    features = heads * HEAD
+    for b in range(samples):
+        for h in range(heads):
+            cols = slice(h * HEAD, (h + 1) * HEAD)
+            value = text_of(own_ref, other_ref, b, features + h * HEAD)
+            attended_ref[b, :, cols] = dot(probs_ref[b, h], value, 0, 0).astype(BF16)
+            key = text_of(own_ref, other_ref, b, h * HEAD)
+            query_grad_ref[b, :, cols] = dot(dscore_ref[b, h], key, 0, 0).astype(BF16)
 
 
 def pair_sum_kernel(own_ref, other_ref, out_ref):
@@ -121,7 +134,16 @@
     lanes = squares[:, :HEAD]
     for at in range(HEAD, width, HEAD):
         lanes = lanes + squares[:, at : at + HEAD]
-    square_ref[...] = jnp.sum(lanes, axis=0, keepdims=True)
+    square_ref[...] = jnp.broadcast_to(jnp.sum(lanes, keepdims=True), square_ref.shape)
+
+
+def scale_kernel(raw_ref, squares_ref, key_ref, value_ref):
+    overall = jnp.sum(squares_ref[...], keepdims=True)
+    spread = jnp.sqrt(overall / (2.0 * DT * HEADS * HEAD) + 1e-06)
+    factor = 1.0 / jnp.maximum(spread, 1.0)
+    features = key_ref.shape[1]
+    key_ref[...] = raw_ref[:, :features] * factor
+    value_ref[...] = raw_ref[:, features:] * factor
 
 
 def call(kernel, out, *args, scalars=0, far=0, scratch=(), mib=12, flops=0):
@@ -159,24 +181,26 @@
     other = swap(own)
     like = shape(video_query.shape, BF16)
     block = (groups, text_rows, wide)
-    attended, query_grad, own_sum, other_sum = call(
-        attend_kernel, [like, like, shape(block, F32), shape(block, BF16)],
-        text_lengths, core, video_query, output_grad, own, other, scalars=2,
-    )
+    tall = shape((samples, features // HEAD, 2 * groups * 8, video_rows), BF16)
+    flops = 4 * samples * features * video_rows * 2 * groups * 8
+    own_sum, other_sum, probs, dscore = call(
+        score_kernel, [shape(block, F32), shape(block, BF16), tall, tall],
+        text_lengths, core, video_query, output_grad, own, other, scalars=2, flops=2 * flops,
+    )
+    attended, query_grad = call(attend_kernel, [like, like], own, other, probs, dscore, flops=flops)
     pair = call(pair_sum_kernel, shape(block, BF16), own_sum, swap(other_sum))
     parts = lax.all_to_all(pair, ZY, 0, 0, tiled=True)
     own_total = lax.all_to_all(call(total_kernel, shape(block, BF16), parts), ZY, 0, 0, tiled=True)
     other_total = swap(own_total)
+    every = lax.axis_size(ALL)
     raw, squares = call(
-        weight_kernel, [shape((HEAD, wide), F32), shape((1, HEAD), F32)],
+        weight_kernel, [shape((HEAD, wide), F32), shape((every, 1), F32)],
         core, own, other, own_total, other_total, scalars=1,
     )
-    every = lax.axis_size(ALL)
-    local = jnp.sum(squares)
-    overall = jnp.sum(lax.all_to_all(jnp.full((every, 1), local), ALL, 0, 0, tiled=True))
-    spread = jnp.sqrt(overall / (2.0 * DT * HEADS * HEAD) + 1e-06)
-    factor = 1.0 / jnp.maximum(spread, 1.0)
-    return (attended, query_grad, raw[:, :features] * factor, raw[:, features:] * factor)
+    squares = lax.all_to_all(squares, ALL, 0, 0, tiled=True)
+    weight = shape((HEAD, features), F32)
+    key_weight_grad, value_weight_grad = call(scale_kernel, [weight, weight], raw, squares)
+    return attended, query_grad, key_weight_grad, value_weight_grad
 
 
 def solution(mesh):

time: 110 us -> 108 us (0.982)
  blocking collectives: 83.7 us -> 64.8 us
  waiting for transfers between devices: 4.24 us -> 13.5 us
  starting transfers between devices: 5.72 us -> 12 us
  other arithmetic: 2.25 us -> 0 us
  Pallas kernels: 11.9 us -> 13.9 us
  local copies, waits for them, and re-layouts: 0.73 us -> 2.55 us
    all_to_all x1 -> x0, blocking collectives: 19 us -> none  [per_device(): lax.all_to_all(jnp.full((every, 1), local), ALL, 0, 0, tiled=True)]
    all_to_all x0 -> x1, waiting for transfers between devices: none -> 9.25 us  [per_device(): squares = lax.all_to_all(squares, ALL, 0, 0, tiled=True)]
    all_to_all x0 -> x1, starting transfers between devices: none -> 6.23 us  [per_device(): squares = lax.all_to_all(squares, ALL, 0, 0, tiled=True)]
    unnamed x6 -> x10, local copies, waits for them, and re-layouts: 0.01 us -> 2.55 us
    pallas_call x5 -> x7, Pallas kernels: 11.9 us -> 13.9 us  [call(): pl.pallas_call(kernel, out_shape=out, in_specs=specs, out_specs=out_specs...]
    reduce_sum x2 -> x0, other arithmetic: 1.48 us -> none  [the longest x1 0.87 us: per_device(): jnp.sum(lax.all_to_all(jnp.full((every, 1), local), ALL, 0, 0, tiled=True))]
  transfers between devices with their start and end apart: 3 -> 4, of which waited for: 3 -> 4; matrix products, arithmetic and copies ran while one was open for 0% -> 0% of each run, Pallas kernels for 0% -> 2%
where the time goes in v3:
time: 108 us; the launch traced here: 107 us
  blocking collectives  64.8 us (60%)
  Pallas kernels  13.9 us (13%)
  waiting for transfers between devices  13.5 us (12%)
  starting transfers between devices  12 us (11%)
  local copies, waits for them, and re-layouts  2.55 us (2%)
    all_to_all x1, blocking collectives, per_device(): own = lax.all_to_all(packed, ZY, 0, 0, tiled=True)  29 us
    all_to_all x1, blocking collectives, per_device(): lax.all_to_all(call(total_kernel, shape(block, BF16), parts), ZY, 0, 0, t...  18.2 us
    all_to_all x1, blocking collectives, per_device(): parts = lax.all_to_all(pair, ZY, 0, 0, tiled=True)  17.6 us
    pallas_call x7, Pallas kernels, call(): pl.pallas_call(kernel, out_shape=out, in_specs=specs, out_specs=out_specs...  13.9 us
    all_to_all x1, waiting for transfers between devices, per_device(): squares = lax.all_to_all(squares, ALL, 0, 0, tiled=True)  9.25 us
    all_to_all x1, starting transfers between devices, per_device(): squares = lax.all_to_all(squares, ALL, 0, 0, tiled=True)  6.23 us
    ppermute x3, starting transfers between devices, swap(): return lax.ppermute(array, 'core', [(0, 1), (1, 0)])  5.8 us
    ppermute x3, waiting for transfers between devices, swap(): return lax.ppermute(array, 'core', [(0, 1), (1, 0)])  4.24 us
  transfers between devices with their start and end apart: 4, of which 4 were waited for; matrix products, arithmetic and copies ran while one was open for 0% of the time, Pallas kernels for 2%

profile of v3, /device:TPU:1, one launch (start us, length us, event | category | flops | bytes accessed | tf_op | source)
XLA Modules:
  0.0 107.5 jit_solution(5155713501112340050)
XLA Ops:
  0.6 0.0 copy-start.4
  0.6 0.0 copy-start.2
  0.7 5.5 %shard_map.93 = bf16[16,16,1024]{2,1,0:T(8,128)(2,1)} custom-call(bf16[2,8,4096]{2,1,0:T(8,128)(2,1)} %text_ref.1, bf16[4096,384]{1,0:T(8,128)(2,1)} %key_ref.1, bf16[4096,384]{1,0:T(8,128)(2,1)} %value_ref.1), custom_call_target="tpu_custom_call" | custom-call | tf_op jit(solution)/shard_map/pallas_call | solution.py:155
  6.1 29.0 %all_to_all.26.own_ref.own_text_ref = bf16[16,16,1024]{2,1,0:T(8,128)(2,1)S(1)} all-to-all(bf16[16,16,1024]{2,1,0:T(8,128)(2,1)} %shard_map.93), channel_id=1, replica_groups=mesh['z'=8,'yh'=2,'core'=2,'yl'=2,'x'=4] {'z','yh'}, dimensions={0} | all-to-all | bytes 1048576 | tf_op jit(solution)/shard_map/all_to_all | solution.py:180
  35.1 2.6 %collective-permute-start = (bf16[16,16,1024]{2,1,0:T(8,128)(2,1)S(1)}, bf16[16,16,1024]{2,1,0:T(8,128)(2,1)S(1)}, u32[]{:S(2)}, u32[]{:S(2)}) collective-permute-start(bf16[16,16,1024]{2,1,0:T(8,128)(2,1)S(1)} %all_to_all.26.own_ref.own_text_ref), channel_id=1, source_target_pairs={{0,8},{8,0},{1,9},{9,1},{2,10},{10,2},{3,11},{11,3},{4,12},{12,4},... | collective-permute-start | bytes 1572872 | tf_op jit(solution)/shard_map/ppermute | solution.py:167
  37.7 1.5 %collective-permute-done.other_ref.other_text_ref = bf16[16,16,1024]{2,1,0:T(8,128)(2,1)S(1)} collective-permute-done((bf16[16,16,1024]{2,1,0:T(8,128)(2,1)S(1)}, bf16[16,16,1024]{2,1,0:T(8,128)(2,1)S(1)}, u32[]{:S(2)}, u32[]{:S(2)}) %collective-permute-start) | collective-permute-done | bytes 524320 | tf_op jit(solution)/shard_map/ppermute | solution.py:167
  39.2 0.0 copy-done.4
  39.2 0.0 copy-done.2
  39.2 0.0 copy-start.3
  39.2 1.1 %copy-done.3 = bf16[2,512,384]{2,1,0:T(8,128)(2,1)S(1)} copy-done((bf16[2,512,384]{2,1,0:T(8,128)(2,1)S(1)}, bf16[2,512,384]{2,1,0:T(8,128)(2,1)}, u32[]{:S(2)}) %copy-start.3) | copy-done | bytes 786456
  40.3 4.1 %shard_map.94 = (f32[16,16,768]{2,1,0:T(8,128)S(1)}, bf16[16,16,768]{2,1,0:T(8,128)(2,1)S(1)}, bf16[2,3,256,512]{3,2,1,0:T(8,128)(2,1)S(1)}, bf16[2,3,256,512]{3,2,1,0:T(8,128)(2,1)S(1)}) custom-call(s32[2]{0:T(128)S(1)} %copy-done.4, s32[1]{0:T(128)} %bitcast.core_ref, bf16[2,512,384]{2,1,0:T(8,128)(2,1)S(1)} %copy-done.2, ...), custom_call_target="tpu_custom_call" | custom-call | flops 805306368 | tf_op jit(solution)/shard_map/pallas_call | solution.py:155
  44.5 0.0 copy-start
  44.5 0.5 collective-permute-start.1
  44.9 1.4 %collective-permute-done.1.other_ref = bf16[16,16,768]{2,1,0:T(8,128)(2,1)S(1)} collective-permute-done((bf16[16,16,768]{2,1,0:T(8,128)(2,1)S(1)}, bf16[16,16,768]{2,1,0:T(8,128)(2,1)S(1)}, u32[]{:S(2)}, u32[]{:S(2)}) %collective-permute-start.1) | collective-permute-done | bytes 393248 | tf_op jit(solution)/shard_map/ppermute | solution.py:167
  46.3 0.1 shard_map.96
  46.4 17.6 %all_to_all.27.parts_ref = bf16[16,16,768]{2,1,0:T(8,128)(2,1)S(1)} all-to-all(bf16[16,16,768]{2,1,0:T(8,128)(2,1)S(1)} %shard_map.96), channel_id=1, replica_groups=mesh['z'=8,'yh'=2,'core'=2,'yl'=2,'x'=4] {'z','yh'}, dimensions={0} | all-to-all | bytes 786432 | tf_op jit(solution)/shard_map/all_to_all | solution.py:192
  64.0 0.1 shard_map.97
  64.1 18.2 %all_to_all.28.own_ref = bf16[16,16,768]{2,1,0:T(8,128)(2,1)S(1)} all-to-all(bf16[16,16,768]{2,1,0:T(8,128)(2,1)S(1)} %shard_map.97), channel_id=1, replica_groups=mesh['z'=8,'yh'=2,'core'=2,'yl'=2,'x'=4] {'z','yh'}, dimensions={0} | all-to-all | bytes 786432 | tf_op jit(solution)/shard_map/all_to_all | solution.py:193
  82.3 2.8 %collective-permute-start.2 = (bf16[16,16,768]{2,1,0:T(8,128)(2,1)S(1)}, bf16[16,16,768]{2,1,0:T(8,128)(2,1)S(1)}, u32[]{:S(2)}, u32[]{:S(2)}) collective-permute-start(bf16[16,16,768]{2,1,0:T(8,128)(2,1)S(1)} %all_to_all.28.own_ref), channel_id=1, source_target_pairs={{0,8},{8,0},{1,9},{9,1},{2,10},{10,2},{3,11},{11,3},{4,12},{12,4},... | collective-permute-start | bytes 1179656 | tf_op jit(solution)/shard_map/ppermute | solution.py:167
  85.0 1.3 %collective-permute-done.2.other_ref = bf16[16,16,768]{2,1,0:T(8,128)(2,1)S(1)} collective-permute-done((bf16[16,16,768]{2,1,0:T(8,128)(2,1)S(1)}, bf16[16,16,768]{2,1,0:T(8,128)(2,1)S(1)}, u32[]{:S(2)}, u32[]{:S(2)}) %collective-permute-start.2) | collective-permute-done | bytes 393248 | tf_op jit(solution)/shard_map/ppermute | solution.py:167
  86.4 1.1 %shard_map.98 = (f32[128,768]{1,0:T(8,128)S(1)}, f32[256,1]{1,0:T(8,128)}) custom-call(s32[1]{0:T(128)} %bitcast.core_ref, bf16[16,16,1024]{2,1,0:T(8,128)(2,1)S(1)} %all_to_all.26.own_ref.own_text_ref, bf16[16,16,1024]{2,1,0:T(8,128)(2,1)S(1)} %collective-permute-done.other_ref.other_text_ref, bf16[16,16,768]{2,1,0:T(8,128)(2,1)S(1)} %all_to_all.28.own_ref, ...), custom_call_target="tpu_custom_call" | custom-call | tf_op jit(solution)/shard_map/pallas_call | solution.py:155
  87.5 0.0 copy-done
  87.5 6.2 %all-to-all-start.3 = ((f32[256,1,1]{2,1,0:T(1,128)}), f32[256,1,1]{2,1,0:T(1,128)S(1)}, u32[]{:S(2)}, u32[]{:S(2)}) async-start(f32[256,1,1]{2,1,0:T(1,128)} %bitcast.1), calls=%async_computation.3 | async-start | bytes 262144 | tf_op jit(solution)/shard_map/all_to_all | solution.py:200
  93.7 0.0 copy-start.1
  93.7 1.4 %copy-done.1 = bf16[2,3,256,512]{3,2,1,0:T(8,128)(2,1)S(1)} copy-done((bf16[2,3,256,512]{3,2,1,0:T(8,128)(2,1)S(1)}, bf16[2,3,256,512]{3,2,1,0:T(8,128)(2,1)}, u32[]{:S(2)}) %copy-start.1) | copy-done | bytes 1572888
  95.1 2.2 %shard_map.95 = (bf16[2,512,384]{2,1,0:T(8,128)(2,1)}, bf16[2,512,384]{2,1,0:T(8,128)(2,1)}) custom-call(bf16[16,16,1024]{2,1,0:T(8,128)(2,1)S(1)} %all_to_all.26.own_ref.own_text_ref, bf16[16,16,1024]{2,1,0:T(8,128)(2,1)S(1)} %collective-permute-done.other_ref.other_text_ref, bf16[2,3,256,512]{3,2,1,0:T(8,128)(2,1)S(1)} %get-tuple-element.14.probs_ref, ...), custom_call_target="tpu_custom_call" | custom-call | flops 402653184 | tf_op jit(solution)/shard_map/pallas_call | solution.py:155
  97.3 9.3 %all-to-all-done.3 = f32[256,1,1]{2,1,0:T(1,128)S(1)} async-done(((f32[256,1,1]{2,1,0:T(1,128)}), f32[256,1,1]{2,1,0:T(1,128)S(1)}, u32[]{:S(2)}, u32[]{:S(2)}) %all-to-all-start.3) | async-done | bytes 1056 | tf_op jit(solution)/shard_map/all_to_all | solution.py:200
  106.6 0.9 shard_map.99
Async XLA Ops:
  0.6 38.6 %copy-start.4 = (s32[2]{0:T(128)S(1)}, s32[2]{0:T(128)}, u32[]{:S(2)}) copy-start(s32[2]{0:T(128)} %lengths_ref.1) | copy-start | bytes 28
  0.6 38.6 %copy-start.2 = (bf16[2,512,384]{2,1,0:T(8,128)(2,1)S(1)}, bf16[2,512,384]{2,1,0:T(8,128)(2,1)}, u32[]{:S(2)}) copy-start(bf16[2,512,384]{2,1,0:T(8,128)(2,1)} %query_ref.1) | copy-start | bytes 2359300
  35.1 4.1 %collective-permute-start = (bf16[16,16,1024]{2,1,0:T(8,128)(2,1)S(1)}, bf16[16,16,1024]{2,1,0:T(8,128)(2,1)S(1)}, u32[]{:S(2)}, u32[]{:S(2)}) collective-permute-start(bf16[16,16,1024]{2,1,0:T(8,128)(2,1)S(1)} %all_to_all.26.own_ref.own_text_ref), channel_id=1, source_target_pairs={{0,8},{8,0},{1,9},{9,1},{2,10},{10,2},{3,11},{11,3},{4,12},{12,4},... | collective-permute-start | bytes 1572872 | tf_op jit(solution)/shard_map/ppermute | solution.py:167
  39.2 1.1 %copy-start.3 = (bf16[2,512,384]{2,1,0:T(8,128)(2,1)S(1)}, bf16[2,512,384]{2,1,0:T(8,128)(2,1)}, u32[]{:S(2)}) copy-start(bf16[2,512,384]{2,1,0:T(8,128)(2,1)} %grad_ref.1) | copy-start | bytes 2359300
  44.5 43.0 %copy-start = (bf16[2,3,256,512]{3,2,1,0:T(8,128)(2,1)}, bf16[2,3,256,512]{3,2,1,0:T(8,128)(2,1)S(1)}, u32[]{:S(2)}) copy-start(bf16[2,3,256,512]{3,2,1,0:T(8,128)(2,1)S(1)} %get-tuple-element.15.dscore_ref) | copy-start | bytes 4718596
  44.5 1.8 %collective-permute-start.1 = (bf16[16,16,768]{2,1,0:T(8,128)(2,1)S(1)}, bf16[16,16,768]{2,1,0:T(8,128)(2,1)S(1)}, u32[]{:S(2)}, u32[]{:S(2)}) collective-permute-start(bf16[16,16,768]{2,1,0:T(8,128)(2,1)S(1)} %get-tuple-element.19), channel_id=1, source_target_pairs={{0,8},{8,0},{1,9},{9,1},{2,10},{10,2},{3,11},{11,3},{4,12},{12,4},... | collective-permute-start | bytes 1179656 | tf_op jit(solution)/shard_map/ppermute | solution.py:167
  82.3 4.1 %collective-permute-start.2 = (bf16[16,16,768]{2,1,0:T(8,128)(2,1)S(1)}, bf16[16,16,768]{2,1,0:T(8,128)(2,1)S(1)}, u32[]{:S(2)}, u32[]{:S(2)}) collective-permute-start(bf16[16,16,768]{2,1,0:T(8,128)(2,1)S(1)} %all_to_all.28.own_ref), channel_id=1, source_target_pairs={{0,8},{8,0},{1,9},{9,1},{2,10},{10,2},{3,11},{11,3},{4,12},{12,4},... | collective-permute-start | bytes 1179656 | tf_op jit(solution)/shard_map/ppermute | solution.py:167
  87.5 19.1 %all-to-all-start.3 = ((f32[256,1,1]{2,1,0:T(1,128)}), f32[256,1,1]{2,1,0:T(1,128)S(1)}, u32[]{:S(2)}, u32[]{:S(2)}) async-start(f32[256,1,1]{2,1,0:T(1,128)} %bitcast.1), calls=%async_computation.3 | async-start | bytes 262144 | tf_op jit(solution)/shard_map/all_to_all | solution.py:200
  93.7 1.4 %copy-start.1 = (bf16[2,3,256,512]{3,2,1,0:T(8,128)(2,1)S(1)}, bf16[2,3,256,512]{3,2,1,0:T(8,128)(2,1)}, u32[]{:S(2)}) copy-start(bf16[2,3,256,512]{3,2,1,0:T(8,128)(2,1)} %copy-done) | copy-start | bytes 4718596

commit v4 on v3

v4 whole, which is shorter than its diff:
```python
import math

import jax
import jax.numpy as jnp
from jax import lax
from jax.experimental import pallas as pl
from jax.experimental.pallas import tpu as pltpu
from jax.sharding import Mesh
from jax.sharding import PartitionSpec as P


DT = 4096
HEADS = 24
HEAD = 128
CHUNKS = 4
ZY = ("z", "yh")
SEQ = ("z", "yh", "core")
TP = ("yl", "x")
ALL = SEQ + TP
SCALING = 1.0 / math.sqrt(HEAD)
BF16 = jnp.bfloat16
F32 = jnp.float32


def dot(a, b, ca, cb):
    return lax.dot_general(a, b, (((ca,), (cb,)), ((), ())), preferred_element_type=F32)


def project_kernel(text_ref, key_ref, value_ref, out_ref, held_ref, arrived):
    groups = out_ref.shape[0]
    features = key_ref.shape[1]
    step = DT // CHUNKS
    copies = []
    for at in range(CHUNKS):
        rows = pl.ds(at * step, step)
        for which, ref in enumerate((key_ref, value_ref)):
            copy = pltpu.make_async_copy(ref.at[rows], held_ref.at[which, rows], arrived.at[which, at])
            copy.start()
            copies.append(copy)
    text = text_ref[...].reshape(-1, DT)
    wide = DT // groups
    for g in range(groups):
        out_ref[g, :, 2 * features :] = text[:, g * wide : (g + 1) * wide]
    sums = [None, None]
    for at in range(CHUNKS):
        rows = slice(at * step, (at + 1) * step)
        for which in range(2):
            copies[2 * at + which].wait()
            part = dot(text[:, rows], held_ref[which, rows], 1, 0)
            sums[which] = part if sums[which] is None else sums[which] + part
    for which in range(2):
        total = sums[which].astype(BF16)
        for g in range(groups):
            out_ref[g, :, which * features : (which + 1) * features] = total


def text_of(own_ref, other_ref, first_core, b, first):
    half = own_ref.shape[0] * 8
    own, other = [ref[:, b * 8 : (b + 1) * 8, first : first + HEAD].reshape(half, HEAD) for ref in (own_ref, other_ref)]
    return jnp.concatenate([jnp.where(first_core, own, other), jnp.where(first_core, other, own)], axis=0)


def score_kernel(lengths_ref, core_ref, query_ref, grad_ref, own_ref, other_ref, own_sum_ref, other_sum_ref, probs_ref, dscore_ref, columns_ref):
    samples, _, features = query_ref.shape
    groups = own_ref.shape[0]
    heads = features // HEAD
    first_core = core_ref[0] == 0
    half = groups * 8
    place = lax.broadcasted_iota(jnp.int32, (2 * half, 1), 0)
    within = place % half
    token = (within // 8) * 16 + (place // half) * 8 + within % 8
    columns_ref[0] = own_ref[:, :, 2 * features :]
    columns_ref[1] = other_ref[:, :, 2 * features :]

    for b in range(samples):
        allowed = token < lengths_ref[b]
        for h in range(heads):
            cols = slice(h * HEAD, (h + 1) * HEAD)
            key = text_of(own_ref, other_ref, first_core, b, h * HEAD)
            value = text_of(own_ref, other_ref, first_core, b, features + h * HEAD)
            query = query_ref[b, :, cols]
            grad = grad_ref[b, :, cols]
            scores = dot(key, query, 1, 1) * SCALING
            scores = jnp.where(allowed, scores, -1e30)
            weights = jnp.exp(scores - jnp.max(scores, axis=0, keepdims=True))
            probs = weights * (1.0 / jnp.sum(weights, axis=0, keepdims=True))
            probs_low = probs.astype(BF16)
            dprob = dot(value, grad, 1, 1)
            delta = jnp.sum(probs * dprob, axis=0, keepdims=True)
            dscore = (probs * (dprob - delta) * SCALING).astype(BF16)
            key_sum = dot(dscore, query, 1, 0)
            value_sum = dot(probs_low, grad, 1, 0)
            own_sum = jnp.where(first_core, key_sum, value_sum)
            other_sum = jnp.where(first_core, value_sum, key_sum).astype(BF16)
            for side in range(2):
                at = slice(side * 16 + b * 8, side * 16 + (b + 1) * 8)
                from_side = slice(side * half, (side + 1) * half)
                own_sum_ref[:, at, cols] = own_sum[from_side].reshape(groups, 8, HEAD)
                other_sum_ref[:, at, cols] = other_sum[from_side].reshape(groups, 8, HEAD)
            probs_ref[b, h] = probs_low
            dscore_ref[b, h] = dscore


def attend_kernel(core_ref, own_ref, other_ref, probs_ref, dscore_ref, attended_ref, query_grad_ref):
    samples, heads = probs_ref.shape[:2]
    first_core = core_ref[0] == 0
    features = heads * HEAD
    for b in range(samples):
        for h in range(heads):
            cols = slice(h * HEAD, (h + 1) * HEAD)
            value = text_of(own_ref, other_ref, first_core, b, features + h * HEAD)
            attended_ref[b, :, cols] = dot(probs_ref[b, h], value, 0, 0).astype(BF16)
            key = text_of(own_ref, other_ref, first_core, b, h * HEAD)
            query_grad_ref[b, :, cols] = dot(dscore_ref[b, h], key, 0, 0).astype(BF16)


def pair_sum_kernel(own_ref, other_ref, out_ref):
    out_ref[...] = (own_ref[...] + other_ref[...].astype(F32)).astype(BF16)


def total_kernel(parts_ref, out_ref):
    total = parts_ref[0].astype(F32)
    for g in range(1, parts_ref.shape[0]):
        total = total + parts_ref[g].astype(F32)
    total = total.astype(BF16)
    for g in range(out_ref.shape[0]):
        out_ref[g] = total


def weight_kernel(core_ref, columns_ref, total_ref, own_raw_ref, other_raw_ref, square_ref):
    groups, rows, features = total_ref.shape
    half = rows // 2
    core = core_ref[0]
    squares = None
    for raw_ref, feature_core in ((own_raw_ref, core), (other_raw_ref, 1 - core)):
        first = pl.multiple_of(feature_core * HEAD, HEAD)
        raw = None
        for which, side in ((0, core), (1, 1 - core)):
            text = columns_ref[which, :, :, pl.ds(first, HEAD)].reshape(groups * half, HEAD)
            total = total_ref[:, pl.ds(pl.multiple_of(side * half, half), half), :].reshape(groups * half, features)
            part = dot(text, total, 0, 0)
            raw = part if raw is None else raw + part
        raw_ref[...] = raw
        part = jnp.sum((raw * raw).reshape(-1, 8, features), axis=0)
        squares = part if squares is None else squares + part
    lanes = squares[:, :HEAD]
    for at in range(HEAD, features, HEAD):
        lanes = lanes + squares[:, at : at + HEAD]
    square_ref[...] = jnp.broadcast_to(jnp.sum(lanes, keepdims=True), square_ref.shape)


def scale_kernel(core_ref, own_ref, other_ref, squares_ref, key_ref, value_ref):
    overall = jnp.sum(squares_ref[...], keepdims=True)
    spread = jnp.sqrt(overall / (2.0 * DT * HEADS * HEAD) + 1e-06)
    factor = 1.0 / jnp.maximum(spread, 1.0)
    first_core = core_ref[0] == 0
    own = own_ref[...]
    other = other_ref[...]
    key_ref[...] = jnp.where(first_core, own, other) * factor
    value_ref[...] = jnp.where(first_core, other, own) * factor


def call(kernel, out, *args, scalars=0, far=0, scratch=(), mib=12):
    near = pl.BlockSpec(memory_space=pltpu.VMEM)
    specs = [pl.BlockSpec(memory_space=pltpu.SMEM)] * scalars + [near] * (len(args) - scalars - far)
    specs += [pl.BlockSpec(memory_space=pl.ANY)] * far
    return pl.pallas_call(
        kernel, out_shape=out, in_specs=specs, out_specs=near if isinstance(out, jax.ShapeDtypeStruct) else [near] * len(out),
        scratch_shapes=scratch, compiler_params=pltpu.CompilerParams(vmem_limit_bytes=mib << 20),
    )(*args)


def shape(dims, dtype):
    return jax.ShapeDtypeStruct(dims, dtype)


def swap(array):
    return lax.ppermute(array, "core", [(0, 1), (1, 0)])


def exchange(array, axes):
    return lax.all_to_all(array, axes, 0, 0, tiled=True)


def per_device(video_query, text_states, key_weight, value_weight, text_lengths, output_grad):
    samples, video_rows, features = video_query.shape
    text_rows = samples * text_states.shape[1]
    groups = lax.axis_size(ZY)
    wide = 2 * features
    core = lax.axis_index("core").astype(jnp.int32).reshape(1)
    packed = call(
        project_kernel, shape((groups, text_rows, wide + DT // groups), BF16), text_states, key_weight, value_weight, far=2, mib=61,
        scratch=[pltpu.VMEM((2, DT, features), BF16), pltpu.SemaphoreType.DMA((2, CHUNKS))],
    )
    own = exchange(packed, ZY)
    other = swap(own)
    like = shape(video_query.shape, BF16)
    block = (groups, 2 * text_rows, features)
    tall = shape((samples, features // HEAD, 2 * groups * 8, video_rows), BF16)
    own_sum, other_sum, probs, dscore, columns = call(
        score_kernel, [shape(block, F32), shape(block, BF16), tall, tall, shape((2, groups, text_rows, DT // groups), BF16)],
        text_lengths, core, video_query, output_grad, own, other, scalars=2,
    )
    attended, query_grad = call(attend_kernel, [like, like], core, own, other, probs, dscore, scalars=1)
    pair = call(pair_sum_kernel, shape(block, BF16), own_sum, swap(other_sum))
    parts = exchange(pair, ZY)
    totals = exchange(call(total_kernel, shape(block, BF16), parts), ZY)
    every = lax.axis_size(ALL)
    weight = shape((HEAD, features), F32)
    own_raw, other_raw, squares = call(
        weight_kernel, [weight, weight, shape((every, 1), F32)], core, columns, totals, scalars=1,
    )
    squares = exchange(squares, ALL)
    key_weight_grad, value_weight_grad = call(
        scale_kernel, [weight, weight], core, own_raw, swap(other_raw), squares, scalars=1,
    )
    return attended, query_grad, key_weight_grad, value_weight_grad


def solution(mesh):
    split = Mesh(mesh.devices.reshape(8, 2, 2, 2, 4), ALL)
    return jax.shard_map(
        per_device,
        mesh=split,
        in_specs=(P(None, SEQ, TP), P(None, SEQ, None), P(None, TP), P(None, TP), P(), P(None, SEQ, TP)),
        out_specs=(P(None, SEQ, TP), P(None, SEQ, TP), P(SEQ, TP), P(SEQ, TP)),
        check_vma=False,
    )
```

time: 108 us -> 107 us (level)
  waiting for transfers between devices: 13.5 us -> 12.1 us
  local copies, waits for them, and re-layouts: 2.55 us -> 3.7 us
    ppermute x3, waiting for transfers between devices: 4.24 us -> 2.89 us  [swap(): return lax.ppermute(array, 'core', [(0, 1), (1, 0)])]
    unnamed x10, local copies, waits for them, and re-layouts: 2.55 us -> 3.7 us
  transfers between devices with their start and end apart: 4 -> 4, of which waited for: 4 -> 3; matrix products, arithmetic and copies ran while one was open for 0% -> 0% of each run, Pallas kernels for 2% -> 2%
where the time goes in v4:
time: 107 us; the launch traced here: 106 us
  blocking collectives  64.8 us (61%)
  Pallas kernels  13.5 us (13%)
  waiting for transfers between devices  12.1 us (11%)
  starting transfers between devices  11.7 us (11%)
  local copies, waits for them, and re-layouts  3.7 us (3%)
    all_to_all x3, blocking collectives, exchange(): return lax.all_to_all(array, axes, 0, 0, tiled=True)  64.8 us
    pallas_call x7, Pallas kernels, call(): pl.pallas_call(kernel, out_shape=out, in_specs=specs, out_specs=near if i...  13.5 us
    all_to_all x1, waiting for transfers between devices, exchange(): return lax.all_to_all(array, axes, 0, 0, tiled=True)  9.24 us
    all_to_all x1, starting transfers between devices, exchange(): return lax.all_to_all(array, axes, 0, 0, tiled=True)  5.98 us
    ppermute x3, starting transfers between devices, swap(): return lax.ppermute(array, 'core', [(0, 1), (1, 0)])  5.71 us
    unnamed x10, local copies, waits for them, and re-layouts  3.7 us
    ppermute x3, waiting for transfers between devices, swap(): return lax.ppermute(array, 'core', [(0, 1), (1, 0)])  2.89 us
  transfers between devices with their start and end apart: 4, of which 3 were waited for; matrix products, arithmetic and copies ran while one was open for 0% of the time, Pallas kernels for 2%

profile of v4, /device:TPU:1, one launch (start us, length us, event | category | flops | bytes accessed | tf_op | source)
XLA Modules:
  0.0 106.5 jit_solution(10112593787388940485)
XLA Ops:
  0.6 0.0 copy-start.4
  0.6 0.0 copy-start.2
  0.7 4.9 %shard_map.93 = bf16[16,16,1024]{2,1,0:T(8,128)(2,1)} custom-call(bf16[2,8,4096]{2,1,0:T(8,128)(2,1)} %text_ref.1, bf16[4096,384]{1,0:T(8,128)(2,1)} %key_ref.1, bf16[4096,384]{1,0:T(8,128)(2,1)} %value_ref.1), custom_call_target="tpu_custom_call" | custom-call | tf_op jit(solution)/shard_map/pallas_call | solution.py:167
  5.6 29.0 %all_to_all.26.own_ref = bf16[16,16,1024]{2,1,0:T(8,128)(2,1)S(1)} all-to-all(bf16[16,16,1024]{2,1,0:T(8,128)(2,1)} %shard_map.93), channel_id=1, replica_groups=mesh['z'=8,'yh'=2,'core'=2,'yl'=2,'x'=4] {'z','yh'}, dimensions={0} | all-to-all | bytes 1048576 | tf_op jit(solution)/shard_map/all_to_all | solution.py:182
  34.5 2.6 %collective-permute-start = (bf16[16,16,1024]{2,1,0:T(8,128)(2,1)S(1)}, bf16[16,16,1024]{2,1,0:T(8,128)(2,1)S(1)}, u32[]{:S(2)}, u32[]{:S(2)}) collective-permute-start(bf16[16,16,1024]{2,1,0:T(8,128)(2,1)S(1)} %all_to_all.26.own_ref), channel_id=1, source_target_pairs={{0,8},{8,0},{1,9},{9,1},{2,10},{10,2},{3,11},{11,3},{4,12},{12,4},... | collective-permute-start | bytes 1572872 | tf_op jit(solution)/shard_map/ppermute | solution.py:178
  37.1 1.5 %collective-permute-done.other_ref = bf16[16,16,1024]{2,1,0:T(8,128)(2,1)S(1)} collective-permute-done((bf16[16,16,1024]{2,1,0:T(8,128)(2,1)S(1)}, bf16[16,16,1024]{2,1,0:T(8,128)(2,1)S(1)}, u32[]{:S(2)}, u32[]{:S(2)}) %collective-permute-start) | collective-permute-done | bytes 524320 | tf_op jit(solution)/shard_map/ppermute | solution.py:178
  38.6 0.0 copy-done.4
  38.6 0.0 copy-done.2
  38.6 0.0 copy-start.3
  38.6 1.1 %copy-done.3 = bf16[2,512,384]{2,1,0:T(8,128)(2,1)S(1)} copy-done((bf16[2,512,384]{2,1,0:T(8,128)(2,1)S(1)}, bf16[2,512,384]{2,1,0:T(8,128)(2,1)}, u32[]{:S(2)}) %copy-start.3) | copy-done | bytes 786456
  39.8 4.2 %shard_map.94 = (f32[16,32,384]{2,1,0:T(8,128)S(1)}, bf16[16,32,384]{2,1,0:T(8,128)(2,1)S(1)}, bf16[2,3,256,512]{3,2,1,0:T(8,128)(2,1)S(1)}, bf16[2,3,256,512]{3...) custom-call(s32[2]{0:T(128)S(1)} %copy-done.4, s32[1]{0:T(128)} %bitcast.core_ref, bf16[2,512,384]{2,1,0:T(8,128)(2,1)S(1)} %copy-done.2, ...), custom_call_target="tpu_custom_call" | custom-call | tf_op jit(solution)/shard_map/pallas_call | solution.py:167
  44.0 0.0 copy-start
  44.0 1.2 %copy-done = bf16[2,3,256,512]{3,2,1,0:T(8,128)(2,1)} copy-done((bf16[2,3,256,512]{3,2,1,0:T(8,128)(2,1)}, bf16[2,3,256,512]{3,2,1,0:T(8,128)(2,1)S(1)}, u32[]{:S(2)}) %copy-start) | copy-done | bytes 1572888
  45.1 0.4 collective-permute-start.1
  45.5 1.4 %collective-permute-done.1.other_ref = bf16[16,32,384]{2,1,0:T(8,128)(2,1)S(1)} collective-permute-done((bf16[16,32,384]{2,1,0:T(8,128)(2,1)S(1)}, bf16[16,32,384]{2,1,0:T(8,128)(2,1)S(1)}, u32[]{:S(2)}, u32[]{:S(2)}) %collective-permute-start.1) | collective-permute-done | bytes 393248 | tf_op jit(solution)/shard_map/ppermute | solution.py:178
  46.8 0.1 shard_map.96
  46.9 17.6 %all_to_all.27.parts_ref = bf16[16,32,384]{2,1,0:T(8,128)(2,1)S(1)} all-to-all(bf16[16,32,384]{2,1,0:T(8,128)(2,1)S(1)} %shard_map.96), channel_id=1, replica_groups=mesh['z'=8,'yh'=2,'core'=2,'yl'=2,'x'=4] {'z','yh'}, dimensions={0} | all-to-all | bytes 786432 | tf_op jit(solution)/shard_map/all_to_all | solution.py:182
  64.6 0.1 shard_map.97
  64.6 18.2 %all_to_all.28.total_ref = bf16[16,32,384]{2,1,0:T(8,128)(2,1)S(1)} all-to-all(bf16[16,32,384]{2,1,0:T(8,128)(2,1)S(1)} %shard_map.97), channel_id=1, replica_groups=mesh['z'=8,'yh'=2,'core'=2,'yl'=2,'x'=4] {'z','yh'}, dimensions={0} | all-to-all | bytes 786432 | tf_op jit(solution)/shard_map/all_to_all | solution.py:182
  82.8 1.1 %shard_map.98 = (f32[128,384]{1,0:T(8,128)S(1)}, f32[128,384]{1,0:T(8,128)S(1)}, f32[256,1]{1,0:T(8,128)}) custom-call(s32[1]{0:T(128)} %bitcast.core_ref, bf16[2,16,16,256]{3,2,1,0:T(8,128)(2,1)S(1)} %get-tuple-element.20.columns_ref, bf16[16,32,384]{2,1,0:T(8,128)(2,1)S(1)} %all_to_all.28.total_ref), custom_call_target="tpu_custom_call" | custom-call | tf_op jit(solution)/shard_map/pallas_call | solution.py:167
  83.9 2.8 %collective-permute-start.2 = (f32[128,384]{1,0:T(8,128)S(1)}, f32[128,384]{1,0:T(8,128)S(1)}, u32[]{:S(2)}, u32[]{:S(2)}) collective-permute-start(f32[128,384]{1,0:T(8,128)S(1)} %get-tuple-element.24), channel_id=1, source_target_pairs={{0,8},{8,0},{1,9},{9,1},{2,10},{10,2},{3,11},{11,3},{4,12},{12,4},... | collective-permute-start | bytes 589832 | tf_op jit(solution)/shard_map/ppermute | solution.py:178
  86.7 6.0 %all-to-all-start.3 = ((f32[256,1,1]{2,1,0:T(1,128)}), f32[256,1,1]{2,1,0:T(1,128)S(1)}, u32[]{:S(2)}, u32[]{:S(2)}) async-start(f32[256,1,1]{2,1,0:T(1,128)} %bitcast.1), calls=%async_computation.3 | async-start | bytes 262144 | tf_op jit(solution)/shard_map/all_to_all | solution.py:182
  92.7 0.0 copy-start.1
  92.7 1.4 %copy-done.1 = bf16[2,3,256,512]{3,2,1,0:T(8,128)(2,1)S(1)} copy-done((bf16[2,3,256,512]{3,2,1,0:T(8,128)(2,1)S(1)}, bf16[2,3,256,512]{3,2,1,0:T(8,128)(2,1)}, u32[]{:S(2)}) %copy-start.1) | copy-done | bytes 1572888
  94.1 2.2 %shard_map.95 = (bf16[2,512,384]{2,1,0:T(8,128)(2,1)}, bf16[2,512,384]{2,1,0:T(8,128)(2,1)}) custom-call(s32[1]{0:T(128)} %bitcast.core_ref, bf16[16,16,1024]{2,1,0:T(8,128)(2,1)S(1)} %all_to_all.26.own_ref, bf16[16,16,1024]{2,1,0:T(8,128)(2,1)S(1)} %collective-permute-done.other_ref, bf16[2,3,256,512]{3,2,1,0:T(8,128)(2,1)S(1)} %get-tuple-element.16.probs_ref, ...), custom_call_target="tpu_custom_call" | custom-call | tf_op jit(solution)/shard_map/pallas_call | solution.py:167
  96.3 9.2 %all-to-all-done.3 = f32[256,1,1]{2,1,0:T(1,128)S(1)} async-done(((f32[256,1,1]{2,1,0:T(1,128)}), f32[256,1,1]{2,1,0:T(1,128)S(1)}, u32[]{:S(2)}, u32[]{:S(2)}) %all-to-all-start.3) | async-done | bytes 1056 | tf_op jit(solution)/shard_map/all_to_all | solution.py:182
  105.5 0.0 collective-permute-done.2.other_ref
  105.6 0.9 shard_map.99
Async XLA Ops:
  0.6 38.0 %copy-start.4 = (s32[2]{0:T(128)S(1)}, s32[2]{0:T(128)}, u32[]{:S(2)}) copy-start(s32[2]{0:T(128)} %lengths_ref.1) | copy-start | bytes 28
  0.6 38.0 %copy-start.2 = (bf16[2,512,384]{2,1,0:T(8,128)(2,1)S(1)}, bf16[2,512,384]{2,1,0:T(8,128)(2,1)}, u32[]{:S(2)}) copy-start(bf16[2,512,384]{2,1,0:T(8,128)(2,1)} %query_ref.1) | copy-start | bytes 2359300
  34.5 4.1 %collective-permute-start = (bf16[16,16,1024]{2,1,0:T(8,128)(2,1)S(1)}, bf16[16,16,1024]{2,1,0:T(8,128)(2,1)S(1)}, u32[]{:S(2)}, u32[]{:S(2)}) collective-permute-start(bf16[16,16,1024]{2,1,0:T(8,128)(2,1)S(1)} %all_to_all.26.own_ref), channel_id=1, source_target_pairs={{0,8},{8,0},{1,9},{9,1},{2,10},{10,2},{3,11},{11,3},{4,12},{12,4},... | collective-permute-start | bytes 1572872 | tf_op jit(solution)/shard_map/ppermute | solution.py:178
  38.6 1.1 %copy-start.3 = (bf16[2,512,384]{2,1,0:T(8,128)(2,1)S(1)}, bf16[2,512,384]{2,1,0:T(8,128)(2,1)}, u32[]{:S(2)}) copy-start(bf16[2,512,384]{2,1,0:T(8,128)(2,1)} %grad_ref.1) | copy-start | bytes 2359300
  44.0 1.2 %copy-start = (bf16[2,3,256,512]{3,2,1,0:T(8,128)(2,1)}, bf16[2,3,256,512]{3,2,1,0:T(8,128)(2,1)S(1)}, u32[]{:S(2)}) copy-start(bf16[2,3,256,512]{3,2,1,0:T(8,128)(2,1)S(1)} %get-tuple-element.17.dscore_ref) | copy-start | bytes 4718596
  45.1 1.7 %collective-permute-start.1 = (bf16[16,32,384]{2,1,0:T(8,128)(2,1)S(1)}, bf16[16,32,384]{2,1,0:T(8,128)(2,1)S(1)}, u32[]{:S(2)}, u32[]{:S(2)}) collective-permute-start(bf16[16,32,384]{2,1,0:T(8,128)(2,1)S(1)} %get-tuple-element.22), channel_id=1, source_target_pairs={{0,8},{8,0},{1,9},{9,1},{2,10},{10,2},{3,11},{11,3},{4,12},{12,4},... | collective-permute-start | bytes 1179656 | tf_op jit(solution)/shard_map/ppermute | solution.py:178
  83.9 21.6 %collective-permute-start.2 = (f32[128,384]{1,0:T(8,128)S(1)}, f32[128,384]{1,0:T(8,128)S(1)}, u32[]{:S(2)}, u32[]{:S(2)}) collective-permute-start(f32[128,384]{1,0:T(8,128)S(1)} %get-tuple-element.24), channel_id=1, source_target_pairs={{0,8},{8,0},{1,9},{9,1},{2,10},{10,2},{3,11},{11,3},{4,12},{12,4},... | collective-permute-start | bytes 589832 | tf_op jit(solution)/shard_map/ppermute | solution.py:178
  86.7 18.8 %all-to-all-start.3 = ((f32[256,1,1]{2,1,0:T(1,128)}), f32[256,1,1]{2,1,0:T(1,128)S(1)}, u32[]{:S(2)}, u32[]{:S(2)}) async-start(f32[256,1,1]{2,1,0:T(1,128)} %bitcast.1), calls=%async_computation.3 | async-start | bytes 262144 | tf_op jit(solution)/shard_map/all_to_all | solution.py:182
  92.7 1.4 %copy-start.1 = (bf16[2,3,256,512]{3,2,1,0:T(8,128)(2,1)S(1)}, bf16[2,3,256,512]{3,2,1,0:T(8,128)(2,1)}, u32[]{:S(2)}) copy-start(bf16[2,3,256,512]{3,2,1,0:T(8,128)(2,1)} %copy-done) | copy-start | bytes 4718596

commit v5 on v4

--- a/solution.py
+++ b/solution.py
@@ -26,10 +26,12 @@
     return lax.dot_general(a, b, (((ca,), (cb,)), ((), ())), preferred_element_type=F32)
 
 
-def project_kernel(text_ref, key_ref, value_ref, out_ref, held_ref, arrived):
+def project_kernel(text_ref, key_ref, value_ref, out_ref, states_ref, held_ref, arrived, here):
     groups = out_ref.shape[0]
     features = key_ref.shape[1]
     step = DT // CHUNKS
+    states = pltpu.make_async_copy(text_ref, states_ref, here)
+    states.start()
     copies = []
     for at in range(CHUNKS):
         rows = pl.ds(at * step, step)
@@ -37,7 +39,8 @@
             copy = pltpu.make_async_copy(ref.at[rows], held_ref.at[which, rows], arrived.at[which, at])
             copy.start()
             copies.append(copy)
-    text = text_ref[...].reshape(-1, DT)
+    states.wait()
+    text = states_ref[...].reshape(-1, DT)
     wide = DT // groups
     for g in range(groups):
         out_ref[g, :, 2 * features :] = text[:, g * wide : (g + 1) * wide]
@@ -72,46 +75,66 @@
     columns_ref[0] = own_ref[:, :, 2 * features :]
     columns_ref[1] = other_ref[:, :, 2 * features :]
 
-    for b in range(samples):
-        allowed = token < lengths_ref[b]
-        for h in range(heads):
-            cols = slice(h * HEAD, (h + 1) * HEAD)
-            key = text_of(own_ref, other_ref, first_core, b, h * HEAD)
-            value = text_of(own_ref, other_ref, first_core, b, features + h * HEAD)
-            query = query_ref[b, :, cols]
-            grad = grad_ref[b, :, cols]
-            scores = dot(key, query, 1, 1) * SCALING
-            scores = jnp.where(allowed, scores, -1e30)
-            weights = jnp.exp(scores - jnp.max(scores, axis=0, keepdims=True))
-            probs = weights * (1.0 / jnp.sum(weights, axis=0, keepdims=True))
-            probs_low = probs.astype(BF16)
-            dprob = dot(value, grad, 1, 1)
-            delta = jnp.sum(probs * dprob, axis=0, keepdims=True)
-            dscore = (probs * (dprob - delta) * SCALING).astype(BF16)
-            key_sum = dot(dscore, query, 1, 0)
-            value_sum = dot(probs_low, grad, 1, 0)
-            own_sum = jnp.where(first_core, key_sum, value_sum)
-            other_sum = jnp.where(first_core, value_sum, key_sum).astype(BF16)
-            for side in range(2):
-                at = slice(side * 16 + b * 8, side * 16 + (b + 1) * 8)
-                from_side = slice(side * half, (side + 1) * half)
-                own_sum_ref[:, at, cols] = own_sum[from_side].reshape(groups, 8, HEAD)
-                other_sum_ref[:, at, cols] = other_sum[from_side].reshape(groups, 8, HEAD)
-            probs_ref[b, h] = probs_low
-            dscore_ref[b, h] = dscore
-
-
-def attend_kernel(core_ref, own_ref, other_ref, probs_ref, dscore_ref, attended_ref, query_grad_ref):
+    def products(b, h):
+        cols = slice(h * HEAD, (h + 1) * HEAD)
+        key = text_of(own_ref, other_ref, first_core, b, h * HEAD)
+        value = text_of(own_ref, other_ref, first_core, b, features + h * HEAD)
+        return dot(key, query_ref[b, :, cols], 1, 1), dot(value, grad_ref[b, :, cols], 1, 1)
+
+    def weigh(b, h, scores, dprob):
+        scores = jnp.where(token < lengths_ref[b], scores * SCALING, -1e30)
+        weights = jnp.exp(scores - jnp.max(scores, axis=0, keepdims=True))
+        probs = weights * (1.0 / jnp.sum(weights, axis=0, keepdims=True))
+        probs_low = probs.astype(BF16)
+        delta = jnp.sum(probs * dprob, axis=0, keepdims=True)
+        dscore = (probs * (dprob - delta) * SCALING).astype(BF16)
+        probs_ref[b, h] = probs_low
+        dscore_ref[b, h] = dscore
+        return b, h, probs_low, dscore
+
+    def add_up(b, h, probs_low, dscore):
+        cols = slice(h * HEAD, (h + 1) * HEAD)
+        key_sum = dot(dscore, query_ref[b, :, cols], 1, 0)
+        value_sum = dot(probs_low, grad_ref[b, :, cols], 1, 0)
+        own_sum = jnp.where(first_core, key_sum, value_sum)
+        other_sum = jnp.where(first_core, value_sum, key_sum).astype(BF16)
+        for side in range(2):
+            at = slice(side * 16 + b * 8, side * 16 + (b + 1) * 8)
+            from_side = slice(side * half, (side + 1) * half)
+            own_sum_ref[:, at, cols] = own_sum[from_side].reshape(groups, 8, HEAD)
+            other_sum_ref[:, at, cols] = other_sum[from_side].reshape(groups, 8, HEAD)
+
+    jobs = [(b, h) for b in range(samples) for h in range(heads)]
+    ahead = products(*jobs[0])
+    behind = None
+    for at, job in enumerate(jobs):
+        now = ahead
+        if at + 1 < len(jobs):
+            ahead = products(*jobs[at + 1])
+        if behind is not None:
+            add_up(*behind)
+        behind = weigh(*job, *now)
+    add_up(*behind)
+
+
+def attend_kernel(core_ref, own_ref, other_ref, probs_ref, dscore_ref, attended_ref, query_grad_ref, held_ref, sent):
     samples, heads = probs_ref.shape[:2]
     first_core = core_ref[0] == 0
     features = heads * HEAD
+    copies = []
     for b in range(samples):
         for h in range(heads):
             cols = slice(h * HEAD, (h + 1) * HEAD)
             value = text_of(own_ref, other_ref, first_core, b, features + h * HEAD)
-            attended_ref[b, :, cols] = dot(probs_ref[b, h], value, 0, 0).astype(BF16)
+            held_ref[0, b, :, cols] = dot(probs_ref[b, h], value, 0, 0).astype(BF16)
             key = text_of(own_ref, other_ref, first_core, b, h * HEAD)
-            query_grad_ref[b, :, cols] = dot(dscore_ref[b, h], key, 0, 0).astype(BF16)
+            held_ref[1, b, :, cols] = dot(dscore_ref[b, h], key, 0, 0).astype(BF16)
+        for which, ref in enumerate((attended_ref, query_grad_ref)):
+            copy = pltpu.make_async_copy(held_ref.at[which, b], ref.at[b], sent.at[which, b])
+            copy.start()
+            copies.append(copy)
+    for copy in copies:
+        copy.wait()
 
 
 def pair_sum_kernel(own_ref, other_ref, out_ref):
@@ -160,13 +183,13 @@
     value_ref[...] = jnp.where(first_core, other, own) * factor
 
 
-def call(kernel, out, *args, scalars=0, far=0, scratch=(), mib=12):
-    near = pl.BlockSpec(memory_space=pltpu.VMEM)
-    specs = [pl.BlockSpec(memory_space=pltpu.SMEM)] * scalars + [near] * (len(args) - scalars - far)
-    specs += [pl.BlockSpec(memory_space=pl.ANY)] * far
+def call(kernel, out, *args, scalars=0, far=0, far_out=False, scratch=(), mib=12):
+    near, away = [pl.BlockSpec(memory_space=space) for space in (pltpu.VMEM, pl.ANY)]
+    specs = [pl.BlockSpec(memory_space=pltpu.SMEM)] * scalars + [near] * (len(args) - scalars - far) + [away] * far
+    out_spec = away if far_out else near
     return pl.pallas_call(
-        kernel, out_shape=out, in_specs=specs, out_specs=near if isinstance(out, jax.ShapeDtypeStruct) else [near] * len(out),
-        scratch_shapes=scratch, compiler_params=pltpu.CompilerParams(vmem_limit_bytes=mib << 20),
+        kernel, out_shape=out, in_specs=specs, out_specs=out_spec if isinstance(out, jax.ShapeDtypeStruct) else [out_spec] * len(out),
+        scratch_shapes=scratch, compiler_params=pltpu.CompilerParams(vmem_limit_bytes=int(mib * 1048576)),
     )(*args)
 
 
@@ -189,8 +212,11 @@
     wide = 2 * features
     core = lax.axis_index("core").astype(jnp.int32).reshape(1)
     packed = call(
-        project_kernel, shape((groups, text_rows, wide + DT // groups), BF16), text_states, key_weight, value_weight, far=2, mib=61,
-        scratch=[pltpu.VMEM((2, DT, features), BF16), pltpu.SemaphoreType.DMA((2, CHUNKS))],
+        project_kernel, shape((groups, text_rows, wide + DT // groups), BF16), text_states, key_weight, value_weight, far=3, mib=61,
+        scratch=[
+            pltpu.VMEM(text_states.shape, BF16), pltpu.VMEM((2, DT, features), BF16),
+            pltpu.SemaphoreType.DMA((2, CHUNKS)), pltpu.SemaphoreType.DMA,
+        ],
     )
     own = exchange(packed, ZY)
     other = swap(own)
@@ -201,7 +227,10 @@
         score_kernel, [shape(block, F32), shape(block, BF16), tall, tall, shape((2, groups, text_rows, DT // groups), BF16)],
         text_lengths, core, video_query, output_grad, own, other, scalars=2,
     )
-    attended, query_grad = call(attend_kernel, [like, like], core, own, other, probs, dscore, scalars=1)
+    attended, query_grad = call(
+        attend_kernel, [like, like], core, own, other, probs, dscore, scalars=1, far_out=True,
+        scratch=[pltpu.VMEM((2,) + video_query.shape, BF16), pltpu.SemaphoreType.DMA((2, samples))],
+    )
     pair = call(pair_sum_kernel, shape(block, BF16), own_sum, swap(other_sum))
     parts = exchange(pair, ZY)
     totals = exchange(call(total_kernel, shape(block, BF16), parts), ZY)

time: 107 us -> 107 us (level)
  no operation moved by 1% of the time
where the time goes in v5:
time: 107 us; the launch traced here: 106 us
  blocking collectives  64.8 us (61%)
  Pallas kernels  13.2 us (12%)
  waiting for transfers between devices  12.4 us (12%)
  starting transfers between devices  11.7 us (11%)
  local copies, waits for them, and re-layouts  3.7 us (3%)
    all_to_all x3, blocking collectives, exchange(): return lax.all_to_all(array, axes, 0, 0, tiled=True)  64.8 us
    pallas_call x7, Pallas kernels, call(): pl.pallas_call(kernel, out_shape=out, in_specs=specs, out_specs=out_spec...  13.2 us
    all_to_all x1, waiting for transfers between devices, exchange(): return lax.all_to_all(array, axes, 0, 0, tiled=True)  9.46 us
    all_to_all x1, starting transfers between devices, exchange(): return lax.all_to_all(array, axes, 0, 0, tiled=True)  5.97 us
    ppermute x3, starting transfers between devices, swap(): return lax.ppermute(array, 'core', [(0, 1), (1, 0)])  5.71 us
    unnamed x10, local copies, waits for them, and re-layouts  3.7 us
    ppermute x3, waiting for transfers between devices, swap(): return lax.ppermute(array, 'core', [(0, 1), (1, 0)])  2.89 us
  transfers between devices with their start and end apart: 4, of which 3 were waited for; matrix products, arithmetic and copies ran while one was open for 0% of the time, Pallas kernels for 2%

profile of v5, /device:TPU:1, one launch (start us, length us, event | category | flops | bytes accessed | tf_op | source)
XLA Modules:
  0.0 106.4 jit_solution(10682077446349890222)
XLA Ops:
  0.6 0.0 copy-start.4
  0.6 0.0 copy-start.2
  0.7 5.1 %shard_map.93 = bf16[16,16,1024]{2,1,0:T(8,128)(2,1)} custom-call(bf16[2,8,4096]{2,1,0:T(8,128)(2,1)} %text_ref.1, bf16[4096,384]{1,0:T(8,128)(2,1)} %key_ref.1, bf16[4096,384]{1,0:T(8,128)(2,1)} %value_ref.1), custom_call_target="tpu_custom_call" | custom-call | tf_op jit(solution)/shard_map/pallas_call | solution.py:190
  5.8 29.0 %all_to_all.26.own_ref = bf16[16,16,1024]{2,1,0:T(8,128)(2,1)S(1)} all-to-all(bf16[16,16,1024]{2,1,0:T(8,128)(2,1)} %shard_map.93), channel_id=1, replica_groups=mesh['z'=8,'yh'=2,'core'=2,'yl'=2,'x'=4] {'z','yh'}, dimensions={0} | all-to-all | bytes 1048576 | tf_op jit(solution)/shard_map/all_to_all | solution.py:205
  34.7 2.6 %collective-permute-start = (bf16[16,16,1024]{2,1,0:T(8,128)(2,1)S(1)}, bf16[16,16,1024]{2,1,0:T(8,128)(2,1)S(1)}, u32[]{:S(2)}, u32[]{:S(2)}) collective-permute-start(bf16[16,16,1024]{2,1,0:T(8,128)(2,1)S(1)} %all_to_all.26.own_ref), channel_id=1, source_target_pairs={{0,8},{8,0},{1,9},{9,1},{2,10},{10,2},{3,11},{11,3},{4,12},{12,4},... | collective-permute-start | bytes 1572872 | tf_op jit(solution)/shard_map/ppermute | solution.py:201
  37.3 1.5 %collective-permute-done.other_ref = bf16[16,16,1024]{2,1,0:T(8,128)(2,1)S(1)} collective-permute-done((bf16[16,16,1024]{2,1,0:T(8,128)(2,1)S(1)}, bf16[16,16,1024]{2,1,0:T(8,128)(2,1)S(1)}, u32[]{:S(2)}, u32[]{:S(2)}) %collective-permute-start) | collective-permute-done | bytes 524320 | tf_op jit(solution)/shard_map/ppermute | solution.py:201
  38.8 0.0 copy-done.4
  38.8 0.0 copy-done.2
  38.8 0.0 copy-start.3
  38.8 1.1 %copy-done.3 = bf16[2,512,384]{2,1,0:T(8,128)(2,1)S(1)} copy-done((bf16[2,512,384]{2,1,0:T(8,128)(2,1)S(1)}, bf16[2,512,384]{2,1,0:T(8,128)(2,1)}, u32[]{:S(2)}) %copy-start.3) | copy-done | bytes 786456
  40.0 3.9 %shard_map.94 = (f32[16,32,384]{2,1,0:T(8,128)S(1)}, bf16[16,32,384]{2,1,0:T(8,128)(2,1)S(1)}, bf16[2,3,256,512]{3,2,1,0:T(8,128)(2,1)S(1)}, bf16[2,3,256,512]{3...) custom-call(s32[2]{0:T(128)S(1)} %copy-done.4, s32[1]{0:T(128)} %bitcast.core_ref, bf16[2,512,384]{2,1,0:T(8,128)(2,1)S(1)} %copy-done.2, ...), custom_call_target="tpu_custom_call" | custom-call | tf_op jit(solution)/shard_map/pallas_call | solution.py:190
  43.9 0.0 copy-start
  43.9 1.2 %copy-done = bf16[2,3,256,512]{3,2,1,0:T(8,128)(2,1)} copy-done((bf16[2,3,256,512]{3,2,1,0:T(8,128)(2,1)}, bf16[2,3,256,512]{3,2,1,0:T(8,128)(2,1)S(1)}, u32[]{:S(2)}) %copy-start) | copy-done | bytes 1572888
  45.0 0.4 collective-permute-start.1
  45.4 1.4 %collective-permute-done.1.other_ref = bf16[16,32,384]{2,1,0:T(8,128)(2,1)S(1)} collective-permute-done((bf16[16,32,384]{2,1,0:T(8,128)(2,1)S(1)}, bf16[16,32,384]{2,1,0:T(8,128)(2,1)S(1)}, u32[]{:S(2)}, u32[]{:S(2)}) %collective-permute-start.1) | collective-permute-done | bytes 393248 | tf_op jit(solution)/shard_map/ppermute | solution.py:201
  46.7 0.1 shard_map.96
  46.9 17.6 %all_to_all.27.parts_ref = bf16[16,32,384]{2,1,0:T(8,128)(2,1)S(1)} all-to-all(bf16[16,32,384]{2,1,0:T(8,128)(2,1)S(1)} %shard_map.96), channel_id=1, replica_groups=mesh['z'=8,'yh'=2,'core'=2,'yl'=2,'x'=4] {'z','yh'}, dimensions={0} | all-to-all | bytes 786432 | tf_op jit(solution)/shard_map/all_to_all | solution.py:205
  64.5 0.1 shard_map.97
  64.5 18.2 %all_to_all.28.total_ref = bf16[16,32,384]{2,1,0:T(8,128)(2,1)S(1)} all-to-all(bf16[16,32,384]{2,1,0:T(8,128)(2,1)S(1)} %shard_map.97), channel_id=1, replica_groups=mesh['z'=8,'yh'=2,'core'=2,'yl'=2,'x'=4] {'z','yh'}, dimensions={0} | all-to-all | bytes 786432 | tf_op jit(solution)/shard_map/all_to_all | solution.py:205
  82.7 1.1 %shard_map.98 = (f32[128,384]{1,0:T(8,128)S(1)}, f32[128,384]{1,0:T(8,128)S(1)}, f32[256,1]{1,0:T(8,128)}) custom-call(s32[1]{0:T(128)} %bitcast.core_ref, bf16[2,16,16,256]{3,2,1,0:T(8,128)(2,1)S(1)} %get-tuple-element.20.columns_ref, bf16[16,32,384]{2,1,0:T(8,128)(2,1)S(1)} %all_to_all.28.total_ref), custom_call_target="tpu_custom_call" | custom-call | tf_op jit(solution)/shard_map/pallas_call | solution.py:190
  83.9 2.8 %collective-permute-start.2 = (f32[128,384]{1,0:T(8,128)S(1)}, f32[128,384]{1,0:T(8,128)S(1)}, u32[]{:S(2)}, u32[]{:S(2)}) collective-permute-start(f32[128,384]{1,0:T(8,128)S(1)} %get-tuple-element.24), channel_id=1, source_target_pairs={{0,8},{8,0},{1,9},{9,1},{2,10},{10,2},{3,11},{11,3},{4,12},{12,4},... | collective-permute-start | bytes 589832 | tf_op jit(solution)/shard_map/ppermute | solution.py:201
  86.6 6.0 %all-to-all-start.3 = ((f32[256,1,1]{2,1,0:T(1,128)}), f32[256,1,1]{2,1,0:T(1,128)S(1)}, u32[]{:S(2)}, u32[]{:S(2)}) async-start(f32[256,1,1]{2,1,0:T(1,128)} %bitcast.1), calls=%async_computation.3 | async-start | bytes 262144 | tf_op jit(solution)/shard_map/all_to_all | solution.py:205
  92.6 0.0 copy-start.1
  92.6 1.4 %copy-done.1 = bf16[2,3,256,512]{3,2,1,0:T(8,128)(2,1)S(1)} copy-done((bf16[2,3,256,512]{3,2,1,0:T(8,128)(2,1)S(1)}, bf16[2,3,256,512]{3,2,1,0:T(8,128)(2,1)}, u32[]{:S(2)}) %copy-start.1) | copy-done | bytes 1572888
  94.0 2.0 %shard_map.95 = (bf16[2,512,384]{2,1,0:T(8,128)(2,1)}, bf16[2,512,384]{2,1,0:T(8,128)(2,1)}) custom-call(s32[1]{0:T(128)} %bitcast.core_ref, bf16[16,16,1024]{2,1,0:T(8,128)(2,1)S(1)} %all_to_all.26.own_ref, bf16[16,16,1024]{2,1,0:T(8,128)(2,1)S(1)} %collective-permute-done.other_ref, bf16[2,3,256,512]{3,2,1,0:T(8,128)(2,1)S(1)} %get-tuple-element.16.probs_ref, ...), custom_call_target="tpu_custom_call" | custom-call | tf_op jit(solution)/shard_map/pallas_call | solution.py:190
  96.0 9.5 %all-to-all-done.3 = f32[256,1,1]{2,1,0:T(1,128)S(1)} async-done(((f32[256,1,1]{2,1,0:T(1,128)}), f32[256,1,1]{2,1,0:T(1,128)S(1)}, u32[]{:S(2)}, u32[]{:S(2)}) %all-to-all-start.3) | async-done | bytes 1056 | tf_op jit(solution)/shard_map/all_to_all | solution.py:205
  105.5 0.0 collective-permute-done.2.other_ref
  105.5 0.9 shard_map.99
Async XLA Ops:
  0.6 38.2 %copy-start.4 = (s32[2]{0:T(128)S(1)}, s32[2]{0:T(128)}, u32[]{:S(2)}) copy-start(s32[2]{0:T(128)} %lengths_ref.1) | copy-start | bytes 28
  0.6 38.2 %copy-start.2 = (bf16[2,512,384]{2,1,0:T(8,128)(2,1)S(1)}, bf16[2,512,384]{2,1,0:T(8,128)(2,1)}, u32[]{:S(2)}) copy-start(bf16[2,512,384]{2,1,0:T(8,128)(2,1)} %query_ref.1) | copy-start | bytes 2359300
  34.7 4.1 %collective-permute-start = (bf16[16,16,1024]{2,1,0:T(8,128)(2,1)S(1)}, bf16[16,16,1024]{2,1,0:T(8,128)(2,1)S(1)}, u32[]{:S(2)}, u32[]{:S(2)}) collective-permute-start(bf16[16,16,1024]{2,1,0:T(8,128)(2,1)S(1)} %all_to_all.26.own_ref), channel_id=1, source_target_pairs={{0,8},{8,0},{1,9},{9,1},{2,10},{10,2},{3,11},{11,3},{4,12},{12,4},... | collective-permute-start | bytes 1572872 | tf_op jit(solution)/shard_map/ppermute | solution.py:201
  38.8 1.1 %copy-start.3 = (bf16[2,512,384]{2,1,0:T(8,128)(2,1)S(1)}, bf16[2,512,384]{2,1,0:T(8,128)(2,1)}, u32[]{:S(2)}) copy-start(bf16[2,512,384]{2,1,0:T(8,128)(2,1)} %grad_ref.1) | copy-start | bytes 2359300
  43.9 1.2 %copy-start = (bf16[2,3,256,512]{3,2,1,0:T(8,128)(2,1)}, bf16[2,3,256,512]{3,2,1,0:T(8,128)(2,1)S(1)}, u32[]{:S(2)}) copy-start(bf16[2,3,256,512]{3,2,1,0:T(8,128)(2,1)S(1)} %get-tuple-element.17.dscore_ref) | copy-start | bytes 4718596
  45.0 1.7 %collective-permute-start.1 = (bf16[16,32,384]{2,1,0:T(8,128)(2,1)S(1)}, bf16[16,32,384]{2,1,0:T(8,128)(2,1)S(1)}, u32[]{:S(2)}, u32[]{:S(2)}) collective-permute-start(bf16[16,32,384]{2,1,0:T(8,128)(2,1)S(1)} %get-tuple-element.22), channel_id=1, source_target_pairs={{0,8},{8,0},{1,9},{9,1},{2,10},{10,2},{3,11},{11,3},{4,12},{12,4},... | collective-permute-start | bytes 1179656 | tf_op jit(solution)/shard_map/ppermute | solution.py:201
  83.9 21.6 %collective-permute-start.2 = (f32[128,384]{1,0:T(8,128)S(1)}, f32[128,384]{1,0:T(8,128)S(1)}, u32[]{:S(2)}, u32[]{:S(2)}) collective-permute-start(f32[128,384]{1,0:T(8,128)S(1)} %get-tuple-element.24), channel_id=1, source_target_pairs={{0,8},{8,0},{1,9},{9,1},{2,10},{10,2},{3,11},{11,3},{4,12},{12,4},... | collective-permute-start | bytes 589832 | tf_op jit(solution)/shard_map/ppermute | solution.py:201
  86.6 18.8 %all-to-all-start.3 = ((f32[256,1,1]{2,1,0:T(1,128)}), f32[256,1,1]{2,1,0:T(1,128)S(1)}, u32[]{:S(2)}, u32[]{:S(2)}) async-start(f32[256,1,1]{2,1,0:T(1,128)} %bitcast.1), calls=%async_computation.3 | async-start | bytes 262144 | tf_op jit(solution)/shard_map/all_to_all | solution.py:205
  92.6 1.4 %copy-start.1 = (bf16[2,3,256,512]{3,2,1,0:T(8,128)(2,1)S(1)}, bf16[2,3,256,512]{3,2,1,0:T(8,128)(2,1)}, u32[]{:S(2)}) copy-start(bf16[2,3,256,512]{3,2,1,0:T(8,128)(2,1)} %copy-done) | copy-start | bytes 4718596

commit v6 on v5

--- a/solution.py
+++ b/solution.py
@@ -17,6 +17,7 @@
 SEQ = ("z", "yh", "core")
 TP = ("yl", "x")
 ALL = SEQ + TP
+ONE_CORE = ZY + TP
 SCALING = 1.0 / math.sqrt(HEAD)
 BF16 = jnp.bfloat16
 F32 = jnp.float32
@@ -172,8 +173,8 @@
     square_ref[...] = jnp.broadcast_to(jnp.sum(lanes, keepdims=True), square_ref.shape)
 
 
-def scale_kernel(core_ref, own_ref, other_ref, squares_ref, key_ref, value_ref):
-    overall = jnp.sum(squares_ref[...], keepdims=True)
+def scale_kernel(core_ref, own_ref, other_ref, own_squares_ref, other_squares_ref, key_ref, value_ref):
+    overall = jnp.sum(own_squares_ref[...] + other_squares_ref[...], keepdims=True)
     spread = jnp.sqrt(overall / (2.0 * DT * HEADS * HEAD) + 1e-06)
     factor = 1.0 / jnp.maximum(spread, 1.0)
     first_core = core_ref[0] == 0
@@ -234,14 +235,14 @@
     pair = call(pair_sum_kernel, shape(block, BF16), own_sum, swap(other_sum))
     parts = exchange(pair, ZY)
     totals = exchange(call(total_kernel, shape(block, BF16), parts), ZY)
-    every = lax.axis_size(ALL)
+    every = lax.axis_size(ONE_CORE)
     weight = shape((HEAD, features), F32)
     own_raw, other_raw, squares = call(
         weight_kernel, [weight, weight, shape((every, 1), F32)], core, columns, totals, scalars=1,
     )
-    squares = exchange(squares, ALL)
+    squares = exchange(squares, ONE_CORE)
     key_weight_grad, value_weight_grad = call(
-        scale_kernel, [weight, weight], core, own_raw, swap(other_raw), squares, scalars=1,
+        scale_kernel, [weight, weight], core, own_raw, swap(other_raw), squares, swap(squares), scalars=1,
     )
     return attended, query_grad, key_weight_grad, value_weight_grad
 

time: 107 us -> 106 us (level)
  blocking collectives: 64.8 us -> 82.5 us
  waiting for transfers between devices: 12.4 us -> 2.89 us
  starting transfers between devices: 11.7 us -> 7.33 us
  local copies, waits for them, and re-layouts: 3.7 us -> 0.01 us
    all_to_all x3 -> x4, blocking collectives: 64.8 us -> 82.5 us  [exchange(): return lax.all_to_all(array, axes, 0, 0, tiled=True)]
    all_to_all x1 -> x0, waiting for transfers between devices: 9.46 us -> none  [exchange(): return lax.all_to_all(array, axes, 0, 0, tiled=True)]
    all_to_all x1 -> x0, starting transfers between devices: 5.97 us -> none  [exchange(): return lax.all_to_all(array, axes, 0, 0, tiled=True)]
    unnamed x10 -> x6, local copies, waits for them, and re-layouts: 3.7 us -> 0.01 us
    ppermute x3 -> x4, starting transfers between devices: 5.71 us -> 7.33 us  [swap(): return lax.ppermute(array, 'core', [(0, 1), (1, 0)])]
    ppermute x3 -> x4, waiting for transfers between devices: 2.89 us -> 2.89 us  [swap(): return lax.ppermute(array, 'core', [(0, 1), (1, 0)])]
  transfers between devices with their start and end apart: 4 -> 4, of which waited for: 3 -> 2; matrix products, arithmetic and copies ran while one was open for 0% -> 0% of each run, Pallas kernels for 2% -> 2%
where the time goes in v6:
time: 106 us
  blocking collectives  82.5 us (78%)
  Pallas kernels  12.5 us (12%)
  starting transfers between devices  7.33 us (7%)
  waiting for transfers between devices  2.89 us (3%)
    all_to_all x4, blocking collectives, exchange(): return lax.all_to_all(array, axes, 0, 0, tiled=True)  82.5 us
    pallas_call x7, Pallas kernels, call(): pl.pallas_call(kernel, out_shape=out, in_specs=specs, out_specs=out_spec...  12.5 us
    ppermute x4, starting transfers between devices, swap(): return lax.ppermute(array, 'core', [(0, 1), (1, 0)])  7.33 us
    ppermute x4, waiting for transfers between devices, swap(): return lax.ppermute(array, 'core', [(0, 1), (1, 0)])  2.89 us
  transfers between devices with their start and end apart: 4, of which 2 were waited for; matrix products, arithmetic and copies ran while one was open for 0% of the time, Pallas kernels for 2%

profile of v6, /device:TPU:1, one launch (start us, length us, event | category | flops | bytes accessed | tf_op | source)
XLA Modules:
  0.0 106.0 jit_solution(13392429073661007485)
XLA Ops:
  0.6 0.0 copy-start.2
  0.6 0.0 copy-start.1
  0.7 0.0 copy-start
  0.7 5.1 %shard_map.93 = bf16[16,16,1024]{2,1,0:T(8,128)(2,1)} custom-call(bf16[2,8,4096]{2,1,0:T(8,128)(2,1)} %text_ref.1, bf16[4096,384]{1,0:T(8,128)(2,1)} %key_ref.1, bf16[4096,384]{1,0:T(8,128)(2,1)} %value_ref.1), custom_call_target="tpu_custom_call" | custom-call | tf_op jit(solution)/shard_map/pallas_call | solution.py:191
  5.8 29.0 %all_to_all.26.own_ref = bf16[16,16,1024]{2,1,0:T(8,128)(2,1)S(1)} all-to-all(bf16[16,16,1024]{2,1,0:T(8,128)(2,1)} %shard_map.93), channel_id=1, replica_groups=mesh['z'=8,'yh'=2,'core'=2,'yl'=2,'x'=4] {'z','yh'}, dimensions={0} | all-to-all | bytes 1048576 | tf_op jit(solution)/shard_map/all_to_all | solution.py:206
  34.8 2.6 %collective-permute-start = (bf16[16,16,1024]{2,1,0:T(8,128)(2,1)S(1)}, bf16[16,16,1024]{2,1,0:T(8,128)(2,1)S(1)}, u32[]{:S(2)}, u32[]{:S(2)}) collective-permute-start(bf16[16,16,1024]{2,1,0:T(8,128)(2,1)S(1)} %all_to_all.26.own_ref), channel_id=1, source_target_pairs={{0,8},{8,0},{1,9},{9,1},{2,10},{10,2},{3,11},{11,3},{4,12},{12,4},... | collective-permute-start | bytes 1572872 | tf_op jit(solution)/shard_map/ppermute | solution.py:202
  37.3 1.5 %collective-permute-done.other_ref = bf16[16,16,1024]{2,1,0:T(8,128)(2,1)S(1)} collective-permute-done((bf16[16,16,1024]{2,1,0:T(8,128)(2,1)S(1)}, bf16[16,16,1024]{2,1,0:T(8,128)(2,1)S(1)}, u32[]{:S(2)}, u32[]{:S(2)}) %collective-permute-start) | collective-permute-done | bytes 524320 | tf_op jit(solution)/shard_map/ppermute | solution.py:202
  38.9 0.0 copy-done.2
  38.9 0.0 copy-done.1
  38.9 0.0 copy-done
  38.9 3.9 %shard_map.94 = (f32[16,32,384]{2,1,0:T(8,128)S(1)}, bf16[16,32,384]{2,1,0:T(8,128)(2,1)S(1)}, bf16[2,3,256,512]{3,2,1,0:T(8,128)(2,1)S(1)}, bf16[2,3,256,512]{3...) custom-call(s32[2]{0:T(128)S(1)} %copy-done.2, s32[1]{0:T(128)} %bitcast.core_ref, bf16[2,512,384]{2,1,0:T(8,128)(2,1)S(1)} %copy-done, ...), custom_call_target="tpu_custom_call" | custom-call | tf_op jit(solution)/shard_map/pallas_call | solution.py:191
  42.7 0.5 collective-permute-start.1
  43.2 1.4 %collective-permute-done.1.other_ref = bf16[16,32,384]{2,1,0:T(8,128)(2,1)S(1)} collective-permute-done((bf16[16,32,384]{2,1,0:T(8,128)(2,1)S(1)}, bf16[16,32,384]{2,1,0:T(8,128)(2,1)S(1)}, u32[]{:S(2)}, u32[]{:S(2)}) %collective-permute-start.1) | collective-permute-done | bytes 393248 | tf_op jit(solution)/shard_map/ppermute | solution.py:202
  44.5 0.1 shard_map.96
  44.6 17.6 %all_to_all.27.parts_ref = bf16[16,32,384]{2,1,0:T(8,128)(2,1)S(1)} all-to-all(bf16[16,32,384]{2,1,0:T(8,128)(2,1)S(1)} %shard_map.96), channel_id=1, replica_groups=mesh['z'=8,'yh'=2,'core'=2,'yl'=2,'x'=4] {'z','yh'}, dimensions={0} | all-to-all | bytes 786432 | tf_op jit(solution)/shard_map/all_to_all | solution.py:206
  62.2 0.1 shard_map.97
  62.3 18.2 %all_to_all.28.total_ref = bf16[16,32,384]{2,1,0:T(8,128)(2,1)S(1)} all-to-all(bf16[16,32,384]{2,1,0:T(8,128)(2,1)S(1)} %shard_map.97), channel_id=1, replica_groups=mesh['z'=8,'yh'=2,'core'=2,'yl'=2,'x'=4] {'z','yh'}, dimensions={0} | all-to-all | bytes 786432 | tf_op jit(solution)/shard_map/all_to_all | solution.py:206
  80.5 0.5 shard_map.98
  81.0 2.9 %collective-permute-start.2 = (f32[128,384]{1,0:T(8,128)S(1)}, f32[128,384]{1,0:T(8,128)S(1)}, u32[]{:S(2)}, u32[]{:S(2)}) collective-permute-start(f32[128,384]{1,0:T(8,128)S(1)} %get-tuple-element.24), channel_id=1, source_target_pairs={{0,8},{8,0},{1,9},{9,1},{2,10},{10,2},{3,11},{11,3},{4,12},{12,4},... | collective-permute-start | bytes 589832 | tf_op jit(solution)/shard_map/ppermute | solution.py:202
  83.9 17.8 %all_to_all.29 = f32[128,1,1]{2,1,0:T(1,128)S(1)} all-to-all(f32[128,1,1]{2,1,0:T(1,128)S(1)} %bitcast.5), channel_id=1, replica_groups=mesh['z'=8,'yh'=2,'core'=2,'yl'=2,'x'=4] {'z','yh','yl','x'}, dimensions={0} | all-to-all | bytes 1024 | tf_op jit(solution)/shard_map/all_to_all | solution.py:206
  101.6 1.4 %collective-permute-start.3 = (f32[128,1]{1,0:T(8,128)S(1)}, f32[128,1]{1,0:T(8,128)S(1)}, u32[]{:S(2)}, u32[]{:S(2)}) collective-permute-start(f32[128,1]{1,0:T(8,128)S(1)} %bitcast.3), channel_id=1, source_target_pairs={{0,8},{8,0},{1,9},{9,1},{2,10},{10,2},{3,11},{11,3},{4,12},{12,4},... | collective-permute-start | bytes 1544 | tf_op jit(solution)/shard_map/ppermute | solution.py:202
  103.1 2.0 %shard_map.95 = (bf16[2,512,384]{2,1,0:T(8,128)(2,1)}, bf16[2,512,384]{2,1,0:T(8,128)(2,1)}) custom-call(s32[1]{0:T(128)} %bitcast.core_ref, bf16[16,16,1024]{2,1,0:T(8,128)(2,1)S(1)} %all_to_all.26.own_ref, bf16[16,16,1024]{2,1,0:T(8,128)(2,1)S(1)} %collective-permute-done.other_ref, bf16[2,3,256,512]{3,2,1,0:T(8,128)(2,1)S(1)} %get-tuple-element.16.probs_ref, ...), custom_call_target="tpu_custom_call" | custom-call | tf_op jit(solution)/shard_map/pallas_call | solution.py:191
  105.0 0.0 collective-permute-done.3.other_squares_ref
  105.0 0.0 collective-permute-done.2.other_ref
  105.0 0.9 shard_map.99
Async XLA Ops:
  0.6 38.2 %copy-start.2 = (s32[2]{0:T(128)S(1)}, s32[2]{0:T(128)}, u32[]{:S(2)}) copy-start(s32[2]{0:T(128)} %lengths_ref.1) | copy-start | bytes 28
  0.6 38.2 %copy-start.1 = (bf16[2,512,384]{2,1,0:T(8,128)(2,1)S(1)}, bf16[2,512,384]{2,1,0:T(8,128)(2,1)}, u32[]{:S(2)}) copy-start(bf16[2,512,384]{2,1,0:T(8,128)(2,1)} %grad_ref.1) | copy-start | bytes 2359300
  0.7 38.2 %copy-start = (bf16[2,512,384]{2,1,0:T(8,128)(2,1)S(1)}, bf16[2,512,384]{2,1,0:T(8,128)(2,1)}, u32[]{:S(2)}) copy-start(bf16[2,512,384]{2,1,0:T(8,128)(2,1)} %query_ref.1) | copy-start | bytes 2359300
  34.8 4.1 %collective-permute-start = (bf16[16,16,1024]{2,1,0:T(8,128)(2,1)S(1)}, bf16[16,16,1024]{2,1,0:T(8,128)(2,1)S(1)}, u32[]{:S(2)}, u32[]{:S(2)}) collective-permute-start(bf16[16,16,1024]{2,1,0:T(8,128)(2,1)S(1)} %all_to_all.26.own_ref), channel_id=1, source_target_pairs={{0,8},{8,0},{1,9},{9,1},{2,10},{10,2},{3,11},{11,3},{4,12},{12,4},... | collective-permute-start | bytes 1572872 | tf_op jit(solution)/shard_map/ppermute | solution.py:202
  42.7 1.8 %collective-permute-start.1 = (bf16[16,32,384]{2,1,0:T(8,128)(2,1)S(1)}, bf16[16,32,384]{2,1,0:T(8,128)(2,1)S(1)}, u32[]{:S(2)}, u32[]{:S(2)}) collective-permute-start(bf16[16,32,384]{2,1,0:T(8,128)(2,1)S(1)} %get-tuple-element.22), channel_id=1, source_target_pairs={{0,8},{8,0},{1,9},{9,1},{2,10},{10,2},{3,11},{11,3},{4,12},{12,4},... | collective-permute-start | bytes 1179656 | tf_op jit(solution)/shard_map/ppermute | solution.py:202
  81.0 24.1 %collective-permute-start.2 = (f32[128,384]{1,0:T(8,128)S(1)}, f32[128,384]{1,0:T(8,128)S(1)}, u32[]{:S(2)}, u32[]{:S(2)}) collective-permute-start(f32[128,384]{1,0:T(8,128)S(1)} %get-tuple-element.24), channel_id=1, source_target_pairs={{0,8},{8,0},{1,9},{9,1},{2,10},{10,2},{3,11},{11,3},{4,12},{12,4},... | collective-permute-start | bytes 589832 | tf_op jit(solution)/shard_map/ppermute | solution.py:202
  101.6 3.4 %collective-permute-start.3 = (f32[128,1]{1,0:T(8,128)S(1)}, f32[128,1]{1,0:T(8,128)S(1)}, u32[]{:S(2)}, u32[]{:S(2)}) collective-permute-start(f32[128,1]{1,0:T(8,128)S(1)} %bitcast.3), channel_id=1, source_target_pairs={{0,8},{8,0},{1,9},{9,1},{2,10},{10,2},{3,11},{11,3},{4,12},{12,4},... | collective-permute-start | bytes 1544 | tf_op jit(solution)/shard_map/ppermute | solution.py:202

commit v7 on v5

--- a/solution.py
+++ b/solution.py
@@ -12,7 +12,7 @@
 DT = 4096
 HEADS = 24
 HEAD = 128
-CHUNKS = 4
+CHUNKS = 2
 ZY = ("z", "yh")
 SEQ = ("z", "yh", "core")
 TP = ("yl", "x")
@@ -36,7 +36,7 @@
     for at in range(CHUNKS):
         rows = pl.ds(at * step, step)
         for which, ref in enumerate((key_ref, value_ref)):
-            copy = pltpu.make_async_copy(ref.at[rows], held_ref.at[which, rows], arrived.at[which, at])
+            copy = pltpu.make_async_copy(ref.at[rows], held_ref.at[rows, pl.ds(which * features, features)], arrived.at[which, at])
             copy.start()
             copies.append(copy)
     states.wait()
@@ -44,17 +44,16 @@
     wide = DT // groups
     for g in range(groups):
         out_ref[g, :, 2 * features :] = text[:, g * wide : (g + 1) * wide]
-    sums = [None, None]
+    total = None
     for at in range(CHUNKS):
         rows = slice(at * step, (at + 1) * step)
-        for which in range(2):
-            copies[2 * at + which].wait()
-            part = dot(text[:, rows], held_ref[which, rows], 1, 0)
-            sums[which] = part if sums[which] is None else sums[which] + part
-    for which in range(2):
-        total = sums[which].astype(BF16)
-        for g in range(groups):
-            out_ref[g, :, which * features : (which + 1) * features] = total
+        copies[2 * at].wait()
+        copies[2 * at + 1].wait()
+        part = dot(text[:, rows], held_ref[rows], 1, 0)
+        total = part if total is None else total + part
+    total = total.astype(BF16)
+    for g in range(groups):
+        out_ref[g, :, : 2 * features] = total
 
 
 def text_of(own_ref, other_ref, first_core, b, first):
@@ -214,7 +213,7 @@
     packed = call(
         project_kernel, shape((groups, text_rows, wide + DT // groups), BF16), text_states, key_weight, value_weight, far=3, mib=61,
         scratch=[
-            pltpu.VMEM(text_states.shape, BF16), pltpu.VMEM((2, DT, features), BF16),
+            pltpu.VMEM(text_states.shape, BF16), pltpu.VMEM((DT, wide), BF16),
             pltpu.SemaphoreType.DMA((2, CHUNKS)), pltpu.SemaphoreType.DMA,
         ],
     )

time: 107 us -> 106 us (level)
  no operation moved by 1% of the time
where the time goes in v7:
time: 106 us
  blocking collectives  64.8 us (61%)
  Pallas kernels  12.8 us (12%)
  waiting for transfers between devices  12.4 us (12%)
  starting transfers between devices  11.7 us (11%)
  local copies, waits for them, and re-layouts  3.7 us (3%)
    all_to_all x3, blocking collectives, exchange(): return lax.all_to_all(array, axes, 0, 0, tiled=True)  64.8 us
    pallas_call x7, Pallas kernels, call(): pl.pallas_call(kernel, out_shape=out, in_specs=specs, out_specs=out_spec...  12.8 us
    all_to_all x1, waiting for transfers between devices, exchange(): return lax.all_to_all(array, axes, 0, 0, tiled=True)  9.46 us
    all_to_all x1, starting transfers between devices, exchange(): return lax.all_to_all(array, axes, 0, 0, tiled=True)  5.97 us
    ppermute x3, starting transfers between devices, swap(): return lax.ppermute(array, 'core', [(0, 1), (1, 0)])  5.72 us
    unnamed x10, local copies, waits for them, and re-layouts  3.7 us
    ppermute x3, waiting for transfers between devices, swap(): return lax.ppermute(array, 'core', [(0, 1), (1, 0)])  2.89 us
  transfers between devices with their start and end apart: 4, of which 3 were waited for; matrix products, arithmetic and copies ran while one was open for 0% of the time, Pallas kernels for 2%

profile of v7, /device:TPU:1, one launch (start us, length us, event | category | flops | bytes accessed | tf_op | source)
XLA Modules:
  0.0 106.0 jit_solution(16194450359378046009)
XLA Ops:
  0.6 0.0 copy-start.4
  0.6 0.0 copy-start.2
  0.7 4.7 %shard_map.93 = bf16[16,16,1024]{2,1,0:T(8,128)(2,1)} custom-call(bf16[2,8,4096]{2,1,0:T(8,128)(2,1)} %text_ref.1, bf16[4096,384]{1,0:T(8,128)(2,1)} %key_ref.1, bf16[4096,384]{1,0:T(8,128)(2,1)} %value_ref.1), custom_call_target="tpu_custom_call" | custom-call | tf_op jit(solution)/shard_map/pallas_call | solution.py:189
  5.4 29.0 %all_to_all.26.own_ref = bf16[16,16,1024]{2,1,0:T(8,128)(2,1)S(1)} all-to-all(bf16[16,16,1024]{2,1,0:T(8,128)(2,1)} %shard_map.93), channel_id=1, replica_groups=mesh['z'=8,'yh'=2,'core'=2,'yl'=2,'x'=4] {'z','yh'}, dimensions={0} | all-to-all | bytes 1048576 | tf_op jit(solution)/shard_map/all_to_all | solution.py:204
  34.4 2.6 %collective-permute-start = (bf16[16,16,1024]{2,1,0:T(8,128)(2,1)S(1)}, bf16[16,16,1024]{2,1,0:T(8,128)(2,1)S(1)}, u32[]{:S(2)}, u32[]{:S(2)}) collective-permute-start(bf16[16,16,1024]{2,1,0:T(8,128)(2,1)S(1)} %all_to_all.26.own_ref), channel_id=1, source_target_pairs={{0,8},{8,0},{1,9},{9,1},{2,10},{10,2},{3,11},{11,3},{4,12},{12,4},... | collective-permute-start | bytes 1572872 | tf_op jit(solution)/shard_map/ppermute | solution.py:200
  36.9 1.5 %collective-permute-done.other_ref = bf16[16,16,1024]{2,1,0:T(8,128)(2,1)S(1)} collective-permute-done((bf16[16,16,1024]{2,1,0:T(8,128)(2,1)S(1)}, bf16[16,16,1024]{2,1,0:T(8,128)(2,1)S(1)}, u32[]{:S(2)}, u32[]{:S(2)}) %collective-permute-start) | collective-permute-done | bytes 524320 | tf_op jit(solution)/shard_map/ppermute | solution.py:200
  38.5 0.0 copy-done.4
  38.5 0.0 copy-done.2
  38.5 0.0 copy-start.3
  38.5 1.1 %copy-done.3 = bf16[2,512,384]{2,1,0:T(8,128)(2,1)S(1)} copy-done((bf16[2,512,384]{2,1,0:T(8,128)(2,1)S(1)}, bf16[2,512,384]{2,1,0:T(8,128)(2,1)}, u32[]{:S(2)}) %copy-start.3) | copy-done | bytes 786456
  39.6 3.9 %shard_map.94 = (f32[16,32,384]{2,1,0:T(8,128)S(1)}, bf16[16,32,384]{2,1,0:T(8,128)(2,1)S(1)}, bf16[2,3,256,512]{3,2,1,0:T(8,128)(2,1)S(1)}, bf16[2,3,256,512]{3...) custom-call(s32[2]{0:T(128)S(1)} %copy-done.4, s32[1]{0:T(128)} %bitcast.core_ref, bf16[2,512,384]{2,1,0:T(8,128)(2,1)S(1)} %copy-done.2, ...), custom_call_target="tpu_custom_call" | custom-call | tf_op jit(solution)/shard_map/pallas_call | solution.py:189
  43.5 0.0 copy-start
  43.5 1.2 %copy-done = bf16[2,3,256,512]{3,2,1,0:T(8,128)(2,1)} copy-done((bf16[2,3,256,512]{3,2,1,0:T(8,128)(2,1)}, bf16[2,3,256,512]{3,2,1,0:T(8,128)(2,1)S(1)}, u32[]{:S(2)}) %copy-start) | copy-done | bytes 1572888
  44.7 0.4 collective-permute-start.1
  45.0 1.3 %collective-permute-done.1.other_ref = bf16[16,32,384]{2,1,0:T(8,128)(2,1)S(1)} collective-permute-done((bf16[16,32,384]{2,1,0:T(8,128)(2,1)S(1)}, bf16[16,32,384]{2,1,0:T(8,128)(2,1)S(1)}, u32[]{:S(2)}, u32[]{:S(2)}) %collective-permute-start.1) | collective-permute-done | bytes 393248 | tf_op jit(solution)/shard_map/ppermute | solution.py:200
  46.4 0.1 shard_map.96
  46.5 17.6 %all_to_all.27.parts_ref = bf16[16,32,384]{2,1,0:T(8,128)(2,1)S(1)} all-to-all(bf16[16,32,384]{2,1,0:T(8,128)(2,1)S(1)} %shard_map.96), channel_id=1, replica_groups=mesh['z'=8,'yh'=2,'core'=2,'yl'=2,'x'=4] {'z','yh'}, dimensions={0} | all-to-all | bytes 786432 | tf_op jit(solution)/shard_map/all_to_all | solution.py:204
  64.1 0.1 shard_map.97
  64.2 18.2 %all_to_all.28.total_ref = bf16[16,32,384]{2,1,0:T(8,128)(2,1)S(1)} all-to-all(bf16[16,32,384]{2,1,0:T(8,128)(2,1)S(1)} %shard_map.97), channel_id=1, replica_groups=mesh['z'=8,'yh'=2,'core'=2,'yl'=2,'x'=4] {'z','yh'}, dimensions={0} | all-to-all | bytes 786432 | tf_op jit(solution)/shard_map/all_to_all | solution.py:204
  82.4 1.1 %shard_map.98 = (f32[128,384]{1,0:T(8,128)S(1)}, f32[128,384]{1,0:T(8,128)S(1)}, f32[256,1]{1,0:T(8,128)}) custom-call(s32[1]{0:T(128)} %bitcast.core_ref, bf16[2,16,16,256]{3,2,1,0:T(8,128)(2,1)S(1)} %get-tuple-element.20.columns_ref, bf16[16,32,384]{2,1,0:T(8,128)(2,1)S(1)} %all_to_all.28.total_ref), custom_call_target="tpu_custom_call" | custom-call | tf_op jit(solution)/shard_map/pallas_call | solution.py:189
  83.5 2.8 %collective-permute-start.2 = (f32[128,384]{1,0:T(8,128)S(1)}, f32[128,384]{1,0:T(8,128)S(1)}, u32[]{:S(2)}, u32[]{:S(2)}) collective-permute-start(f32[128,384]{1,0:T(8,128)S(1)} %get-tuple-element.24), channel_id=1, source_target_pairs={{0,8},{8,0},{1,9},{9,1},{2,10},{10,2},{3,11},{11,3},{4,12},{12,4},... | collective-permute-start | bytes 589832 | tf_op jit(solution)/shard_map/ppermute | solution.py:200
  86.3 6.0 %all-to-all-start.3 = ((f32[256,1,1]{2,1,0:T(1,128)}), f32[256,1,1]{2,1,0:T(1,128)S(1)}, u32[]{:S(2)}, u32[]{:S(2)}) async-start(f32[256,1,1]{2,1,0:T(1,128)} %bitcast.1), calls=%async_computation.3 | async-start | bytes 262144 | tf_op jit(solution)/shard_map/all_to_all | solution.py:204
  92.2 0.0 copy-start.1
  92.3 1.4 %copy-done.1 = bf16[2,3,256,512]{3,2,1,0:T(8,128)(2,1)S(1)} copy-done((bf16[2,3,256,512]{3,2,1,0:T(8,128)(2,1)S(1)}, bf16[2,3,256,512]{3,2,1,0:T(8,128)(2,1)}, u32[]{:S(2)}) %copy-start.1) | copy-done | bytes 1572888
  93.7 2.0 %shard_map.95 = (bf16[2,512,384]{2,1,0:T(8,128)(2,1)}, bf16[2,512,384]{2,1,0:T(8,128)(2,1)}) custom-call(s32[1]{0:T(128)} %bitcast.core_ref, bf16[16,16,1024]{2,1,0:T(8,128)(2,1)S(1)} %all_to_all.26.own_ref, bf16[16,16,1024]{2,1,0:T(8,128)(2,1)S(1)} %collective-permute-done.other_ref, bf16[2,3,256,512]{3,2,1,0:T(8,128)(2,1)S(1)} %get-tuple-element.16.probs_ref, ...), custom_call_target="tpu_custom_call" | custom-call | tf_op jit(solution)/shard_map/pallas_call | solution.py:189
  95.6 9.5 %all-to-all-done.3 = f32[256,1,1]{2,1,0:T(1,128)S(1)} async-done(((f32[256,1,1]{2,1,0:T(1,128)}), f32[256,1,1]{2,1,0:T(1,128)S(1)}, u32[]{:S(2)}, u32[]{:S(2)}) %all-to-all-start.3) | async-done | bytes 1056 | tf_op jit(solution)/shard_map/all_to_all | solution.py:204
  105.1 0.0 collective-permute-done.2.other_ref
  105.1 0.9 shard_map.99
Async XLA Ops:
  0.6 37.8 %copy-start.4 = (s32[2]{0:T(128)S(1)}, s32[2]{0:T(128)}, u32[]{:S(2)}) copy-start(s32[2]{0:T(128)} %lengths_ref.1) | copy-start | bytes 28
  0.6 37.8 %copy-start.2 = (bf16[2,512,384]{2,1,0:T(8,128)(2,1)S(1)}, bf16[2,512,384]{2,1,0:T(8,128)(2,1)}, u32[]{:S(2)}) copy-start(bf16[2,512,384]{2,1,0:T(8,128)(2,1)} %query_ref.1) | copy-start | bytes 2359300
  34.4 4.1 %collective-permute-start = (bf16[16,16,1024]{2,1,0:T(8,128)(2,1)S(1)}, bf16[16,16,1024]{2,1,0:T(8,128)(2,1)S(1)}, u32[]{:S(2)}, u32[]{:S(2)}) collective-permute-start(bf16[16,16,1024]{2,1,0:T(8,128)(2,1)S(1)} %all_to_all.26.own_ref), channel_id=1, source_target_pairs={{0,8},{8,0},{1,9},{9,1},{2,10},{10,2},{3,11},{11,3},{4,12},{12,4},... | collective-permute-start | bytes 1572872 | tf_op jit(solution)/shard_map/ppermute | solution.py:200
  38.5 1.1 %copy-start.3 = (bf16[2,512,384]{2,1,0:T(8,128)(2,1)S(1)}, bf16[2,512,384]{2,1,0:T(8,128)(2,1)}, u32[]{:S(2)}) copy-start(bf16[2,512,384]{2,1,0:T(8,128)(2,1)} %grad_ref.1) | copy-start | bytes 2359300
  43.5 1.2 %copy-start = (bf16[2,3,256,512]{3,2,1,0:T(8,128)(2,1)}, bf16[2,3,256,512]{3,2,1,0:T(8,128)(2,1)S(1)}, u32[]{:S(2)}) copy-start(bf16[2,3,256,512]{3,2,1,0:T(8,128)(2,1)S(1)} %get-tuple-element.17.dscore_ref) | copy-start | bytes 4718596
  44.7 1.7 %collective-permute-start.1 = (bf16[16,32,384]{2,1,0:T(8,128)(2,1)S(1)}, bf16[16,32,384]{2,1,0:T(8,128)(2,1)S(1)}, u32[]{:S(2)}, u32[]{:S(2)}) collective-permute-start(bf16[16,32,384]{2,1,0:T(8,128)(2,1)S(1)} %get-tuple-element.22), channel_id=1, source_target_pairs={{0,8},{8,0},{1,9},{9,1},{2,10},{10,2},{3,11},{11,3},{4,12},{12,4},... | collective-permute-start | bytes 1179656 | tf_op jit(solution)/shard_map/ppermute | solution.py:200
  83.5 21.6 %collective-permute-start.2 = (f32[128,384]{1,0:T(8,128)S(1)}, f32[128,384]{1,0:T(8,128)S(1)}, u32[]{:S(2)}, u32[]{:S(2)}) collective-permute-start(f32[128,384]{1,0:T(8,128)S(1)} %get-tuple-element.24), channel_id=1, source_target_pairs={{0,8},{8,0},{1,9},{9,1},{2,10},{10,2},{3,11},{11,3},{4,12},{12,4},... | collective-permute-start | bytes 589832 | tf_op jit(solution)/shard_map/ppermute | solution.py:200
  86.3 18.8 %all-to-all-start.3 = ((f32[256,1,1]{2,1,0:T(1,128)}), f32[256,1,1]{2,1,0:T(1,128)S(1)}, u32[]{:S(2)}, u32[]{:S(2)}) async-start(f32[256,1,1]{2,1,0:T(1,128)} %bitcast.1), calls=%async_computation.3 | async-start | bytes 262144 | tf_op jit(solution)/shard_map/all_to_all | solution.py:204
  92.2 1.4 %copy-start.1 = (bf16[2,3,256,512]{3,2,1,0:T(8,128)(2,1)S(1)}, bf16[2,3,256,512]{3,2,1,0:T(8,128)(2,1)}, u32[]{:S(2)}) copy-start(bf16[2,3,256,512]{3,2,1,0:T(8,128)(2,1)} %copy-done) | copy-start | bytes 4718596

commit v8 on v7

--- a/solution.py
+++ b/solution.py
@@ -13,13 +13,17 @@
 HEADS = 24
 HEAD = 128
 CHUNKS = 2
-ZY = ("z", "yh")
+YZ = ("yh", "z")
 SEQ = ("z", "yh", "core")
 TP = ("yl", "x")
 ALL = SEQ + TP
 SCALING = 1.0 / math.sqrt(HEAD)
 BF16 = jnp.bfloat16
 F32 = jnp.float32
+
+
+def position(group, groups):
+    return group % (groups // 2) * 2 + group // (groups // 2)
 
 
 def dot(a, b, ca, cb):
@@ -43,7 +47,8 @@
     text = states_ref[...].reshape(-1, DT)
     wide = DT // groups
     for g in range(groups):
-        out_ref[g, :, 2 * features :] = text[:, g * wide : (g + 1) * wide]
+        first = position(g, groups) * wide
+        out_ref[g, :, 2 * features :] = text[:, first : first + wide]
     total = None
     for at in range(CHUNKS):
         rows = slice(at * step, (at + 1) * step)
@@ -70,7 +75,7 @@
     half = groups * 8
     place = lax.broadcasted_iota(jnp.int32, (2 * half, 1), 0)
     within = place % half
-    token = (within // 8) * 16 + (place // half) * 8 + within % 8
+    token = position(within // 8, groups) * 16 + (place // half) * 8 + within % 8
     columns_ref[0] = own_ref[:, :, 2 * features :]
     columns_ref[1] = other_ref[:, :, 2 * features :]
 
@@ -207,7 +212,7 @@
 def per_device(video_query, text_states, key_weight, value_weight, text_lengths, output_grad):
     samples, video_rows, features = video_query.shape
     text_rows = samples * text_states.shape[1]
-    groups = lax.axis_size(ZY)
+    groups = lax.axis_size(YZ)
     wide = 2 * features
     core = lax.axis_index("core").astype(jnp.int32).reshape(1)
     packed = call(
@@ -217,7 +222,7 @@
             pltpu.SemaphoreType.DMA((2, CHUNKS)), pltpu.SemaphoreType.DMA,
         ],
     )
-    own = exchange(packed, ZY)
+    own = exchange(packed, YZ)
     other = swap(own)
     like = shape(video_query.shape, BF16)
     block = (groups, 2 * text_rows, features)
@@ -231,8 +236,8 @@
         scratch=[pltpu.VMEM((2,) + video_query.shape, BF16), pltpu.SemaphoreType.DMA((2, samples))],
     )
     pair = call(pair_sum_kernel, shape(block, BF16), own_sum, swap(other_sum))
-    parts = exchange(pair, ZY)
-    totals = exchange(call(total_kernel, shape(block, BF16), parts), ZY)
+    parts = exchange(pair, YZ)
+    totals = exchange(call(total_kernel, shape(block, BF16), parts), YZ)
     every = lax.axis_size(ALL)
     weight = shape((HEAD, features), F32)
     own_raw, other_raw, squares = call(

time: 106 us -> 106 us (level)
  blocking collectives: 64.8 us -> 62 us
  starting transfers between devices: 11.7 us -> 13.8 us
    all_to_all x3, blocking collectives: 64.8 us -> 62 us  [exchange(): return lax.all_to_all(array, axes, 0, 0, tiled=True)]
    all_to_all x1, starting transfers between devices: 5.97 us -> 7.87 us  [exchange(): return lax.all_to_all(array, axes, 0, 0, tiled=True)]
where the time goes in v8:
time: 106 us; the launch traced here: 105 us
  blocking collectives  62 us (58%)
  starting transfers between devices  13.8 us (13%)
  Pallas kernels  12.9 us (12%)
  waiting for transfers between devices  12.4 us (12%)
  local copies, waits for them, and re-layouts  3.7 us (3%)
    all_to_all x3, blocking collectives, exchange(): return lax.all_to_all(array, axes, 0, 0, tiled=True)  62 us
    pallas_call x7, Pallas kernels, call(): pl.pallas_call(kernel, out_shape=out, in_specs=specs, out_specs=out_spec...  12.9 us
    all_to_all x1, waiting for transfers between devices, exchange(): return lax.all_to_all(array, axes, 0, 0, tiled=True)  9.46 us
    all_to_all x1, starting transfers between devices, exchange(): return lax.all_to_all(array, axes, 0, 0, tiled=True)  7.87 us
    ppermute x3, starting transfers between devices, swap(): return lax.ppermute(array, 'core', [(0, 1), (1, 0)])  5.94 us
    unnamed x10, local copies, waits for them, and re-layouts  3.7 us
    ppermute x3, waiting for transfers between devices, swap(): return lax.ppermute(array, 'core', [(0, 1), (1, 0)])  2.89 us
  transfers between devices with their start and end apart: 4, of which 3 were waited for; matrix products, arithmetic and copies ran while one was open for 0% of the time, Pallas kernels for 2%

profile of v8, /device:TPU:1, one launch (start us, length us, event | category | flops | bytes accessed | tf_op | source)
XLA Modules:
  0.0 105.4 jit_solution(8081269738577582088)
XLA Ops:
  0.6 0.0 copy-start.4
  0.6 0.0 copy-start.2
  0.7 4.7 %shard_map.93 = bf16[16,16,1024]{2,1,0:T(8,128)(2,1)} custom-call(bf16[2,8,4096]{2,1,0:T(8,128)(2,1)} %text_ref.1, bf16[4096,384]{1,0:T(8,128)(2,1)} %key_ref.1, bf16[4096,384]{1,0:T(8,128)(2,1)} %value_ref.1), custom_call_target="tpu_custom_call" | custom-call | tf_op jit(solution)/shard_map/pallas_call | solution.py:194
  5.4 27.0 %all_to_all.26.own_ref = bf16[16,16,1024]{2,1,0:T(8,128)(2,1)S(1)} all-to-all(bf16[16,16,1024]{2,1,0:T(8,128)(2,1)} %shard_map.93), channel_id=1, replica_groups=mesh['z'=8,'yh'=2,'core'=2,'yl'=2,'x'=4] {'yh','z'}, dimensions={0} | all-to-all | bytes 1048576 | tf_op jit(solution)/shard_map/all_to_all | solution.py:209
  32.4 2.8 %collective-permute-start = (bf16[16,16,1024]{2,1,0:T(8,128)(2,1)S(1)}, bf16[16,16,1024]{2,1,0:T(8,128)(2,1)S(1)}, u32[]{:S(2)}, u32[]{:S(2)}) collective-permute-start(bf16[16,16,1024]{2,1,0:T(8,128)(2,1)S(1)} %all_to_all.26.own_ref), channel_id=1, source_target_pairs={{0,8},{8,0},{1,9},{9,1},{2,10},{10,2},{3,11},{11,3},{4,12},{12,4},... | collective-permute-start | bytes 1572872 | tf_op jit(solution)/shard_map/ppermute | solution.py:205
  35.3 1.5 %collective-permute-done.other_ref = bf16[16,16,1024]{2,1,0:T(8,128)(2,1)S(1)} collective-permute-done((bf16[16,16,1024]{2,1,0:T(8,128)(2,1)S(1)}, bf16[16,16,1024]{2,1,0:T(8,128)(2,1)S(1)}, u32[]{:S(2)}, u32[]{:S(2)}) %collective-permute-start) | collective-permute-done | bytes 524320 | tf_op jit(solution)/shard_map/ppermute | solution.py:205
  36.8 0.0 copy-done.4
  36.8 0.0 copy-done.2
  36.8 0.0 copy-start.3
  36.8 1.1 %copy-done.3 = bf16[2,512,384]{2,1,0:T(8,128)(2,1)S(1)} copy-done((bf16[2,512,384]{2,1,0:T(8,128)(2,1)S(1)}, bf16[2,512,384]{2,1,0:T(8,128)(2,1)}, u32[]{:S(2)}) %copy-start.3) | copy-done | bytes 786456
  37.9 3.9 %shard_map.94 = (f32[16,32,384]{2,1,0:T(8,128)S(1)}, bf16[16,32,384]{2,1,0:T(8,128)(2,1)S(1)}, bf16[2,3,256,512]{3,2,1,0:T(8,128)(2,1)S(1)}, bf16[2,3,256,512]{3...) custom-call(s32[2]{0:T(128)S(1)} %copy-done.4, s32[1]{0:T(128)} %bitcast.core_ref, bf16[2,512,384]{2,1,0:T(8,128)(2,1)S(1)} %copy-done.2, ...), custom_call_target="tpu_custom_call" | custom-call | tf_op jit(solution)/shard_map/pallas_call | solution.py:194
  41.9 0.0 copy-start
  41.9 1.2 %copy-done = bf16[2,3,256,512]{3,2,1,0:T(8,128)(2,1)} copy-done((bf16[2,3,256,512]{3,2,1,0:T(8,128)(2,1)}, bf16[2,3,256,512]{3,2,1,0:T(8,128)(2,1)S(1)}, u32[]{:S(2)}) %copy-start) | copy-done | bytes 1572888
  43.1 0.4 collective-permute-start.1
  43.4 1.3 %collective-permute-done.1.other_ref = bf16[16,32,384]{2,1,0:T(8,128)(2,1)S(1)} collective-permute-done((bf16[16,32,384]{2,1,0:T(8,128)(2,1)S(1)}, bf16[16,32,384]{2,1,0:T(8,128)(2,1)S(1)}, u32[]{:S(2)}, u32[]{:S(2)}) %collective-permute-start.1) | collective-permute-done | bytes 393248 | tf_op jit(solution)/shard_map/ppermute | solution.py:205
  44.8 0.1 shard_map.96
  44.9 16.7 %all_to_all.27.parts_ref = bf16[16,32,384]{2,1,0:T(8,128)(2,1)S(1)} all-to-all(bf16[16,32,384]{2,1,0:T(8,128)(2,1)S(1)} %shard_map.96), channel_id=1, replica_groups=mesh['z'=8,'yh'=2,'core'=2,'yl'=2,'x'=4] {'yh','z'}, dimensions={0} | all-to-all | bytes 786432 | tf_op jit(solution)/shard_map/all_to_all | solution.py:209
  61.6 0.1 shard_map.97
  61.7 18.2 %all_to_all.28.total_ref = bf16[16,32,384]{2,1,0:T(8,128)(2,1)S(1)} all-to-all(bf16[16,32,384]{2,1,0:T(8,128)(2,1)S(1)} %shard_map.97), channel_id=1, replica_groups=mesh['z'=8,'yh'=2,'core'=2,'yl'=2,'x'=4] {'yh','z'}, dimensions={0} | all-to-all | bytes 786432 | tf_op jit(solution)/shard_map/all_to_all | solution.py:209
  79.9 1.1 %shard_map.98 = (f32[128,384]{1,0:T(8,128)S(1)}, f32[128,384]{1,0:T(8,128)S(1)}, f32[256,1]{1,0:T(8,128)}) custom-call(s32[1]{0:T(128)} %bitcast.core_ref, bf16[2,16,16,256]{3,2,1,0:T(8,128)(2,1)S(1)} %get-tuple-element.20.columns_ref, bf16[16,32,384]{2,1,0:T(8,128)(2,1)S(1)} %all_to_all.28.total_ref), custom_call_target="tpu_custom_call" | custom-call | tf_op jit(solution)/shard_map/pallas_call | solution.py:194
  81.0 2.7 %collective-permute-start.2 = (f32[128,384]{1,0:T(8,128)S(1)}, f32[128,384]{1,0:T(8,128)S(1)}, u32[]{:S(2)}, u32[]{:S(2)}) collective-permute-start(f32[128,384]{1,0:T(8,128)S(1)} %get-tuple-element.24), channel_id=1, source_target_pairs={{0,8},{8,0},{1,9},{9,1},{2,10},{10,2},{3,11},{11,3},{4,12},{12,4},... | collective-permute-start | bytes 589832 | tf_op jit(solution)/shard_map/ppermute | solution.py:205
  83.7 7.9 %all-to-all-start.3 = ((f32[256,1,1]{2,1,0:T(1,128)}), f32[256,1,1]{2,1,0:T(1,128)S(1)}, u32[]{:S(2)}, u32[]{:S(2)}) async-start(f32[256,1,1]{2,1,0:T(1,128)} %bitcast.1), calls=%async_computation.3 | async-start | bytes 262144 | tf_op jit(solution)/shard_map/all_to_all | solution.py:209
  91.6 0.0 copy-start.1
  91.6 1.4 %copy-done.1 = bf16[2,3,256,512]{3,2,1,0:T(8,128)(2,1)S(1)} copy-done((bf16[2,3,256,512]{3,2,1,0:T(8,128)(2,1)S(1)}, bf16[2,3,256,512]{3,2,1,0:T(8,128)(2,1)}, u32[]{:S(2)}) %copy-start.1) | copy-done | bytes 1572888
  93.0 2.0 %shard_map.95 = (bf16[2,512,384]{2,1,0:T(8,128)(2,1)}, bf16[2,512,384]{2,1,0:T(8,128)(2,1)}) custom-call(s32[1]{0:T(128)} %bitcast.core_ref, bf16[16,16,1024]{2,1,0:T(8,128)(2,1)S(1)} %all_to_all.26.own_ref, bf16[16,16,1024]{2,1,0:T(8,128)(2,1)S(1)} %collective-permute-done.other_ref, bf16[2,3,256,512]{3,2,1,0:T(8,128)(2,1)S(1)} %get-tuple-element.16.probs_ref, ...), custom_call_target="tpu_custom_call" | custom-call | tf_op jit(solution)/shard_map/pallas_call | solution.py:194
  95.0 9.5 %all-to-all-done.3 = f32[256,1,1]{2,1,0:T(1,128)S(1)} async-done(((f32[256,1,1]{2,1,0:T(1,128)}), f32[256,1,1]{2,1,0:T(1,128)S(1)}, u32[]{:S(2)}, u32[]{:S(2)}) %all-to-all-start.3) | async-done | bytes 1056 | tf_op jit(solution)/shard_map/all_to_all | solution.py:209
  104.5 0.0 collective-permute-done.2.other_ref
  104.5 0.9 shard_map.99
Async XLA Ops:
  0.6 36.2 %copy-start.4 = (s32[2]{0:T(128)S(1)}, s32[2]{0:T(128)}, u32[]{:S(2)}) copy-start(s32[2]{0:T(128)} %lengths_ref.1) | copy-start | bytes 28
  0.6 36.2 %copy-start.2 = (bf16[2,512,384]{2,1,0:T(8,128)(2,1)S(1)}, bf16[2,512,384]{2,1,0:T(8,128)(2,1)}, u32[]{:S(2)}) copy-start(bf16[2,512,384]{2,1,0:T(8,128)(2,1)} %query_ref.1) | copy-start | bytes 2359300
  32.4 4.4 %collective-permute-start = (bf16[16,16,1024]{2,1,0:T(8,128)(2,1)S(1)}, bf16[16,16,1024]{2,1,0:T(8,128)(2,1)S(1)}, u32[]{:S(2)}, u32[]{:S(2)}) collective-permute-start(bf16[16,16,1024]{2,1,0:T(8,128)(2,1)S(1)} %all_to_all.26.own_ref), channel_id=1, source_target_pairs={{0,8},{8,0},{1,9},{9,1},{2,10},{10,2},{3,11},{11,3},{4,12},{12,4},... | collective-permute-start | bytes 1572872 | tf_op jit(solution)/shard_map/ppermute | solution.py:205
  36.8 1.1 %copy-start.3 = (bf16[2,512,384]{2,1,0:T(8,128)(2,1)S(1)}, bf16[2,512,384]{2,1,0:T(8,128)(2,1)}, u32[]{:S(2)}) copy-start(bf16[2,512,384]{2,1,0:T(8,128)(2,1)} %grad_ref.1) | copy-start | bytes 2359300
  41.9 1.2 %copy-start = (bf16[2,3,256,512]{3,2,1,0:T(8,128)(2,1)}, bf16[2,3,256,512]{3,2,1,0:T(8,128)(2,1)S(1)}, u32[]{:S(2)}) copy-start(bf16[2,3,256,512]{3,2,1,0:T(8,128)(2,1)S(1)} %get-tuple-element.17.dscore_ref) | copy-start | bytes 4718596
  43.1 1.7 %collective-permute-start.1 = (bf16[16,32,384]{2,1,0:T(8,128)(2,1)S(1)}, bf16[16,32,384]{2,1,0:T(8,128)(2,1)S(1)}, u32[]{:S(2)}, u32[]{:S(2)}) collective-permute-start(bf16[16,32,384]{2,1,0:T(8,128)(2,1)S(1)} %get-tuple-element.22), channel_id=1, source_target_pairs={{0,8},{8,0},{1,9},{9,1},{2,10},{10,2},{3,11},{11,3},{4,12},{12,4},... | collective-permute-start | bytes 1179656 | tf_op jit(solution)/shard_map/ppermute | solution.py:205
  81.0 23.4 %collective-permute-start.2 = (f32[128,384]{1,0:T(8,128)S(1)}, f32[128,384]{1,0:T(8,128)S(1)}, u32[]{:S(2)}, u32[]{:S(2)}) collective-permute-start(f32[128,384]{1,0:T(8,128)S(1)} %get-tuple-element.24), channel_id=1, source_target_pairs={{0,8},{8,0},{1,9},{9,1},{2,10},{10,2},{3,11},{11,3},{4,12},{12,4},... | collective-permute-start | bytes 589832 | tf_op jit(solution)/shard_map/ppermute | solution.py:205
  83.7 20.7 %all-to-all-start.3 = ((f32[256,1,1]{2,1,0:T(1,128)}), f32[256,1,1]{2,1,0:T(1,128)S(1)}, u32[]{:S(2)}, u32[]{:S(2)}) async-start(f32[256,1,1]{2,1,0:T(1,128)} %bitcast.1), calls=%async_computation.3 | async-start | bytes 262144 | tf_op jit(solution)/shard_map/all_to_all | solution.py:209
  91.6 1.4 %copy-start.1 = (bf16[2,3,256,512]{3,2,1,0:T(8,128)(2,1)S(1)}, bf16[2,3,256,512]{3,2,1,0:T(8,128)(2,1)}, u32[]{:S(2)}) copy-start(bf16[2,3,256,512]{3,2,1,0:T(8,128)(2,1)} %copy-done) | copy-start | bytes 4718596

commit v9 on v8

--- a/solution.py
+++ b/solution.py
@@ -133,10 +133,11 @@
             held_ref[0, b, :, cols] = dot(probs_ref[b, h], value, 0, 0).astype(BF16)
             key = text_of(own_ref, other_ref, first_core, b, h * HEAD)
             held_ref[1, b, :, cols] = dot(dscore_ref[b, h], key, 0, 0).astype(BF16)
-        for which, ref in enumerate((attended_ref, query_grad_ref)):
-            copy = pltpu.make_async_copy(held_ref.at[which, b], ref.at[b], sent.at[which, b])
-            copy.start()
-            copies.append(copy)
+            part = pl.ds(h * HEAD, HEAD)
+            for which, ref in enumerate((attended_ref, query_grad_ref)):
+                copy = pltpu.make_async_copy(held_ref.at[which, b, :, part], ref.at[b, :, part], sent.at[which, b * heads + h])
+                copy.start()
+                copies.append(copy)
     for copy in copies:
         copy.wait()
 
@@ -233,7 +234,7 @@
     )
     attended, query_grad = call(
         attend_kernel, [like, like], core, own, other, probs, dscore, scalars=1, far_out=True,
-        scratch=[pltpu.VMEM((2,) + video_query.shape, BF16), pltpu.SemaphoreType.DMA((2, samples))],
+        scratch=[pltpu.VMEM((2,) + video_query.shape, BF16), pltpu.SemaphoreType.DMA((2, samples * features // HEAD))],
     )
     pair = call(pair_sum_kernel, shape(block, BF16), own_sum, swap(other_sum))
     parts = exchange(pair, YZ)

time: 106 us -> 106 us (level)
  no operation moved by 1% of the time
where the time goes in v9:
time: 106 us; the launch traced here: 105 us
  blocking collectives  62 us (58%)
  starting transfers between devices  13.8 us (13%)
  Pallas kernels  12.8 us (12%)
  waiting for transfers between devices  12.5 us (12%)
  local copies, waits for them, and re-layouts  3.7 us (3%)
    all_to_all x3, blocking collectives, exchange(): return lax.all_to_all(array, axes, 0, 0, tiled=True)  62 us
    pallas_call x7, Pallas kernels, call(): pl.pallas_call(kernel, out_shape=out, in_specs=specs, out_specs=out_spec...  12.8 us
    all_to_all x1, waiting for transfers between devices, exchange(): return lax.all_to_all(array, axes, 0, 0, tiled=True)  9.57 us
    all_to_all x1, starting transfers between devices, exchange(): return lax.all_to_all(array, axes, 0, 0, tiled=True)  7.87 us
    ppermute x3, starting transfers between devices, swap(): return lax.ppermute(array, 'core', [(0, 1), (1, 0)])  5.94 us
    unnamed x10, local copies, waits for them, and re-layouts  3.7 us
    ppermute x3, waiting for transfers between devices, swap(): return lax.ppermute(array, 'core', [(0, 1), (1, 0)])  2.89 us
  transfers between devices with their start and end apart: 4, of which 3 were waited for; matrix products, arithmetic and copies ran while one was open for 0% of the time, Pallas kernels for 2%

profile of v9, /device:TPU:1, one launch (start us, length us, event | category | flops | bytes accessed | tf_op | source)
XLA Modules:
  0.0 105.4 jit_solution(8374421184630917854)
XLA Ops:
  0.6 0.0 copy-start.4
  0.6 0.0 copy-start.2
  0.7 4.7 %shard_map.93 = bf16[16,16,1024]{2,1,0:T(8,128)(2,1)} custom-call(bf16[2,8,4096]{2,1,0:T(8,128)(2,1)} %text_ref.1, bf16[4096,384]{1,0:T(8,128)(2,1)} %key_ref.1, bf16[4096,384]{1,0:T(8,128)(2,1)} %value_ref.1), custom_call_target="tpu_custom_call" | custom-call | tf_op jit(solution)/shard_map/pallas_call | solution.py:195
  5.4 27.0 %all_to_all.26.own_ref = bf16[16,16,1024]{2,1,0:T(8,128)(2,1)S(1)} all-to-all(bf16[16,16,1024]{2,1,0:T(8,128)(2,1)} %shard_map.93), channel_id=1, replica_groups=mesh['z'=8,'yh'=2,'core'=2,'yl'=2,'x'=4] {'yh','z'}, dimensions={0} | all-to-all | bytes 1048576 | tf_op jit(solution)/shard_map/all_to_all | solution.py:210
  32.4 2.8 %collective-permute-start = (bf16[16,16,1024]{2,1,0:T(8,128)(2,1)S(1)}, bf16[16,16,1024]{2,1,0:T(8,128)(2,1)S(1)}, u32[]{:S(2)}, u32[]{:S(2)}) collective-permute-start(bf16[16,16,1024]{2,1,0:T(8,128)(2,1)S(1)} %all_to_all.26.own_ref), channel_id=1, source_target_pairs={{0,8},{8,0},{1,9},{9,1},{2,10},{10,2},{3,11},{11,3},{4,12},{12,4},... | collective-permute-start | bytes 1572872 | tf_op jit(solution)/shard_map/ppermute | solution.py:206
  35.3 1.5 %collective-permute-done.other_ref = bf16[16,16,1024]{2,1,0:T(8,128)(2,1)S(1)} collective-permute-done((bf16[16,16,1024]{2,1,0:T(8,128)(2,1)S(1)}, bf16[16,16,1024]{2,1,0:T(8,128)(2,1)S(1)}, u32[]{:S(2)}, u32[]{:S(2)}) %collective-permute-start) | collective-permute-done | bytes 524320 | tf_op jit(solution)/shard_map/ppermute | solution.py:206
  36.8 0.0 copy-done.4
  36.8 0.0 copy-done.2
  36.8 0.0 copy-start.3
  36.8 1.1 %copy-done.3 = bf16[2,512,384]{2,1,0:T(8,128)(2,1)S(1)} copy-done((bf16[2,512,384]{2,1,0:T(8,128)(2,1)S(1)}, bf16[2,512,384]{2,1,0:T(8,128)(2,1)}, u32[]{:S(2)}) %copy-start.3) | copy-done | bytes 786456
  37.9 3.9 %shard_map.94 = (f32[16,32,384]{2,1,0:T(8,128)S(1)}, bf16[16,32,384]{2,1,0:T(8,128)(2,1)S(1)}, bf16[2,3,256,512]{3,2,1,0:T(8,128)(2,1)S(1)}, bf16[2,3,256,512]{3...) custom-call(s32[2]{0:T(128)S(1)} %copy-done.4, s32[1]{0:T(128)} %bitcast.core_ref, bf16[2,512,384]{2,1,0:T(8,128)(2,1)S(1)} %copy-done.2, ...), custom_call_target="tpu_custom_call" | custom-call | tf_op jit(solution)/shard_map/pallas_call | solution.py:195
  41.9 0.0 copy-start
  41.9 1.2 %copy-done = bf16[2,3,256,512]{3,2,1,0:T(8,128)(2,1)} copy-done((bf16[2,3,256,512]{3,2,1,0:T(8,128)(2,1)}, bf16[2,3,256,512]{3,2,1,0:T(8,128)(2,1)S(1)}, u32[]{:S(2)}) %copy-start) | copy-done | bytes 1572888
  43.1 0.4 collective-permute-start.1
  43.4 1.3 %collective-permute-done.1.other_ref = bf16[16,32,384]{2,1,0:T(8,128)(2,1)S(1)} collective-permute-done((bf16[16,32,384]{2,1,0:T(8,128)(2,1)S(1)}, bf16[16,32,384]{2,1,0:T(8,128)(2,1)S(1)}, u32[]{:S(2)}, u32[]{:S(2)}) %collective-permute-start.1) | collective-permute-done | bytes 393248 | tf_op jit(solution)/shard_map/ppermute | solution.py:206
  44.8 0.1 shard_map.96
  44.9 16.7 %all_to_all.27.parts_ref = bf16[16,32,384]{2,1,0:T(8,128)(2,1)S(1)} all-to-all(bf16[16,32,384]{2,1,0:T(8,128)(2,1)S(1)} %shard_map.96), channel_id=1, replica_groups=mesh['z'=8,'yh'=2,'core'=2,'yl'=2,'x'=4] {'yh','z'}, dimensions={0} | all-to-all | bytes 786432 | tf_op jit(solution)/shard_map/all_to_all | solution.py:210
  61.6 0.1 shard_map.97
  61.7 18.2 %all_to_all.28.total_ref = bf16[16,32,384]{2,1,0:T(8,128)(2,1)S(1)} all-to-all(bf16[16,32,384]{2,1,0:T(8,128)(2,1)S(1)} %shard_map.97), channel_id=1, replica_groups=mesh['z'=8,'yh'=2,'core'=2,'yl'=2,'x'=4] {'yh','z'}, dimensions={0} | all-to-all | bytes 786432 | tf_op jit(solution)/shard_map/all_to_all | solution.py:210
  79.9 1.1 %shard_map.98 = (f32[128,384]{1,0:T(8,128)S(1)}, f32[128,384]{1,0:T(8,128)S(1)}, f32[256,1]{1,0:T(8,128)}) custom-call(s32[1]{0:T(128)} %bitcast.core_ref, bf16[2,16,16,256]{3,2,1,0:T(8,128)(2,1)S(1)} %get-tuple-element.20.columns_ref, bf16[16,32,384]{2,1,0:T(8,128)(2,1)S(1)} %all_to_all.28.total_ref), custom_call_target="tpu_custom_call" | custom-call | tf_op jit(solution)/shard_map/pallas_call | solution.py:195
  81.0 2.7 %collective-permute-start.2 = (f32[128,384]{1,0:T(8,128)S(1)}, f32[128,384]{1,0:T(8,128)S(1)}, u32[]{:S(2)}, u32[]{:S(2)}) collective-permute-start(f32[128,384]{1,0:T(8,128)S(1)} %get-tuple-element.24), channel_id=1, source_target_pairs={{0,8},{8,0},{1,9},{9,1},{2,10},{10,2},{3,11},{11,3},{4,12},{12,4},... | collective-permute-start | bytes 589832 | tf_op jit(solution)/shard_map/ppermute | solution.py:206
  83.7 7.9 %all-to-all-start.3 = ((f32[256,1,1]{2,1,0:T(1,128)}), f32[256,1,1]{2,1,0:T(1,128)S(1)}, u32[]{:S(2)}, u32[]{:S(2)}) async-start(f32[256,1,1]{2,1,0:T(1,128)} %bitcast.1), calls=%async_computation.3 | async-start | bytes 262144 | tf_op jit(solution)/shard_map/all_to_all | solution.py:210
  91.6 0.0 copy-start.1
  91.6 1.4 %copy-done.1 = bf16[2,3,256,512]{3,2,1,0:T(8,128)(2,1)S(1)} copy-done((bf16[2,3,256,512]{3,2,1,0:T(8,128)(2,1)S(1)}, bf16[2,3,256,512]{3,2,1,0:T(8,128)(2,1)}, u32[]{:S(2)}) %copy-start.1) | copy-done | bytes 1572888
  93.0 1.8 %shard_map.95 = (bf16[2,512,384]{2,1,0:T(8,128)(2,1)}, bf16[2,512,384]{2,1,0:T(8,128)(2,1)}) custom-call(s32[1]{0:T(128)} %bitcast.core_ref, bf16[16,16,1024]{2,1,0:T(8,128)(2,1)S(1)} %all_to_all.26.own_ref, bf16[16,16,1024]{2,1,0:T(8,128)(2,1)S(1)} %collective-permute-done.other_ref, bf16[2,3,256,512]{3,2,1,0:T(8,128)(2,1)S(1)} %get-tuple-element.16.probs_ref, ...), custom_call_target="tpu_custom_call" | custom-call | tf_op jit(solution)/shard_map/pallas_call | solution.py:195
  94.9 9.6 %all-to-all-done.3 = f32[256,1,1]{2,1,0:T(1,128)S(1)} async-done(((f32[256,1,1]{2,1,0:T(1,128)}), f32[256,1,1]{2,1,0:T(1,128)S(1)}, u32[]{:S(2)}, u32[]{:S(2)}) %all-to-all-start.3) | async-done | bytes 1056 | tf_op jit(solution)/shard_map/all_to_all | solution.py:210
  104.5 0.0 collective-permute-done.2.other_ref
  104.5 0.9 shard_map.99
Async XLA Ops:
  0.6 36.2 %copy-start.4 = (s32[2]{0:T(128)S(1)}, s32[2]{0:T(128)}, u32[]{:S(2)}) copy-start(s32[2]{0:T(128)} %lengths_ref.1) | copy-start | bytes 28
  0.6 36.2 %copy-start.2 = (bf16[2,512,384]{2,1,0:T(8,128)(2,1)S(1)}, bf16[2,512,384]{2,1,0:T(8,128)(2,1)}, u32[]{:S(2)}) copy-start(bf16[2,512,384]{2,1,0:T(8,128)(2,1)} %query_ref.1) | copy-start | bytes 2359300
  32.4 4.4 %collective-permute-start = (bf16[16,16,1024]{2,1,0:T(8,128)(2,1)S(1)}, bf16[16,16,1024]{2,1,0:T(8,128)(2,1)S(1)}, u32[]{:S(2)}, u32[]{:S(2)}) collective-permute-start(bf16[16,16,1024]{2,1,0:T(8,128)(2,1)S(1)} %all_to_all.26.own_ref), channel_id=1, source_target_pairs={{0,8},{8,0},{1,9},{9,1},{2,10},{10,2},{3,11},{11,3},{4,12},{12,4},... | collective-permute-start | bytes 1572872 | tf_op jit(solution)/shard_map/ppermute | solution.py:206
  36.8 1.1 %copy-start.3 = (bf16[2,512,384]{2,1,0:T(8,128)(2,1)S(1)}, bf16[2,512,384]{2,1,0:T(8,128)(2,1)}, u32[]{:S(2)}) copy-start(bf16[2,512,384]{2,1,0:T(8,128)(2,1)} %grad_ref.1) | copy-start | bytes 2359300
  41.9 1.2 %copy-start = (bf16[2,3,256,512]{3,2,1,0:T(8,128)(2,1)}, bf16[2,3,256,512]{3,2,1,0:T(8,128)(2,1)S(1)}, u32[]{:S(2)}) copy-start(bf16[2,3,256,512]{3,2,1,0:T(8,128)(2,1)S(1)} %get-tuple-element.17.dscore_ref) | copy-start | bytes 4718596
  43.1 1.7 %collective-permute-start.1 = (bf16[16,32,384]{2,1,0:T(8,128)(2,1)S(1)}, bf16[16,32,384]{2,1,0:T(8,128)(2,1)S(1)}, u32[]{:S(2)}, u32[]{:S(2)}) collective-permute-start(bf16[16,32,384]{2,1,0:T(8,128)(2,1)S(1)} %get-tuple-element.22), channel_id=1, source_target_pairs={{0,8},{8,0},{1,9},{9,1},{2,10},{10,2},{3,11},{11,3},{4,12},{12,4},... | collective-permute-start | bytes 1179656 | tf_op jit(solution)/shard_map/ppermute | solution.py:206
  81.0 23.4 %collective-permute-start.2 = (f32[128,384]{1,0:T(8,128)S(1)}, f32[128,384]{1,0:T(8,128)S(1)}, u32[]{:S(2)}, u32[]{:S(2)}) collective-permute-start(f32[128,384]{1,0:T(8,128)S(1)} %get-tuple-element.24), channel_id=1, source_target_pairs={{0,8},{8,0},{1,9},{9,1},{2,10},{10,2},{3,11},{11,3},{4,12},{12,4},... | collective-permute-start | bytes 589832 | tf_op jit(solution)/shard_map/ppermute | solution.py:206
  83.7 20.7 %all-to-all-start.3 = ((f32[256,1,1]{2,1,0:T(1,128)}), f32[256,1,1]{2,1,0:T(1,128)S(1)}, u32[]{:S(2)}, u32[]{:S(2)}) async-start(f32[256,1,1]{2,1,0:T(1,128)} %bitcast.1), calls=%async_computation.3 | async-start | bytes 262144 | tf_op jit(solution)/shard_map/all_to_all | solution.py:210
  91.6 1.4 %copy-start.1 = (bf16[2,3,256,512]{3,2,1,0:T(8,128)(2,1)S(1)}, bf16[2,3,256,512]{3,2,1,0:T(8,128)(2,1)}, u32[]{:S(2)}) copy-start(bf16[2,3,256,512]{3,2,1,0:T(8,128)(2,1)} %copy-done) | copy-start | bytes 4718596

commit v10 on v9

--- a/solution.py
+++ b/solution.py
@@ -31,7 +31,6 @@
 
 
 def project_kernel(text_ref, key_ref, value_ref, out_ref, states_ref, held_ref, arrived, here):
-    groups = out_ref.shape[0]
     features = key_ref.shape[1]
     step = DT // CHUNKS
     states = pltpu.make_async_copy(text_ref, states_ref, here)
@@ -45,10 +44,6 @@
             copies.append(copy)
     states.wait()
     text = states_ref[...].reshape(-1, DT)
-    wide = DT // groups
-    for g in range(groups):
-        first = position(g, groups) * wide
-        out_ref[g, :, 2 * features :] = text[:, first : first + wide]
     total = None
     for at in range(CHUNKS):
         rows = slice(at * step, (at + 1) * step)
@@ -56,9 +51,19 @@
         copies[2 * at + 1].wait()
         part = dot(text[:, rows], held_ref[rows], 1, 0)
         total = part if total is None else total + part
-    total = total.astype(BF16)
+    out_ref[...] = total.astype(BF16)
+
+
+def pack_kernel(text_ref, part_ref, out_ref):
+    groups = out_ref.shape[0]
+    features = part_ref.shape[1]
+    wide = DT // groups
+    text = text_ref[...].reshape(-1, DT)
+    part = part_ref[...]
     for g in range(groups):
-        out_ref[g, :, : 2 * features] = total
+        first = position(g, groups) * wide
+        out_ref[g, :, :features] = part
+        out_ref[g, :, features:] = text[:, first : first + wide]
 
 
 def text_of(own_ref, other_ref, first_core, b, first):
@@ -216,13 +221,14 @@
     groups = lax.axis_size(YZ)
     wide = 2 * features
     core = lax.axis_index("core").astype(jnp.int32).reshape(1)
-    packed = call(
-        project_kernel, shape((groups, text_rows, wide + DT // groups), BF16), text_states, key_weight, value_weight, far=3, mib=61,
+    part = call(
+        project_kernel, shape((text_rows, wide), BF16), text_states, key_weight, value_weight, far=3, mib=53.5,
         scratch=[
             pltpu.VMEM(text_states.shape, BF16), pltpu.VMEM((DT, wide), BF16),
             pltpu.SemaphoreType.DMA((2, CHUNKS)), pltpu.SemaphoreType.DMA,
         ],
     )
+    packed = call(pack_kernel, shape((groups, text_rows, wide + DT // groups), BF16), text_states, part)
     own = exchange(packed, YZ)
     other = swap(own)
     like = shape(video_query.shape, BF16)

time: 106 us -> 106 us (level)
    unnamed x10 -> x12, local copies, waits for them, and re-layouts: 3.7 us -> 4.6 us
    pallas_call x7 -> x8, Pallas kernels: 12.8 us -> 12.1 us  [call(): pl.pallas_call(kernel, out_shape=out, in_specs=specs, out_specs=out_spec...]
where the time goes in v10:
time: 106 us; the launch traced here: 105 us
  blocking collectives  61.7 us (58%)
  starting transfers between devices  13.8 us (13%)
  waiting for transfers between devices  12.5 us (12%)
  Pallas kernels  12.1 us (11%)
  local copies, waits for them, and re-layouts  4.6 us (4%)
    all_to_all x3, blocking collectives, exchange(): return lax.all_to_all(array, axes, 0, 0, tiled=True)  61.7 us
    pallas_call x8, Pallas kernels, call(): pl.pallas_call(kernel, out_shape=out, in_specs=specs, out_specs=out_spec...  12.1 us
    all_to_all x1, waiting for transfers between devices, exchange(): return lax.all_to_all(array, axes, 0, 0, tiled=True)  9.57 us
    all_to_all x1, starting transfers between devices, exchange(): return lax.all_to_all(array, axes, 0, 0, tiled=True)  7.89 us
    ppermute x3, starting transfers between devices, swap(): return lax.ppermute(array, 'core', [(0, 1), (1, 0)])  5.95 us
    unnamed x12, local copies, waits for them, and re-layouts  4.6 us
    ppermute x3, waiting for transfers between devices, swap(): return lax.ppermute(array, 'core', [(0, 1), (1, 0)])  2.89 us
  transfers between devices with their start and end apart: 4, of which 3 were waited for; matrix products, arithmetic and copies ran while one was open for 0% of the time, Pallas kernels for 2%

profile of v10, /device:TPU:1, one launch (start us, length us, event | category | flops | bytes accessed | tf_op | source)
XLA Modules:
  0.0 105.4 jit_solution(11136367194393461921)
XLA Ops:
  0.6 0.0 copy-start.4
  0.6 0.9 copy-done.4
  1.5 0.0 copy-start.2
  1.5 0.0 copy-start.5
  1.5 4.0 %shard_map.93.part_ref = bf16[16,768]{1,0:T(8,128)(2,1)S(1)} custom-call(bf16[2,8,4096]{2,1,0:T(8,128)(2,1)S(1)} %copy-done.4, bf16[4096,384]{1,0:T(8,128)(2,1)} %key_ref.1, bf16[4096,384]{1,0:T(8,128)(2,1)} %value_ref.1), custom_call_target="tpu_custom_call" | custom-call | tf_op jit(solution)/shard_map/pallas_call | solution.py:200
  5.6 26.8 %all_to_all.26.own_ref = bf16[16,16,1024]{2,1,0:T(8,128)(2,1)S(1)} all-to-all(bf16[16,16,1024]{2,1,0:T(8,128)(2,1)S(1)} %shard_map.94), channel_id=1, replica_groups=mesh['z'=8,'yh'=2,'core'=2,'yl'=2,'x'=4] {'yh','z'}, dimensions={0} | all-to-all | bytes 1048576 | tf_op jit(solution)/shard_map/all_to_all | solution.py:215
  32.5 2.8 %collective-permute-start = (bf16[16,16,1024]{2,1,0:T(8,128)(2,1)S(1)}, bf16[16,16,1024]{2,1,0:T(8,128)(2,1)S(1)}, u32[]{:S(2)}, u32[]{:S(2)}) collective-permute-start(bf16[16,16,1024]{2,1,0:T(8,128)(2,1)S(1)} %all_to_all.26.own_ref), channel_id=1, source_target_pairs={{0,8},{8,0},{1,9},{9,1},{2,10},{10,2},{3,11},{11,3},{4,12},{12,4},... | collective-permute-start | bytes 1572872 | tf_op jit(solution)/shard_map/ppermute | solution.py:211
  35.3 1.5 %collective-permute-done.other_ref = bf16[16,16,1024]{2,1,0:T(8,128)(2,1)S(1)} collective-permute-done((bf16[16,16,1024]{2,1,0:T(8,128)(2,1)S(1)}, bf16[16,16,1024]{2,1,0:T(8,128)(2,1)S(1)}, u32[]{:S(2)}, u32[]{:S(2)}) %collective-permute-start) | collective-permute-done | bytes 524320 | tf_op jit(solution)/shard_map/ppermute | solution.py:211
  36.8 0.0 copy-done.2
  36.8 0.0 copy-done.5
  36.8 0.0 copy-start.3
  36.8 1.1 %copy-done.3 = bf16[2,512,384]{2,1,0:T(8,128)(2,1)S(1)} copy-done((bf16[2,512,384]{2,1,0:T(8,128)(2,1)S(1)}, bf16[2,512,384]{2,1,0:T(8,128)(2,1)}, u32[]{:S(2)}) %copy-start.3) | copy-done | bytes 786456
  38.0 3.9 %shard_map.95 = (f32[16,32,384]{2,1,0:T(8,128)S(1)}, bf16[16,32,384]{2,1,0:T(8,128)(2,1)S(1)}, bf16[2,3,256,512]{3,2,1,0:T(8,128)(2,1)S(1)}, bf16[2,3,256,512]{3...) custom-call(s32[2]{0:T(128)S(1)} %copy-done.5, s32[1]{0:T(128)} %bitcast.core_ref, bf16[2,512,384]{2,1,0:T(8,128)(2,1)S(1)} %copy-done.2, ...), custom_call_target="tpu_custom_call" | custom-call | tf_op jit(solution)/shard_map/pallas_call | solution.py:200
  41.9 0.0 copy-start
  41.9 1.2 %copy-done = bf16[2,3,256,512]{3,2,1,0:T(8,128)(2,1)} copy-done((bf16[2,3,256,512]{3,2,1,0:T(8,128)(2,1)}, bf16[2,3,256,512]{3,2,1,0:T(8,128)(2,1)S(1)}, u32[]{:S(2)}) %copy-start) | copy-done | bytes 1572888
  43.1 0.4 collective-permute-start.1
  43.5 1.4 %collective-permute-done.1.other_ref = bf16[16,32,384]{2,1,0:T(8,128)(2,1)S(1)} collective-permute-done((bf16[16,32,384]{2,1,0:T(8,128)(2,1)S(1)}, bf16[16,32,384]{2,1,0:T(8,128)(2,1)S(1)}, u32[]{:S(2)}, u32[]{:S(2)}) %collective-permute-start.1) | collective-permute-done | bytes 393248 | tf_op jit(solution)/shard_map/ppermute | solution.py:211
  44.8 0.1 shard_map.97
  44.9 16.7 %all_to_all.27.parts_ref = bf16[16,32,384]{2,1,0:T(8,128)(2,1)S(1)} all-to-all(bf16[16,32,384]{2,1,0:T(8,128)(2,1)S(1)} %shard_map.97), channel_id=1, replica_groups=mesh['z'=8,'yh'=2,'core'=2,'yl'=2,'x'=4] {'yh','z'}, dimensions={0} | all-to-all | bytes 786432 | tf_op jit(solution)/shard_map/all_to_all | solution.py:215
  61.6 0.1 shard_map.98
  61.7 18.2 %all_to_all.28.total_ref = bf16[16,32,384]{2,1,0:T(8,128)(2,1)S(1)} all-to-all(bf16[16,32,384]{2,1,0:T(8,128)(2,1)S(1)} %shard_map.98), channel_id=1, replica_groups=mesh['z'=8,'yh'=2,'core'=2,'yl'=2,'x'=4] {'yh','z'}, dimensions={0} | all-to-all | bytes 786432 | tf_op jit(solution)/shard_map/all_to_all | solution.py:215
  79.9 1.1 %shard_map.99 = (f32[128,384]{1,0:T(8,128)S(1)}, f32[128,384]{1,0:T(8,128)S(1)}, f32[256,1]{1,0:T(8,128)}) custom-call(s32[1]{0:T(128)} %bitcast.core_ref, bf16[2,16,16,256]{3,2,1,0:T(8,128)(2,1)S(1)} %get-tuple-element.20.columns_ref, bf16[16,32,384]{2,1,0:T(8,128)(2,1)S(1)} %all_to_all.28.total_ref), custom_call_target="tpu_custom_call" | custom-call | tf_op jit(solution)/shard_map/pallas_call | solution.py:200
  81.0 2.7 %collective-permute-start.2 = (f32[128,384]{1,0:T(8,128)S(1)}, f32[128,384]{1,0:T(8,128)S(1)}, u32[]{:S(2)}, u32[]{:S(2)}) collective-permute-start(f32[128,384]{1,0:T(8,128)S(1)} %get-tuple-element.24), channel_id=1, source_target_pairs={{0,8},{8,0},{1,9},{9,1},{2,10},{10,2},{3,11},{11,3},{4,12},{12,4},... | collective-permute-start | bytes 589832 | tf_op jit(solution)/shard_map/ppermute | solution.py:211
  83.8 7.9 %all-to-all-start.3 = ((f32[256,1,1]{2,1,0:T(1,128)}), f32[256,1,1]{2,1,0:T(1,128)S(1)}, u32[]{:S(2)}, u32[]{:S(2)}) async-start(f32[256,1,1]{2,1,0:T(1,128)} %bitcast.1), calls=%async_computation.3 | async-start | bytes 262144 | tf_op jit(solution)/shard_map/all_to_all | solution.py:215
  91.7 0.0 copy-start.1
  91.7 1.4 %copy-done.1 = bf16[2,3,256,512]{3,2,1,0:T(8,128)(2,1)S(1)} copy-done((bf16[2,3,256,512]{3,2,1,0:T(8,128)(2,1)S(1)}, bf16[2,3,256,512]{3,2,1,0:T(8,128)(2,1)}, u32[]{:S(2)}) %copy-start.1) | copy-done | bytes 1572888
  93.1 1.9 %shard_map.96 = (bf16[2,512,384]{2,1,0:T(8,128)(2,1)}, bf16[2,512,384]{2,1,0:T(8,128)(2,1)}) custom-call(s32[1]{0:T(128)} %bitcast.core_ref, bf16[16,16,1024]{2,1,0:T(8,128)(2,1)S(1)} %all_to_all.26.own_ref, bf16[16,16,1024]{2,1,0:T(8,128)(2,1)S(1)} %collective-permute-done.other_ref, bf16[2,3,256,512]{3,2,1,0:T(8,128)(2,1)S(1)} %get-tuple-element.16.probs_ref, ...), custom_call_target="tpu_custom_call" | custom-call | tf_op jit(solution)/shard_map/pallas_call | solution.py:200
  94.9 9.6 %all-to-all-done.3 = f32[256,1,1]{2,1,0:T(1,128)S(1)} async-done(((f32[256,1,1]{2,1,0:T(1,128)}), f32[256,1,1]{2,1,0:T(1,128)S(1)}, u32[]{:S(2)}, u32[]{:S(2)}) %all-to-all-start.3) | async-done | bytes 1056 | tf_op jit(solution)/shard_map/all_to_all | solution.py:215
  104.5 0.0 collective-permute-done.2.other_ref
  104.5 0.9 shard_map.100
  (1 shorter events, 0.0 us)
Async XLA Ops:
  0.6 0.9 copy-start.4
  1.5 35.3 %copy-start.2 = (bf16[2,512,384]{2,1,0:T(8,128)(2,1)S(1)}, bf16[2,512,384]{2,1,0:T(8,128)(2,1)}, u32[]{:S(2)}) copy-start(bf16[2,512,384]{2,1,0:T(8,128)(2,1)} %query_ref.1) | copy-start | bytes 2359300
  1.5 35.3 %copy-start.5 = (s32[2]{0:T(128)S(1)}, s32[2]{0:T(128)}, u32[]{:S(2)}) copy-start(s32[2]{0:T(128)} %lengths_ref.1) | copy-start | bytes 28
  32.5 4.4 %collective-permute-start = (bf16[16,16,1024]{2,1,0:T(8,128)(2,1)S(1)}, bf16[16,16,1024]{2,1,0:T(8,128)(2,1)S(1)}, u32[]{:S(2)}, u32[]{:S(2)}) collective-permute-start(bf16[16,16,1024]{2,1,0:T(8,128)(2,1)S(1)} %all_to_all.26.own_ref), channel_id=1, source_target_pairs={{0,8},{8,0},{1,9},{9,1},{2,10},{10,2},{3,11},{11,3},{4,12},{12,4},... | collective-permute-start | bytes 1572872 | tf_op jit(solution)/shard_map/ppermute | solution.py:211
  36.8 1.1 %copy-start.3 = (bf16[2,512,384]{2,1,0:T(8,128)(2,1)S(1)}, bf16[2,512,384]{2,1,0:T(8,128)(2,1)}, u32[]{:S(2)}) copy-start(bf16[2,512,384]{2,1,0:T(8,128)(2,1)} %grad_ref.1) | copy-start | bytes 2359300
  41.9 1.2 %copy-start = (bf16[2,3,256,512]{3,2,1,0:T(8,128)(2,1)}, bf16[2,3,256,512]{3,2,1,0:T(8,128)(2,1)S(1)}, u32[]{:S(2)}) copy-start(bf16[2,3,256,512]{3,2,1,0:T(8,128)(2,1)S(1)} %get-tuple-element.17.dscore_ref) | copy-start | bytes 4718596
  43.1 1.7 %collective-permute-start.1 = (bf16[16,32,384]{2,1,0:T(8,128)(2,1)S(1)}, bf16[16,32,384]{2,1,0:T(8,128)(2,1)S(1)}, u32[]{:S(2)}, u32[]{:S(2)}) collective-permute-start(bf16[16,32,384]{2,1,0:T(8,128)(2,1)S(1)} %get-tuple-element.22), channel_id=1, source_target_pairs={{0,8},{8,0},{1,9},{9,1},{2,10},{10,2},{3,11},{11,3},{4,12},{12,4},... | collective-permute-start | bytes 1179656 | tf_op jit(solution)/shard_map/ppermute | solution.py:211
  81.0 23.5 %collective-permute-start.2 = (f32[128,384]{1,0:T(8,128)S(1)}, f32[128,384]{1,0:T(8,128)S(1)}, u32[]{:S(2)}, u32[]{:S(2)}) collective-permute-start(f32[128,384]{1,0:T(8,128)S(1)} %get-tuple-element.24), channel_id=1, source_target_pairs={{0,8},{8,0},{1,9},{9,1},{2,10},{10,2},{3,11},{11,3},{4,12},{12,4},... | collective-permute-start | bytes 589832 | tf_op jit(solution)/shard_map/ppermute | solution.py:211
  83.8 20.7 %all-to-all-start.3 = ((f32[256,1,1]{2,1,0:T(1,128)}), f32[256,1,1]{2,1,0:T(1,128)S(1)}, u32[]{:S(2)}, u32[]{:S(2)}) async-start(f32[256,1,1]{2,1,0:T(1,128)} %bitcast.1), calls=%async_computation.3 | async-start | bytes 262144 | tf_op jit(solution)/shard_map/all_to_all | solution.py:215
  91.7 1.4 %copy-start.1 = (bf16[2,3,256,512]{3,2,1,0:T(8,128)(2,1)S(1)}, bf16[2,3,256,512]{3,2,1,0:T(8,128)(2,1)}, u32[]{:S(2)}) copy-start(bf16[2,3,256,512]{3,2,1,0:T(8,128)(2,1)} %copy-done) | copy-start | bytes 4718596

commit v11 on v9

--- a/solution.py
+++ b/solution.py
@@ -86,12 +86,12 @@
         return dot(key, query_ref[b, :, cols], 1, 1), dot(value, grad_ref[b, :, cols], 1, 1)
 
     def weigh(b, h, scores, dprob):
-        scores = jnp.where(token < lengths_ref[b], scores * SCALING, -1e30)
-        weights = jnp.exp(scores - jnp.max(scores, axis=0, keepdims=True))
+        scores = jnp.where(token < lengths_ref[b], scores, -1e30)
+        weights = jnp.exp2((scores - jnp.max(scores, axis=0, keepdims=True)) * (SCALING * math.log2(math.e)))
         probs = weights * (1.0 / jnp.sum(weights, axis=0, keepdims=True))
         probs_low = probs.astype(BF16)
         delta = jnp.sum(probs * dprob, axis=0, keepdims=True)
-        dscore = (probs * (dprob - delta) * SCALING).astype(BF16)
+        dscore = ((probs * SCALING) * (dprob - delta)).astype(BF16)
         probs_ref[b, h] = probs_low
         dscore_ref[b, h] = dscore
         return b, h, probs_low, dscore

time: 106 us -> 106 us (level)
  no operation moved by 1% of the time
where the time goes in v11:
time: 106 us; the launch traced here: 105 us
  blocking collectives  61.9 us (58%)
  starting transfers between devices  13.8 us (13%)
  Pallas kernels  12.6 us (12%)
  waiting for transfers between devices  12.5 us (12%)
  local copies, waits for them, and re-layouts  3.7 us (3%)
    all_to_all x3, blocking collectives, exchange(): return lax.all_to_all(array, axes, 0, 0, tiled=True)  61.9 us
    pallas_call x7, Pallas kernels, call(): pl.pallas_call(kernel, out_shape=out, in_specs=specs, out_specs=out_spec...  12.6 us
    all_to_all x1, waiting for transfers between devices, exchange(): return lax.all_to_all(array, axes, 0, 0, tiled=True)  9.57 us
    all_to_all x1, starting transfers between devices, exchange(): return lax.all_to_all(array, axes, 0, 0, tiled=True)  7.9 us
    ppermute x3, starting transfers between devices, swap(): return lax.ppermute(array, 'core', [(0, 1), (1, 0)])  5.94 us
    unnamed x10, local copies, waits for them, and re-layouts  3.7 us
    ppermute x3, waiting for transfers between devices, swap(): return lax.ppermute(array, 'core', [(0, 1), (1, 0)])  2.89 us
  transfers between devices with their start and end apart: 4, of which 3 were waited for; matrix products, arithmetic and copies ran while one was open for 0% of the time, Pallas kernels for 2%

profile of v11, /device:TPU:1, one launch (start us, length us, event | category | flops | bytes accessed | tf_op | source)
XLA Modules:
  0.0 105.2 jit_solution(12888242313025737979)
XLA Ops:
  0.6 0.0 copy-start.4
  0.6 0.0 copy-start.2
  0.7 4.7 %shard_map.93 = bf16[16,16,1024]{2,1,0:T(8,128)(2,1)} custom-call(bf16[2,8,4096]{2,1,0:T(8,128)(2,1)} %text_ref.1, bf16[4096,384]{1,0:T(8,128)(2,1)} %key_ref.1, bf16[4096,384]{1,0:T(8,128)(2,1)} %value_ref.1), custom_call_target="tpu_custom_call" | custom-call | tf_op jit(solution)/shard_map/pallas_call | solution.py:195
  5.4 27.0 %all_to_all.26.own_ref = bf16[16,16,1024]{2,1,0:T(8,128)(2,1)S(1)} all-to-all(bf16[16,16,1024]{2,1,0:T(8,128)(2,1)} %shard_map.93), channel_id=1, replica_groups=mesh['z'=8,'yh'=2,'core'=2,'yl'=2,'x'=4] {'yh','z'}, dimensions={0} | all-to-all | bytes 1048576 | tf_op jit(solution)/shard_map/all_to_all | solution.py:210
  32.4 2.8 %collective-permute-start = (bf16[16,16,1024]{2,1,0:T(8,128)(2,1)S(1)}, bf16[16,16,1024]{2,1,0:T(8,128)(2,1)S(1)}, u32[]{:S(2)}, u32[]{:S(2)}) collective-permute-start(bf16[16,16,1024]{2,1,0:T(8,128)(2,1)S(1)} %all_to_all.26.own_ref), channel_id=1, source_target_pairs={{0,8},{8,0},{1,9},{9,1},{2,10},{10,2},{3,11},{11,3},{4,12},{12,4},... | collective-permute-start | bytes 1572872 | tf_op jit(solution)/shard_map/ppermute | solution.py:206
  35.3 1.5 %collective-permute-done.other_ref = bf16[16,16,1024]{2,1,0:T(8,128)(2,1)S(1)} collective-permute-done((bf16[16,16,1024]{2,1,0:T(8,128)(2,1)S(1)}, bf16[16,16,1024]{2,1,0:T(8,128)(2,1)S(1)}, u32[]{:S(2)}, u32[]{:S(2)}) %collective-permute-start) | collective-permute-done | bytes 524320 | tf_op jit(solution)/shard_map/ppermute | solution.py:206
  36.8 0.0 copy-done.4
  36.8 0.0 copy-done.2
  36.8 0.0 copy-start.3
  36.8 1.1 %copy-done.3 = bf16[2,512,384]{2,1,0:T(8,128)(2,1)S(1)} copy-done((bf16[2,512,384]{2,1,0:T(8,128)(2,1)S(1)}, bf16[2,512,384]{2,1,0:T(8,128)(2,1)}, u32[]{:S(2)}) %copy-start.3) | copy-done | bytes 786456
  37.9 3.8 %shard_map.94 = (f32[16,32,384]{2,1,0:T(8,128)S(1)}, bf16[16,32,384]{2,1,0:T(8,128)(2,1)S(1)}, bf16[2,3,256,512]{3,2,1,0:T(8,128)(2,1)S(1)}, bf16[2,3,256,512]{3...) custom-call(s32[2]{0:T(128)S(1)} %copy-done.4, s32[1]{0:T(128)} %bitcast.core_ref, bf16[2,512,384]{2,1,0:T(8,128)(2,1)S(1)} %copy-done.2, ...), custom_call_target="tpu_custom_call" | custom-call | tf_op jit(solution)/shard_map/pallas_call | solution.py:195
  41.7 0.0 copy-start
  41.7 1.2 %copy-done = bf16[2,3,256,512]{3,2,1,0:T(8,128)(2,1)} copy-done((bf16[2,3,256,512]{3,2,1,0:T(8,128)(2,1)}, bf16[2,3,256,512]{3,2,1,0:T(8,128)(2,1)S(1)}, u32[]{:S(2)}) %copy-start) | copy-done | bytes 1572888
  42.9 0.4 collective-permute-start.1
  43.2 1.4 %collective-permute-done.1.other_ref = bf16[16,32,384]{2,1,0:T(8,128)(2,1)S(1)} collective-permute-done((bf16[16,32,384]{2,1,0:T(8,128)(2,1)S(1)}, bf16[16,32,384]{2,1,0:T(8,128)(2,1)S(1)}, u32[]{:S(2)}, u32[]{:S(2)}) %collective-permute-start.1) | collective-permute-done | bytes 393248 | tf_op jit(solution)/shard_map/ppermute | solution.py:206
  44.6 0.1 shard_map.96
  44.7 16.7 %all_to_all.27.parts_ref = bf16[16,32,384]{2,1,0:T(8,128)(2,1)S(1)} all-to-all(bf16[16,32,384]{2,1,0:T(8,128)(2,1)S(1)} %shard_map.96), channel_id=1, replica_groups=mesh['z'=8,'yh'=2,'core'=2,'yl'=2,'x'=4] {'yh','z'}, dimensions={0} | all-to-all | bytes 786432 | tf_op jit(solution)/shard_map/all_to_all | solution.py:210
  61.4 0.1 shard_map.97
  61.5 18.2 %all_to_all.28.total_ref = bf16[16,32,384]{2,1,0:T(8,128)(2,1)S(1)} all-to-all(bf16[16,32,384]{2,1,0:T(8,128)(2,1)S(1)} %shard_map.97), channel_id=1, replica_groups=mesh['z'=8,'yh'=2,'core'=2,'yl'=2,'x'=4] {'yh','z'}, dimensions={0} | all-to-all | bytes 786432 | tf_op jit(solution)/shard_map/all_to_all | solution.py:210
  79.7 1.1 %shard_map.98 = (f32[128,384]{1,0:T(8,128)S(1)}, f32[128,384]{1,0:T(8,128)S(1)}, f32[256,1]{1,0:T(8,128)}) custom-call(s32[1]{0:T(128)} %bitcast.core_ref, bf16[2,16,16,256]{3,2,1,0:T(8,128)(2,1)S(1)} %get-tuple-element.20.columns_ref, bf16[16,32,384]{2,1,0:T(8,128)(2,1)S(1)} %all_to_all.28.total_ref), custom_call_target="tpu_custom_call" | custom-call | tf_op jit(solution)/shard_map/pallas_call | solution.py:195
  80.8 2.7 %collective-permute-start.2 = (f32[128,384]{1,0:T(8,128)S(1)}, f32[128,384]{1,0:T(8,128)S(1)}, u32[]{:S(2)}, u32[]{:S(2)}) collective-permute-start(f32[128,384]{1,0:T(8,128)S(1)} %get-tuple-element.24), channel_id=1, source_target_pairs={{0,8},{8,0},{1,9},{9,1},{2,10},{10,2},{3,11},{11,3},{4,12},{12,4},... | collective-permute-start | bytes 589832 | tf_op jit(solution)/shard_map/ppermute | solution.py:206
  83.5 7.9 %all-to-all-start.3 = ((f32[256,1,1]{2,1,0:T(1,128)}), f32[256,1,1]{2,1,0:T(1,128)S(1)}, u32[]{:S(2)}, u32[]{:S(2)}) async-start(f32[256,1,1]{2,1,0:T(1,128)} %bitcast.1), calls=%async_computation.3 | async-start | bytes 262144 | tf_op jit(solution)/shard_map/all_to_all | solution.py:210
  91.4 0.0 copy-start.1
  91.4 1.4 %copy-done.1 = bf16[2,3,256,512]{3,2,1,0:T(8,128)(2,1)S(1)} copy-done((bf16[2,3,256,512]{3,2,1,0:T(8,128)(2,1)S(1)}, bf16[2,3,256,512]{3,2,1,0:T(8,128)(2,1)}, u32[]{:S(2)}) %copy-start.1) | copy-done | bytes 1572888
  92.8 1.8 %shard_map.95 = (bf16[2,512,384]{2,1,0:T(8,128)(2,1)}, bf16[2,512,384]{2,1,0:T(8,128)(2,1)}) custom-call(s32[1]{0:T(128)} %bitcast.core_ref, bf16[16,16,1024]{2,1,0:T(8,128)(2,1)S(1)} %all_to_all.26.own_ref, bf16[16,16,1024]{2,1,0:T(8,128)(2,1)S(1)} %collective-permute-done.other_ref, bf16[2,3,256,512]{3,2,1,0:T(8,128)(2,1)S(1)} %get-tuple-element.16.probs_ref, ...), custom_call_target="tpu_custom_call" | custom-call | tf_op jit(solution)/shard_map/pallas_call | solution.py:195
  94.7 9.6 %all-to-all-done.3 = f32[256,1,1]{2,1,0:T(1,128)S(1)} async-done(((f32[256,1,1]{2,1,0:T(1,128)}), f32[256,1,1]{2,1,0:T(1,128)S(1)}, u32[]{:S(2)}, u32[]{:S(2)}) %all-to-all-start.3) | async-done | bytes 1056 | tf_op jit(solution)/shard_map/all_to_all | solution.py:210
  104.3 0.0 collective-permute-done.2.other_ref
  104.3 0.9 shard_map.99
Async XLA Ops:
  0.6 36.2 %copy-start.4 = (s32[2]{0:T(128)S(1)}, s32[2]{0:T(128)}, u32[]{:S(2)}) copy-start(s32[2]{0:T(128)} %lengths_ref.1) | copy-start | bytes 28
  0.6 36.2 %copy-start.2 = (bf16[2,512,384]{2,1,0:T(8,128)(2,1)S(1)}, bf16[2,512,384]{2,1,0:T(8,128)(2,1)}, u32[]{:S(2)}) copy-start(bf16[2,512,384]{2,1,0:T(8,128)(2,1)} %query_ref.1) | copy-start | bytes 2359300
  32.4 4.4 %collective-permute-start = (bf16[16,16,1024]{2,1,0:T(8,128)(2,1)S(1)}, bf16[16,16,1024]{2,1,0:T(8,128)(2,1)S(1)}, u32[]{:S(2)}, u32[]{:S(2)}) collective-permute-start(bf16[16,16,1024]{2,1,0:T(8,128)(2,1)S(1)} %all_to_all.26.own_ref), channel_id=1, source_target_pairs={{0,8},{8,0},{1,9},{9,1},{2,10},{10,2},{3,11},{11,3},{4,12},{12,4},... | collective-permute-start | bytes 1572872 | tf_op jit(solution)/shard_map/ppermute | solution.py:206
  36.8 1.1 %copy-start.3 = (bf16[2,512,384]{2,1,0:T(8,128)(2,1)S(1)}, bf16[2,512,384]{2,1,0:T(8,128)(2,1)}, u32[]{:S(2)}) copy-start(bf16[2,512,384]{2,1,0:T(8,128)(2,1)} %grad_ref.1) | copy-start | bytes 2359300
  41.7 1.2 %copy-start = (bf16[2,3,256,512]{3,2,1,0:T(8,128)(2,1)}, bf16[2,3,256,512]{3,2,1,0:T(8,128)(2,1)S(1)}, u32[]{:S(2)}) copy-start(bf16[2,3,256,512]{3,2,1,0:T(8,128)(2,1)S(1)} %get-tuple-element.17.dscore_ref) | copy-start | bytes 4718596
  42.9 1.7 %collective-permute-start.1 = (bf16[16,32,384]{2,1,0:T(8,128)(2,1)S(1)}, bf16[16,32,384]{2,1,0:T(8,128)(2,1)S(1)}, u32[]{:S(2)}, u32[]{:S(2)}) collective-permute-start(bf16[16,32,384]{2,1,0:T(8,128)(2,1)S(1)} %get-tuple-element.22), channel_id=1, source_target_pairs={{0,8},{8,0},{1,9},{9,1},{2,10},{10,2},{3,11},{11,3},{4,12},{12,4},... | collective-permute-start | bytes 1179656 | tf_op jit(solution)/shard_map/ppermute | solution.py:206
  80.8 23.5 %collective-permute-start.2 = (f32[128,384]{1,0:T(8,128)S(1)}, f32[128,384]{1,0:T(8,128)S(1)}, u32[]{:S(2)}, u32[]{:S(2)}) collective-permute-start(f32[128,384]{1,0:T(8,128)S(1)} %get-tuple-element.24), channel_id=1, source_target_pairs={{0,8},{8,0},{1,9},{9,1},{2,10},{10,2},{3,11},{11,3},{4,12},{12,4},... | collective-permute-start | bytes 589832 | tf_op jit(solution)/shard_map/ppermute | solution.py:206
  83.5 20.7 %all-to-all-start.3 = ((f32[256,1,1]{2,1,0:T(1,128)}), f32[256,1,1]{2,1,0:T(1,128)S(1)}, u32[]{:S(2)}, u32[]{:S(2)}) async-start(f32[256,1,1]{2,1,0:T(1,128)} %bitcast.1), calls=%async_computation.3 | async-start | bytes 262144 | tf_op jit(solution)/shard_map/all_to_all | solution.py:210
  91.4 1.4 %copy-start.1 = (bf16[2,3,256,512]{3,2,1,0:T(8,128)(2,1)S(1)}, bf16[2,3,256,512]{3,2,1,0:T(8,128)(2,1)}, u32[]{:S(2)}) copy-start(bf16[2,3,256,512]{3,2,1,0:T(8,128)(2,1)} %copy-done) | copy-start | bytes 4718596

commit v12 on v11

--- a/solution.py
+++ b/solution.py
@@ -12,11 +12,12 @@
 DT = 4096
 HEADS = 24
 HEAD = 128
-CHUNKS = 2
+CHUNKS = 1
 YZ = ("yh", "z")
 SEQ = ("z", "yh", "core")
 TP = ("yl", "x")
 ALL = SEQ + TP
+PEERS = ("core", "x", "yl", "yh", "z")
 SCALING = 1.0 / math.sqrt(HEAD)
 BF16 = jnp.bfloat16
 F32 = jnp.float32
@@ -244,7 +245,7 @@
     own_raw, other_raw, squares = call(
         weight_kernel, [weight, weight, shape((every, 1), F32)], core, columns, totals, scalars=1,
     )
-    squares = exchange(squares, ALL)
+    squares = exchange(squares, PEERS)
     key_weight_grad, value_weight_grad = call(
         scale_kernel, [weight, weight], core, own_raw, swap(other_raw), squares, scalars=1,
     )

time: 106 us -> 106 us (level)
  no operation moved by 1% of the time
where the time goes in v12:
time: 106 us; the launch traced here: 105 us
  blocking collectives  61.9 us (58%)
  starting transfers between devices  13.8 us (13%)
  Pallas kernels  12.5 us (12%)
  waiting for transfers between devices  12.5 us (12%)
  local copies, waits for them, and re-layouts  3.7 us (3%)
    all_to_all x3, blocking collectives, exchange(): return lax.all_to_all(array, axes, 0, 0, tiled=True)  61.9 us
    pallas_call x7, Pallas kernels, call(): pl.pallas_call(kernel, out_shape=out, in_specs=specs, out_specs=out_spec...  12.5 us
    all_to_all x1, waiting for transfers between devices, exchange(): return lax.all_to_all(array, axes, 0, 0, tiled=True)  9.59 us
    all_to_all x1, starting transfers between devices, exchange(): return lax.all_to_all(array, axes, 0, 0, tiled=True)  7.9 us
    ppermute x3, starting transfers between devices, swap(): return lax.ppermute(array, 'core', [(0, 1), (1, 0)])  5.94 us
    unnamed x10, local copies, waits for them, and re-layouts  3.7 us
    ppermute x3, waiting for transfers between devices, swap(): return lax.ppermute(array, 'core', [(0, 1), (1, 0)])  2.89 us
  transfers between devices with their start and end apart: 4, of which 3 were waited for; matrix products, arithmetic and copies ran while one was open for 0% of the time, Pallas kernels for 2%

profile of v12, /device:TPU:1, one launch (start us, length us, event | category | flops | bytes accessed | tf_op | source)
XLA Modules:
  0.0 105.2 jit_solution(3574714174056953469)
XLA Ops:
  0.6 0.0 copy-start.4
  0.6 0.0 copy-start.2
  0.7 4.7 %shard_map.93 = bf16[16,16,1024]{2,1,0:T(8,128)(2,1)} custom-call(bf16[2,8,4096]{2,1,0:T(8,128)(2,1)} %text_ref.1, bf16[4096,384]{1,0:T(8,128)(2,1)} %key_ref.1, bf16[4096,384]{1,0:T(8,128)(2,1)} %value_ref.1), custom_call_target="tpu_custom_call" | custom-call | tf_op jit(solution)/shard_map/pallas_call | solution.py:196
  5.4 27.0 %all_to_all.26.own_ref = bf16[16,16,1024]{2,1,0:T(8,128)(2,1)S(1)} all-to-all(bf16[16,16,1024]{2,1,0:T(8,128)(2,1)} %shard_map.93), channel_id=1, replica_groups=mesh['z'=8,'yh'=2,'core'=2,'yl'=2,'x'=4] {'yh','z'}, dimensions={0} | all-to-all | bytes 1048576 | tf_op jit(solution)/shard_map/all_to_all | solution.py:211
  32.4 2.8 %collective-permute-start = (bf16[16,16,1024]{2,1,0:T(8,128)(2,1)S(1)}, bf16[16,16,1024]{2,1,0:T(8,128)(2,1)S(1)}, u32[]{:S(2)}, u32[]{:S(2)}) collective-permute-start(bf16[16,16,1024]{2,1,0:T(8,128)(2,1)S(1)} %all_to_all.26.own_ref), channel_id=1, source_target_pairs={{0,8},{8,0},{1,9},{9,1},{2,10},{10,2},{3,11},{11,3},{4,12},{12,4},... | collective-permute-start | bytes 1572872 | tf_op jit(solution)/shard_map/ppermute | solution.py:207
  35.3 1.5 %collective-permute-done.other_ref = bf16[16,16,1024]{2,1,0:T(8,128)(2,1)S(1)} collective-permute-done((bf16[16,16,1024]{2,1,0:T(8,128)(2,1)S(1)}, bf16[16,16,1024]{2,1,0:T(8,128)(2,1)S(1)}, u32[]{:S(2)}, u32[]{:S(2)}) %collective-permute-start) | collective-permute-done | bytes 524320 | tf_op jit(solution)/shard_map/ppermute | solution.py:207
  36.8 0.0 copy-done.4
  36.8 0.0 copy-done.2
  36.8 0.0 copy-start.3
  36.8 1.1 %copy-done.3 = bf16[2,512,384]{2,1,0:T(8,128)(2,1)S(1)} copy-done((bf16[2,512,384]{2,1,0:T(8,128)(2,1)S(1)}, bf16[2,512,384]{2,1,0:T(8,128)(2,1)}, u32[]{:S(2)}) %copy-start.3) | copy-done | bytes 786456
  37.9 3.8 %shard_map.94 = (f32[16,32,384]{2,1,0:T(8,128)S(1)}, bf16[16,32,384]{2,1,0:T(8,128)(2,1)S(1)}, bf16[2,3,256,512]{3,2,1,0:T(8,128)(2,1)S(1)}, bf16[2,3,256,512]{3...) custom-call(s32[2]{0:T(128)S(1)} %copy-done.4, s32[1]{0:T(128)} %bitcast.core_ref, bf16[2,512,384]{2,1,0:T(8,128)(2,1)S(1)} %copy-done.2, ...), custom_call_target="tpu_custom_call" | custom-call | tf_op jit(solution)/shard_map/pallas_call | solution.py:196
  41.7 0.0 copy-start
  41.7 1.2 %copy-done = bf16[2,3,256,512]{3,2,1,0:T(8,128)(2,1)} copy-done((bf16[2,3,256,512]{3,2,1,0:T(8,128)(2,1)}, bf16[2,3,256,512]{3,2,1,0:T(8,128)(2,1)S(1)}, u32[]{:S(2)}) %copy-start) | copy-done | bytes 1572888
  42.9 0.4 collective-permute-start.1
  43.2 1.4 %collective-permute-done.1.other_ref = bf16[16,32,384]{2,1,0:T(8,128)(2,1)S(1)} collective-permute-done((bf16[16,32,384]{2,1,0:T(8,128)(2,1)S(1)}, bf16[16,32,384]{2,1,0:T(8,128)(2,1)S(1)}, u32[]{:S(2)}, u32[]{:S(2)}) %collective-permute-start.1) | collective-permute-done | bytes 393248 | tf_op jit(solution)/shard_map/ppermute | solution.py:207
  44.6 0.1 shard_map.96
  44.7 16.7 %all_to_all.27.parts_ref = bf16[16,32,384]{2,1,0:T(8,128)(2,1)S(1)} all-to-all(bf16[16,32,384]{2,1,0:T(8,128)(2,1)S(1)} %shard_map.96), channel_id=1, replica_groups=mesh['z'=8,'yh'=2,'core'=2,'yl'=2,'x'=4] {'yh','z'}, dimensions={0} | all-to-all | bytes 786432 | tf_op jit(solution)/shard_map/all_to_all | solution.py:211
  61.4 0.1 shard_map.97
  61.5 18.2 %all_to_all.28.total_ref = bf16[16,32,384]{2,1,0:T(8,128)(2,1)S(1)} all-to-all(bf16[16,32,384]{2,1,0:T(8,128)(2,1)S(1)} %shard_map.97), channel_id=1, replica_groups=mesh['z'=8,'yh'=2,'core'=2,'yl'=2,'x'=4] {'yh','z'}, dimensions={0} | all-to-all | bytes 786432 | tf_op jit(solution)/shard_map/all_to_all | solution.py:211
  79.7 1.1 %shard_map.98 = (f32[128,384]{1,0:T(8,128)S(1)}, f32[128,384]{1,0:T(8,128)S(1)}, f32[256,1]{1,0:T(8,128)}) custom-call(s32[1]{0:T(128)} %bitcast.core_ref, bf16[2,16,16,256]{3,2,1,0:T(8,128)(2,1)S(1)} %get-tuple-element.20.columns_ref, bf16[16,32,384]{2,1,0:T(8,128)(2,1)S(1)} %all_to_all.28.total_ref), custom_call_target="tpu_custom_call" | custom-call | tf_op jit(solution)/shard_map/pallas_call | solution.py:196
  80.8 2.7 %collective-permute-start.2 = (f32[128,384]{1,0:T(8,128)S(1)}, f32[128,384]{1,0:T(8,128)S(1)}, u32[]{:S(2)}, u32[]{:S(2)}) collective-permute-start(f32[128,384]{1,0:T(8,128)S(1)} %get-tuple-element.24), channel_id=1, source_target_pairs={{0,8},{8,0},{1,9},{9,1},{2,10},{10,2},{3,11},{11,3},{4,12},{12,4},... | collective-permute-start | bytes 589832 | tf_op jit(solution)/shard_map/ppermute | solution.py:207
  83.5 7.9 %all-to-all-start.3 = ((f32[256,1,1]{2,1,0:T(1,128)}), f32[256,1,1]{2,1,0:T(1,128)S(1)}, u32[]{:S(2)}, u32[]{:S(2)}) async-start(f32[256,1,1]{2,1,0:T(1,128)} %bitcast.1), calls=%async_computation.3 | async-start | bytes 262144 | tf_op jit(solution)/shard_map/all_to_all | solution.py:211
  91.4 0.0 copy-start.1
  91.4 1.4 %copy-done.1 = bf16[2,3,256,512]{3,2,1,0:T(8,128)(2,1)S(1)} copy-done((bf16[2,3,256,512]{3,2,1,0:T(8,128)(2,1)S(1)}, bf16[2,3,256,512]{3,2,1,0:T(8,128)(2,1)}, u32[]{:S(2)}) %copy-start.1) | copy-done | bytes 1572888
  92.8 1.8 %shard_map.95 = (bf16[2,512,384]{2,1,0:T(8,128)(2,1)}, bf16[2,512,384]{2,1,0:T(8,128)(2,1)}) custom-call(s32[1]{0:T(128)} %bitcast.core_ref, bf16[16,16,1024]{2,1,0:T(8,128)(2,1)S(1)} %all_to_all.26.own_ref, bf16[16,16,1024]{2,1,0:T(8,128)(2,1)S(1)} %collective-permute-done.other_ref, bf16[2,3,256,512]{3,2,1,0:T(8,128)(2,1)S(1)} %get-tuple-element.16.probs_ref, ...), custom_call_target="tpu_custom_call" | custom-call | tf_op jit(solution)/shard_map/pallas_call | solution.py:196
  94.7 9.6 %all-to-all-done.3 = f32[256,1,1]{2,1,0:T(1,128)S(1)} async-done(((f32[256,1,1]{2,1,0:T(1,128)}), f32[256,1,1]{2,1,0:T(1,128)S(1)}, u32[]{:S(2)}, u32[]{:S(2)}) %all-to-all-start.3) | async-done | bytes 1056 | tf_op jit(solution)/shard_map/all_to_all | solution.py:211
  104.3 0.0 collective-permute-done.2.other_ref
  104.3 0.9 shard_map.99
Async XLA Ops:
  0.6 36.2 %copy-start.4 = (s32[2]{0:T(128)S(1)}, s32[2]{0:T(128)}, u32[]{:S(2)}) copy-start(s32[2]{0:T(128)} %lengths_ref.1) | copy-start | bytes 28
  0.6 36.2 %copy-start.2 = (bf16[2,512,384]{2,1,0:T(8,128)(2,1)S(1)}, bf16[2,512,384]{2,1,0:T(8,128)(2,1)}, u32[]{:S(2)}) copy-start(bf16[2,512,384]{2,1,0:T(8,128)(2,1)} %query_ref.1) | copy-start | bytes 2359300
  32.4 4.4 %collective-permute-start = (bf16[16,16,1024]{2,1,0:T(8,128)(2,1)S(1)}, bf16[16,16,1024]{2,1,0:T(8,128)(2,1)S(1)}, u32[]{:S(2)}, u32[]{:S(2)}) collective-permute-start(bf16[16,16,1024]{2,1,0:T(8,128)(2,1)S(1)} %all_to_all.26.own_ref), channel_id=1, source_target_pairs={{0,8},{8,0},{1,9},{9,1},{2,10},{10,2},{3,11},{11,3},{4,12},{12,4},... | collective-permute-start | bytes 1572872 | tf_op jit(solution)/shard_map/ppermute | solution.py:207
  36.8 1.1 %copy-start.3 = (bf16[2,512,384]{2,1,0:T(8,128)(2,1)S(1)}, bf16[2,512,384]{2,1,0:T(8,128)(2,1)}, u32[]{:S(2)}) copy-start(bf16[2,512,384]{2,1,0:T(8,128)(2,1)} %grad_ref.1) | copy-start | bytes 2359300
  41.7 1.2 %copy-start = (bf16[2,3,256,512]{3,2,1,0:T(8,128)(2,1)}, bf16[2,3,256,512]{3,2,1,0:T(8,128)(2,1)S(1)}, u32[]{:S(2)}) copy-start(bf16[2,3,256,512]{3,2,1,0:T(8,128)(2,1)S(1)} %get-tuple-element.17.dscore_ref) | copy-start | bytes 4718596
  42.9 1.7 %collective-permute-start.1 = (bf16[16,32,384]{2,1,0:T(8,128)(2,1)S(1)}, bf16[16,32,384]{2,1,0:T(8,128)(2,1)S(1)}, u32[]{:S(2)}, u32[]{:S(2)}) collective-permute-start(bf16[16,32,384]{2,1,0:T(8,128)(2,1)S(1)} %get-tuple-element.22), channel_id=1, source_target_pairs={{0,8},{8,0},{1,9},{9,1},{2,10},{10,2},{3,11},{11,3},{4,12},{12,4},... | collective-permute-start | bytes 1179656 | tf_op jit(solution)/shard_map/ppermute | solution.py:207
  80.8 23.5 %collective-permute-start.2 = (f32[128,384]{1,0:T(8,128)S(1)}, f32[128,384]{1,0:T(8,128)S(1)}, u32[]{:S(2)}, u32[]{:S(2)}) collective-permute-start(f32[128,384]{1,0:T(8,128)S(1)} %get-tuple-element.24), channel_id=1, source_target_pairs={{0,8},{8,0},{1,9},{9,1},{2,10},{10,2},{3,11},{11,3},{4,12},{12,4},... | collective-permute-start | bytes 589832 | tf_op jit(solution)/shard_map/ppermute | solution.py:207
  83.5 20.8 %all-to-all-start.3 = ((f32[256,1,1]{2,1,0:T(1,128)}), f32[256,1,1]{2,1,0:T(1,128)S(1)}, u32[]{:S(2)}, u32[]{:S(2)}) async-start(f32[256,1,1]{2,1,0:T(1,128)} %bitcast.1), calls=%async_computation.3 | async-start | bytes 262144 | tf_op jit(solution)/shard_map/all_to_all | solution.py:211
  91.4 1.4 %copy-start.1 = (bf16[2,3,256,512]{3,2,1,0:T(8,128)(2,1)S(1)}, bf16[2,3,256,512]{3,2,1,0:T(8,128)(2,1)}, u32[]{:S(2)}) copy-start(bf16[2,3,256,512]{3,2,1,0:T(8,128)(2,1)} %copy-done) | copy-start | bytes 4718596

commit v13 on v11

--- a/solution.py
+++ b/solution.py
@@ -88,9 +88,10 @@
     def weigh(b, h, scores, dprob):
         scores = jnp.where(token < lengths_ref[b], scores, -1e30)
         weights = jnp.exp2((scores - jnp.max(scores, axis=0, keepdims=True)) * (SCALING * math.log2(math.e)))
-        probs = weights * (1.0 / jnp.sum(weights, axis=0, keepdims=True))
+        inverse = 1.0 / jnp.sum(weights, axis=0, keepdims=True)
+        probs = weights * inverse
         probs_low = probs.astype(BF16)
-        delta = jnp.sum(probs * dprob, axis=0, keepdims=True)
+        delta = jnp.sum(weights * dprob, axis=0, keepdims=True) * inverse
         dscore = ((probs * SCALING) * (dprob - delta)).astype(BF16)
         probs_ref[b, h] = probs_low
         dscore_ref[b, h] = dscore

time: 106 us -> 105 us (level)
  no operation moved by 1% of the time
where the time goes in v13:
time: 105 us
  blocking collectives  62 us (59%)
  starting transfers between devices  13.8 us (13%)
  Pallas kernels  12.5 us (12%)
  waiting for transfers between devices  12.5 us (12%)
  local copies, waits for them, and re-layouts  3.7 us (4%)
    all_to_all x3, blocking collectives, exchange(): return lax.all_to_all(array, axes, 0, 0, tiled=True)  62 us
    pallas_call x7, Pallas kernels, call(): pl.pallas_call(kernel, out_shape=out, in_specs=specs, out_specs=out_spec...  12.5 us
    all_to_all x1, waiting for transfers between devices, exchange(): return lax.all_to_all(array, axes, 0, 0, tiled=True)  9.57 us
    all_to_all x1, starting transfers between devices, exchange(): return lax.all_to_all(array, axes, 0, 0, tiled=True)  7.89 us
    ppermute x3, starting transfers between devices, swap(): return lax.ppermute(array, 'core', [(0, 1), (1, 0)])  5.95 us
    unnamed x10, local copies, waits for them, and re-layouts  3.7 us
    ppermute x3, waiting for transfers between devices, swap(): return lax.ppermute(array, 'core', [(0, 1), (1, 0)])  2.89 us
  transfers between devices with their start and end apart: 4, of which 3 were waited for; matrix products, arithmetic and copies ran while one was open for 0% of the time, Pallas kernels for 2%

profile of v13, /device:TPU:1, one launch (start us, length us, event | category | flops | bytes accessed | tf_op | source)
XLA Modules:
  0.0 105.1 jit_solution(18314541892614537305)
XLA Ops:
  0.6 0.0 copy-start.4
  0.6 0.0 copy-start.2
  0.7 4.7 %shard_map.93 = bf16[16,16,1024]{2,1,0:T(8,128)(2,1)} custom-call(bf16[2,8,4096]{2,1,0:T(8,128)(2,1)} %text_ref.1, bf16[4096,384]{1,0:T(8,128)(2,1)} %key_ref.1, bf16[4096,384]{1,0:T(8,128)(2,1)} %value_ref.1), custom_call_target="tpu_custom_call" | custom-call | tf_op jit(solution)/shard_map/pallas_call | solution.py:196
  5.4 27.0 %all_to_all.26.own_ref = bf16[16,16,1024]{2,1,0:T(8,128)(2,1)S(1)} all-to-all(bf16[16,16,1024]{2,1,0:T(8,128)(2,1)} %shard_map.93), channel_id=1, replica_groups=mesh['z'=8,'yh'=2,'core'=2,'yl'=2,'x'=4] {'yh','z'}, dimensions={0} | all-to-all | bytes 1048576 | tf_op jit(solution)/shard_map/all_to_all | solution.py:211
  32.4 2.8 %collective-permute-start = (bf16[16,16,1024]{2,1,0:T(8,128)(2,1)S(1)}, bf16[16,16,1024]{2,1,0:T(8,128)(2,1)S(1)}, u32[]{:S(2)}, u32[]{:S(2)}) collective-permute-start(bf16[16,16,1024]{2,1,0:T(8,128)(2,1)S(1)} %all_to_all.26.own_ref), channel_id=1, source_target_pairs={{0,8},{8,0},{1,9},{9,1},{2,10},{10,2},{3,11},{11,3},{4,12},{12,4},... | collective-permute-start | bytes 1572872 | tf_op jit(solution)/shard_map/ppermute | solution.py:207
  35.3 1.5 %collective-permute-done.other_ref = bf16[16,16,1024]{2,1,0:T(8,128)(2,1)S(1)} collective-permute-done((bf16[16,16,1024]{2,1,0:T(8,128)(2,1)S(1)}, bf16[16,16,1024]{2,1,0:T(8,128)(2,1)S(1)}, u32[]{:S(2)}, u32[]{:S(2)}) %collective-permute-start) | collective-permute-done | bytes 524320 | tf_op jit(solution)/shard_map/ppermute | solution.py:207
  36.8 0.0 copy-done.4
  36.8 0.0 copy-done.2
  36.8 0.0 copy-start.3
  36.8 1.1 %copy-done.3 = bf16[2,512,384]{2,1,0:T(8,128)(2,1)S(1)} copy-done((bf16[2,512,384]{2,1,0:T(8,128)(2,1)S(1)}, bf16[2,512,384]{2,1,0:T(8,128)(2,1)}, u32[]{:S(2)}) %copy-start.3) | copy-done | bytes 786456
  37.9 3.7 %shard_map.94 = (f32[16,32,384]{2,1,0:T(8,128)S(1)}, bf16[16,32,384]{2,1,0:T(8,128)(2,1)S(1)}, bf16[2,3,256,512]{3,2,1,0:T(8,128)(2,1)S(1)}, bf16[2,3,256,512]{3...) custom-call(s32[2]{0:T(128)S(1)} %copy-done.4, s32[1]{0:T(128)} %bitcast.core_ref, bf16[2,512,384]{2,1,0:T(8,128)(2,1)S(1)} %copy-done.2, ...), custom_call_target="tpu_custom_call" | custom-call | tf_op jit(solution)/shard_map/pallas_call | solution.py:196
  41.6 0.0 copy-start
  41.6 1.2 %copy-done = bf16[2,3,256,512]{3,2,1,0:T(8,128)(2,1)} copy-done((bf16[2,3,256,512]{3,2,1,0:T(8,128)(2,1)}, bf16[2,3,256,512]{3,2,1,0:T(8,128)(2,1)S(1)}, u32[]{:S(2)}) %copy-start) | copy-done | bytes 1572888
  42.8 0.4 collective-permute-start.1
  43.2 1.3 %collective-permute-done.1.other_ref = bf16[16,32,384]{2,1,0:T(8,128)(2,1)S(1)} collective-permute-done((bf16[16,32,384]{2,1,0:T(8,128)(2,1)S(1)}, bf16[16,32,384]{2,1,0:T(8,128)(2,1)S(1)}, u32[]{:S(2)}, u32[]{:S(2)}) %collective-permute-start.1) | collective-permute-done | bytes 393248 | tf_op jit(solution)/shard_map/ppermute | solution.py:207
  44.5 0.1 shard_map.96
  44.6 16.7 %all_to_all.27.parts_ref = bf16[16,32,384]{2,1,0:T(8,128)(2,1)S(1)} all-to-all(bf16[16,32,384]{2,1,0:T(8,128)(2,1)S(1)} %shard_map.96), channel_id=1, replica_groups=mesh['z'=8,'yh'=2,'core'=2,'yl'=2,'x'=4] {'yh','z'}, dimensions={0} | all-to-all | bytes 786432 | tf_op jit(solution)/shard_map/all_to_all | solution.py:211
  61.3 0.1 shard_map.97
  61.4 18.2 %all_to_all.28.total_ref = bf16[16,32,384]{2,1,0:T(8,128)(2,1)S(1)} all-to-all(bf16[16,32,384]{2,1,0:T(8,128)(2,1)S(1)} %shard_map.97), channel_id=1, replica_groups=mesh['z'=8,'yh'=2,'core'=2,'yl'=2,'x'=4] {'yh','z'}, dimensions={0} | all-to-all | bytes 786432 | tf_op jit(solution)/shard_map/all_to_all | solution.py:211
  79.6 1.1 %shard_map.98 = (f32[128,384]{1,0:T(8,128)S(1)}, f32[128,384]{1,0:T(8,128)S(1)}, f32[256,1]{1,0:T(8,128)}) custom-call(s32[1]{0:T(128)} %bitcast.core_ref, bf16[2,16,16,256]{3,2,1,0:T(8,128)(2,1)S(1)} %get-tuple-element.20.columns_ref, bf16[16,32,384]{2,1,0:T(8,128)(2,1)S(1)} %all_to_all.28.total_ref), custom_call_target="tpu_custom_call" | custom-call | tf_op jit(solution)/shard_map/pallas_call | solution.py:196
  80.7 2.7 %collective-permute-start.2 = (f32[128,384]{1,0:T(8,128)S(1)}, f32[128,384]{1,0:T(8,128)S(1)}, u32[]{:S(2)}, u32[]{:S(2)}) collective-permute-start(f32[128,384]{1,0:T(8,128)S(1)} %get-tuple-element.24), channel_id=1, source_target_pairs={{0,8},{8,0},{1,9},{9,1},{2,10},{10,2},{3,11},{11,3},{4,12},{12,4},... | collective-permute-start | bytes 589832 | tf_op jit(solution)/shard_map/ppermute | solution.py:207
  83.5 7.9 %all-to-all-start.3 = ((f32[256,1,1]{2,1,0:T(1,128)}), f32[256,1,1]{2,1,0:T(1,128)S(1)}, u32[]{:S(2)}, u32[]{:S(2)}) async-start(f32[256,1,1]{2,1,0:T(1,128)} %bitcast.1), calls=%async_computation.3 | async-start | bytes 262144 | tf_op jit(solution)/shard_map/all_to_all | solution.py:211
  91.4 0.0 copy-start.1
  91.4 1.4 %copy-done.1 = bf16[2,3,256,512]{3,2,1,0:T(8,128)(2,1)S(1)} copy-done((bf16[2,3,256,512]{3,2,1,0:T(8,128)(2,1)S(1)}, bf16[2,3,256,512]{3,2,1,0:T(8,128)(2,1)}, u32[]{:S(2)}) %copy-start.1) | copy-done | bytes 1572888
  92.8 1.9 %shard_map.95 = (bf16[2,512,384]{2,1,0:T(8,128)(2,1)}, bf16[2,512,384]{2,1,0:T(8,128)(2,1)}) custom-call(s32[1]{0:T(128)} %bitcast.core_ref, bf16[16,16,1024]{2,1,0:T(8,128)(2,1)S(1)} %all_to_all.26.own_ref, bf16[16,16,1024]{2,1,0:T(8,128)(2,1)S(1)} %collective-permute-done.other_ref, bf16[2,3,256,512]{3,2,1,0:T(8,128)(2,1)S(1)} %get-tuple-element.16.probs_ref, ...), custom_call_target="tpu_custom_call" | custom-call | tf_op jit(solution)/shard_map/pallas_call | solution.py:196
  94.6 9.6 %all-to-all-done.3 = f32[256,1,1]{2,1,0:T(1,128)S(1)} async-done(((f32[256,1,1]{2,1,0:T(1,128)}), f32[256,1,1]{2,1,0:T(1,128)S(1)}, u32[]{:S(2)}, u32[]{:S(2)}) %all-to-all-start.3) | async-done | bytes 1056 | tf_op jit(solution)/shard_map/all_to_all | solution.py:211
  104.2 0.0 collective-permute-done.2.other_ref
  104.2 0.9 shard_map.99
Async XLA Ops:
  0.6 36.2 %copy-start.4 = (s32[2]{0:T(128)S(1)}, s32[2]{0:T(128)}, u32[]{:S(2)}) copy-start(s32[2]{0:T(128)} %lengths_ref.1) | copy-start | bytes 28
  0.6 36.2 %copy-start.2 = (bf16[2,512,384]{2,1,0:T(8,128)(2,1)S(1)}, bf16[2,512,384]{2,1,0:T(8,128)(2,1)}, u32[]{:S(2)}) copy-start(bf16[2,512,384]{2,1,0:T(8,128)(2,1)} %query_ref.1) | copy-start | bytes 2359300
  32.4 4.4 %collective-permute-start = (bf16[16,16,1024]{2,1,0:T(8,128)(2,1)S(1)}, bf16[16,16,1024]{2,1,0:T(8,128)(2,1)S(1)}, u32[]{:S(2)}, u32[]{:S(2)}) collective-permute-start(bf16[16,16,1024]{2,1,0:T(8,128)(2,1)S(1)} %all_to_all.26.own_ref), channel_id=1, source_target_pairs={{0,8},{8,0},{1,9},{9,1},{2,10},{10,2},{3,11},{11,3},{4,12},{12,4},... | collective-permute-start | bytes 1572872 | tf_op jit(solution)/shard_map/ppermute | solution.py:207
  36.8 1.1 %copy-start.3 = (bf16[2,512,384]{2,1,0:T(8,128)(2,1)S(1)}, bf16[2,512,384]{2,1,0:T(8,128)(2,1)}, u32[]{:S(2)}) copy-start(bf16[2,512,384]{2,1,0:T(8,128)(2,1)} %grad_ref.1) | copy-start | bytes 2359300
  41.6 1.2 %copy-start = (bf16[2,3,256,512]{3,2,1,0:T(8,128)(2,1)}, bf16[2,3,256,512]{3,2,1,0:T(8,128)(2,1)S(1)}, u32[]{:S(2)}) copy-start(bf16[2,3,256,512]{3,2,1,0:T(8,128)(2,1)S(1)} %get-tuple-element.17.dscore_ref) | copy-start | bytes 4718596
  42.8 1.7 %collective-permute-start.1 = (bf16[16,32,384]{2,1,0:T(8,128)(2,1)S(1)}, bf16[16,32,384]{2,1,0:T(8,128)(2,1)S(1)}, u32[]{:S(2)}, u32[]{:S(2)}) collective-permute-start(bf16[16,32,384]{2,1,0:T(8,128)(2,1)S(1)} %get-tuple-element.22), channel_id=1, source_target_pairs={{0,8},{8,0},{1,9},{9,1},{2,10},{10,2},{3,11},{11,3},{4,12},{12,4},... | collective-permute-start | bytes 1179656 | tf_op jit(solution)/shard_map/ppermute | solution.py:207
  80.7 23.5 %collective-permute-start.2 = (f32[128,384]{1,0:T(8,128)S(1)}, f32[128,384]{1,0:T(8,128)S(1)}, u32[]{:S(2)}, u32[]{:S(2)}) collective-permute-start(f32[128,384]{1,0:T(8,128)S(1)} %get-tuple-element.24), channel_id=1, source_target_pairs={{0,8},{8,0},{1,9},{9,1},{2,10},{10,2},{3,11},{11,3},{4,12},{12,4},... | collective-permute-start | bytes 589832 | tf_op jit(solution)/shard_map/ppermute | solution.py:207
  83.5 20.7 %all-to-all-start.3 = ((f32[256,1,1]{2,1,0:T(1,128)}), f32[256,1,1]{2,1,0:T(1,128)S(1)}, u32[]{:S(2)}, u32[]{:S(2)}) async-start(f32[256,1,1]{2,1,0:T(1,128)} %bitcast.1), calls=%async_computation.3 | async-start | bytes 262144 | tf_op jit(solution)/shard_map/all_to_all | solution.py:211
  91.4 1.4 %copy-start.1 = (bf16[2,3,256,512]{3,2,1,0:T(8,128)(2,1)S(1)}, bf16[2,3,256,512]{3,2,1,0:T(8,128)(2,1)}, u32[]{:S(2)}) copy-start(bf16[2,3,256,512]{3,2,1,0:T(8,128)(2,1)} %copy-done) | copy-start | bytes 4718596
